TPU v7x, 32 devices: a whole 2x2x4 slice. The times are simulated.
32 devices in a mesh: seq: 8 (over z, y), frame: 4 (over x, core).
Axes of the slice: x: 2, y: 2, z: 4, core: 2. Of those that a mesh axis runs over, the one named last changes fastest.
Arguments:
- patches: bfloat16 [3072, 1280], P('frame'), may hold values from -4 to 4
- vit_gain: float32 [1280], replicated, may hold values from 0.5 to 1.5
- vision_qkv: bfloat16 [1280, 3840], P(None, 'seq')
- vision_out: bfloat16 [1280, 1280], P('seq'), may hold values from -0.15625 to 0.15625
- video_ids: int32 [768], replicated, may hold values from 0 to 2, never falling along the last dimension, each value on 1 to 480 neighbouring positions
- merge_gain: float32 [1280], replicated, may hold values from 0.5 to 1.5
- merge_up: bfloat16 [5120, 5120], P(None, 'seq'), may hold values from -0.078125 to 0.078125
- merge_down: bfloat16 [5120, 8192], P('seq')
- vision_pos: int32 [768], replicated, may hold values from 0 to 4095, as said below
- text_embed: bfloat16 [4096, 8192], P(('seq', 'frame')), may hold values from -6 to 6
- llm_gain: float32 [8192], replicated, may hold values from 0.5 to 1.5
- query_weight: bfloat16 [8192, 2048], P(None, 'frame')
- keyvalue_weight: bfloat16 [8192, 1024], P(None, 'frame')
Outputs:
- context: bfloat16 [4096, 2048], P('seq', 'frame')
Inputs may be any that keep to these rules, and one draw needn't show every extreme that they name: `vision_pos`: distinct positions. Of the tokens in rows f * 192 to (f + 1) * 192 - 1, for any f, at most 36 lie in one block of 512 positions that starts at a multiple of 512; some block holds exactly 36 of them for every f. `video_ids`: the tokens of one video are consecutive rows.
All inputs are finite; a program needn't handle non-finite values.
Results may differ from a plain program's by a relative error of at most 0.02.
Values may be sent and summed in bfloat16 or wider, within the bound.
A program may use at most 128 MiB of HBM per device.

v0:
```python
import math

import jax
import jax.numpy as jnp
from jax import lax
from jax.experimental import pallas as pl
from jax.experimental.pallas import tpu as pltpu
from jax.sharding import PartitionSpec as P

VIT_HDIM = 80
HDIM = 128


epsilon = 1e-06
rope_base = 1000000.0
lowest = -1e30
vmem_limit = 56 * 1024 * 1024


def rms_scale(matrix, scales):
    widened = matrix.astype(jnp.float32)
    factor = lax.rsqrt(jnp.mean(widened * widened, axis=-1, keepdims=True) + epsilon)
    return widened * factor * scales


def rotary(tensor, positions):
    head_width = tensor.shape[-1]
    half_width = head_width // 2
    inverse = rope_base ** (-2.0 * jnp.arange(half_width, dtype=jnp.float32) / head_width)
    angles = positions.astype(jnp.float32)[:, None] * inverse[None, :]
    cosine = jnp.cos(angles)[:, None, :]
    sine_part = jnp.sin(angles)[:, None, :]
    first_half = tensor[..., :half_width]
    second_half = tensor[..., half_width:]
    return jnp.concatenate(
        [
            first_half * cosine - second_half * sine_part,
            second_half * cosine + first_half * sine_part,
        ],
        axis=-1,
    )


def vit_attention_kernel(own_ref, ids_ref, q_ref, k_ref, v_ref, out_ref):
    allowed = own_ref[...] == ids_ref[...]
    parts = []
    for head in range(q_ref.shape[1] // VIT_HDIM):
        columns = slice(head * VIT_HDIM, (head + 1) * VIT_HDIM)
        scores = lax.dot_general(
            q_ref[:, columns],
            k_ref[:, columns],
            (((1,), (1,)), ((), ())),
            preferred_element_type=jnp.float32,
        )
        scores = jnp.where(allowed, scores, lowest)
        highest = jnp.max(scores, axis=1, keepdims=True)
        weights = jnp.exp((scores - highest) * VIT_HDIM ** (-0.5))
        row_sum = jnp.sum(weights, axis=1, keepdims=True)
        mixed = jnp.dot(
            weights.astype(jnp.bfloat16), v_ref[:, columns], preferred_element_type=jnp.float32
        )
        parts.append(mixed / row_sum)
    out_ref[...] = jnp.concatenate(parts, axis=1).astype(out_ref.dtype)


def vit_attention(own_ids, all_ids, queries, key_rows, value_rows):
    rows, width = queries.shape
    keys = key_rows.shape[0]
    step = math.gcd(rows, 256)
    return pl.pallas_call(
        vit_attention_kernel,
        grid=(rows // step,),
        in_specs=[
            pl.BlockSpec((step, 1), lambda i: (i, 0)),
            pl.BlockSpec((1, keys), lambda i: (0, 0)),
            pl.BlockSpec((step, width), lambda i: (i, 0)),
            pl.BlockSpec((keys, width), lambda i: (0, 0)),
            pl.BlockSpec((keys, width), lambda i: (0, 0)),
        ],
        out_specs=pl.BlockSpec((step, width), lambda i: (i, 0)),
        out_shape=jax.ShapeDtypeStruct((rows, width), jnp.bfloat16),
        compiler_params=pltpu.CompilerParams(vmem_limit_bytes=vmem_limit),
    )(own_ids[:, None], all_ids[None, :], queries, key_rows, value_rows)


def causal_kernel(block_ref, q_ref, k_ref, v_ref, out_ref):
    rows = q_ref.shape[0]
    queries = q_ref[...]

    def fold(start, state_in, masked):
        running_max, running_sum, weighted = state_in
        scores = lax.dot_general(
            queries,
            k_ref[pl.ds(start, rows), :],
            (((1,), (1,)), ((), ())),
            preferred_element_type=jnp.float32,
        )
        if masked:
            row_id = lax.broadcasted_iota(jnp.int32, (rows, rows), 0)
            column_id = lax.broadcasted_iota(jnp.int32, (rows, rows), 1)
            scores = jnp.where(row_id >= column_id, scores, lowest)
        new_max = jnp.maximum(running_max, jnp.max(scores, axis=1, keepdims=True))
        weights = jnp.exp((scores - new_max) * HDIM ** (-0.5))
        shrink = jnp.exp((running_max - new_max) * HDIM ** (-0.5))
        running_sum = running_sum * shrink + jnp.sum(weights, axis=1, keepdims=True)
        update = jnp.dot(
            weights.astype(jnp.bfloat16),
            v_ref[pl.ds(start, rows), :],
            preferred_element_type=jnp.float32,
        )
        return (new_max, running_sum, weighted * shrink + update)

    state = (
        jnp.full((rows, 1), lowest, jnp.float32),
        jnp.zeros((rows, 1), jnp.float32),
        jnp.zeros((rows, HDIM), jnp.float32),
    )
    own = block_ref[0]
    state = fold(pl.multiple_of(own * rows, rows), state, True)
    _, running_sum, weighted = lax.fori_loop(
        0, own, lambda i, now: fold(pl.multiple_of(i * rows, rows), now, False), state
    )
    out_ref[...] = (weighted / running_sum).astype(out_ref.dtype)


def causal_attention(block_index, queries, key_rows, value_rows):
    rows, width = queries.shape
    keys = key_rows.shape[0]
    return pl.pallas_call(
        causal_kernel,
        grid=(width // HDIM,),
        in_specs=[
            pl.BlockSpec(memory_space=pltpu.SMEM),
            pl.BlockSpec((rows, HDIM), lambda h: (0, h)),
            pl.BlockSpec((keys, HDIM), lambda h: (0, 0)),
            pl.BlockSpec((keys, HDIM), lambda h: (0, 0)),
        ],
        out_specs=pl.BlockSpec((rows, HDIM), lambda h: (0, h)),
        out_shape=jax.ShapeDtypeStruct((rows, width), jnp.bfloat16),
        compiler_params=pltpu.CompilerParams(vmem_limit_bytes=vmem_limit),
    )(block_index[None], queries, key_rows, value_rows)


def project(tokens, positions, query_weight, keyvalue_weight):
    rows = tokens.shape[0]
    query_full = jnp.dot(tokens, query_weight, preferred_element_type=jnp.float32)
    query = rotary(query_full.reshape(rows, -1, HDIM), positions).reshape(rows, -1)
    pair_full = jnp.dot(tokens, keyvalue_weight, preferred_element_type=jnp.float32)
    key = rotary(pair_full[:, :HDIM].reshape(rows, 1, HDIM), positions).reshape(rows, HDIM)
    pair = jnp.concatenate([key, pair_full[:, HDIM:]], axis=1)
    return query.astype(jnp.bfloat16), pair.astype(jnp.bfloat16)


def place(token_pos, first, text_rows, vision_rows):
    spots = first + jnp.arange(text_rows.shape[0], dtype=jnp.int32)
    hit = spots[:, None] == token_pos[None, :]
    moved = jnp.dot(hit.astype(jnp.bfloat16), vision_rows, preferred_element_type=jnp.float32)
    taken = jnp.any(hit, axis=1, keepdims=True)
    return jnp.where(taken, moved.astype(jnp.bfloat16), text_rows)


def local(
    patches,
    vit_gain,
    vision_qkv,
    vision_out,
    video_ids,
    merge_gain,
    merge_up,
    merge_down,
    vision_pos,
    text_embed,
    llm_gain,
    query_weight,
    keyvalue_weight,
):
    frame_index = lax.axis_index("frame")
    seq_index = lax.axis_index("seq")
    frame_count = lax.axis_size("frame")
    seq_count = lax.axis_size("seq")
    patch_rows = patches.shape[0]
    local_heads = vision_qkv.shape[1] // (3 * VIT_HDIM)
    normed_patches = rms_scale(patches, vit_gain).astype(jnp.bfloat16)
    projected = jnp.dot(normed_patches, vision_qkv, preferred_element_type=jnp.float32).astype(
        jnp.bfloat16
    )
    width = local_heads * VIT_HDIM
    projected = projected.reshape(patch_rows, local_heads, 3, VIT_HDIM)
    vit_query = projected[:, :, 0].reshape(patch_rows, width)
    vit_key = projected[:, :, 1].reshape(patch_rows, width)
    vit_value = projected[:, :, 2].reshape(patch_rows, width)
    patch_video = jnp.repeat(video_ids, 4)
    own_video = lax.dynamic_slice_in_dim(patch_video, frame_index * patch_rows, patch_rows)
    out_full = lax.all_gather(vision_out, "seq", axis=0, tiled=True)
    key_all = lax.all_gather(vit_key, "frame", axis=0, tiled=True)
    value_all = lax.all_gather(vit_value, "frame", axis=0, tiled=True)
    vit_query, out_full = lax.optimization_barrier((vit_query, out_full))
    vit_context = vit_attention(own_video, patch_video, vit_query, key_all, value_all)
    context_all = lax.all_gather(vit_context.T, "seq", axis=0, tiled=True)
    head_total = lax.dot_general(
        context_all, out_full, (((0,), (0,)), ((), ())), preferred_element_type=jnp.float32
    )
    vit_output = patches.astype(jnp.float32) + head_total
    merged_input = (
        rms_scale(vit_output, merge_gain).astype(jnp.bfloat16).reshape(patch_rows // 4, -1)
    )
    merge_hidden = jax.nn.gelu(
        jnp.dot(merged_input, merge_up, preferred_element_type=jnp.float32), approximate=False
    ).astype(jnp.bfloat16)

    part_rows = text_embed.shape[0]
    seq_block = part_rows * frame_count
    first = seq_index * seq_block
    text_block = text_embed[None]
    owners = [0]
    bit = frame_count // 2
    while bit:
        swap = [(i, i ^ bit) for i in range(frame_count)]
        if len(owners) > 1:
            text_block, key_tie = lax.optimization_barrier((text_block, key_all))
        text_block = jnp.concatenate([text_block, lax.ppermute(text_block, "frame", swap)], axis=0)
        owners = owners + [mask ^ bit for mask in owners]
        bit //= 2
    spots = jnp.arange(part_rows, dtype=jnp.int32)
    positions = jnp.concatenate(
        [first + (frame_index ^ mask) * part_rows + spots for mask in owners]
    )
    text_tokens = rms_scale(text_block.reshape(seq_block, -1), llm_gain).astype(jnp.bfloat16)
    text_query, text_pair = project(text_tokens, positions, query_weight, keyvalue_weight)

    def in_order(rows):
        split = rows.reshape(frame_count, part_rows, -1)
        return [
            lax.dynamic_index_in_dim(
                split, sum(jnp.where(mask == (frame_index ^ f), slot, 0) for slot, mask in enumerate(owners)), 0, False
            )
            for f in range(frame_count)
        ]

    vision_part = jnp.dot(
        merge_hidden, merge_down, preferred_element_type=jnp.float32
    ).astype(jnp.bfloat16)
    vision_part, text_pair = lax.optimization_barrier((vision_part, text_pair))
    vision_rows = lax.psum_scatter(vision_part, "seq", scatter_dimension=0, tiled=True)
    text_query = jnp.concatenate(in_order(text_query), axis=0)
    text_pair_all = jnp.concatenate(
        [lax.all_gather(rows, "seq", axis=0) for rows in in_order(text_pair)], axis=1
    ).reshape(seq_count * seq_block, -1)
    vision_rows, text_pair_all = lax.optimization_barrier((vision_rows, text_pair_all))
    share = vision_rows.shape[0]
    token_pos = vision_pos.reshape(frame_count, seq_count, share).transpose(1, 0, 2)
    vision_normed = rms_scale(vision_rows, llm_gain).astype(jnp.bfloat16)
    vision_tokens = jnp.concatenate(
        [
            lax.all_gather(piece, "frame", axis=0, tiled=True)
            for piece in jnp.split(vision_normed, 2, axis=1)
        ],
        axis=1,
    )
    here = lax.dynamic_index_in_dim(token_pos, seq_index, 0, keepdims=False).reshape(-1)
    vision_query, vision_pair = project(vision_tokens, here, query_weight, keyvalue_weight)
    vision_query = lax.all_gather(vision_query, "seq", axis=0, tiled=True)
    vision_pair = lax.all_gather(vision_pair, "seq", axis=0, tiled=True)
    token_pos = token_pos.reshape(-1)
    llm_query = place(token_pos, first, text_query, vision_query)
    llm_pair = place(token_pos, 0, text_pair_all, vision_pair)
    return causal_attention(seq_index, llm_query, llm_pair[:, :HDIM], llm_pair[:, HDIM:])


def solution(mesh):
    return jax.shard_map(
        local,
        mesh=mesh,
        in_specs=(
            P("frame", None),
            P(),
            P(None, "seq"),
            P("seq", None),
            P(),
            P(),
            P(None, "seq"),
            P("seq", None),
            P(),
            P(("seq", "frame"), None),
            P(),
            P(None, "frame"),
            P(None, "frame"),
        ),
        out_specs=P("seq", "frame"),
        check_vma=False,
    )
```

profile of v0, /device:TPU:28, one launch (start us, length us, event | category | flops | bytes accessed | tf_op | source)
XLA Modules:
  0.0 452.5 jit_solution(17180890028857297824)
XLA Ops:
  6.5 1.5 collective-permute-start
  8.1 2.0 fusion.7
  10.1 2.8 fusion.16
  13.2 50.8 %all_gather.41.k_ref = bf16[3072,160]{1,0:T(8,128)(2,1)} all-gather(bf16[768,160]{1,0:T(8,128)(2,1)S(1)} %copy.80), channel_id=1, replica_groups=mesh['seq'=8,'frame'=4] {'frame'}, dimensions={0}, use_global_device_ids=true | all-gather | bytes 1228800 | tf_op jit(solution)/shard_map/all_gather | solution.py:195
  64.0 3.9 pad_maximum_fusion
  70.7 13.3 %all_gather.42.v_ref = bf16[3072,160]{1,0:T(8,128)(2,1)} all-gather(bf16[768,160]{1,0:T(8,128)(2,1)S(1)} %copy.82), channel_id=1, replica_groups=mesh['seq'=8,'frame'=4] {'frame'}, dimensions={0}, use_global_device_ids=true | all-gather | bytes 1228800 | tf_op jit(solution)/shard_map/all_gather | solution.py:196
  84.9 12.4 %shard_map.127 = bf16[768,160]{1,0:T(8,128)(2,1)} custom-call(s32[768,1]{1,0:T(8,128)} %broadcast_in_dim.24.own_ref, s32[1,3072]{1,0:T(1,128)} %broadcast_in_dim_reshape.2.ids_ref, bf16[768,160]{1,0:T(8,128)(2,1)} %copy.84.q_ref, bf16[3072,160]{1,0:T(8,128)(2,1)} %all_gather.41.k_ref, bf16[3072,160]{1,0:T(8,128)(2,1)} %all_gather.42.v_ref), custom_call_target="tpu_custom_call" | custom-call | tf_op jit(solution)/shard_map/pallas_call | solution.py:70
  97.4 1.8 copy.85
  99.5 4.8 %multiply_reduce_fusion = f32[4,128]{1,0:T(4,128)S(1)} fusion(bf16[2,128,8192]{2,1,0:T(8,128)(2,1)} %collective-permute-done.1, bf16[2,128,8192]{2,1,0:T(8,128)(2,1)} %pad_maximum_fusion), kind=kLoop, calls=%fused_computation.4 | loop fusion | flops 16776704 | bytes 8390656 | tf_op jit(solution)/shard_map/reduce_sum | solution.py:22
  104.4 10.3 %maximum_convert_fusion = f32[4,128,8192]{2,1,0:T(8,128)} fusion(bf16[2,128,8192]{2,1,0:T(8,128)(2,1)} %collective-permute-done.1, bf16[2,128,8192]{2,1,0:T(8,128)(2,1)} %pad_maximum_fusion), kind=kLoop, calls=%fused_computation.9 | loop fusion | flops 8388608 | bytes 25165824 | tf_op jit(solution)/shard_map/convert_element_type | solution.py:21
  114.7 7.1 %fusion.1 = bf16[512,8192]{1,0:T(8,128)(2,1)S(1)} fusion(f32[4,128,8192]{2,1,0:T(8,128)} %maximum_convert_fusion, f32[8192]{0:T(1024)S(1)} %copy-done.6, f32[512]{0:T(512)S(1)} %get-tuple-element.45), kind=kLoop, calls=%fused_computation.2 | loop fusion | flops 12582912 | bytes 25200640 | tf_op jit(solution)/shard_map/convert_element_type | solution.py:228
  121.8 2.4 fusion.125
  124.8 20.9 %all-gather.5.cloned.1.call-done = bf16[1280,768]{1,0:T(8,128)(2,1)} async-done(((bf16[160,768]{1,0:T(8,128)(2,1)}), bf16[1280,768]{1,0:T(8,128)(2,1)}) %all-gather.5.cloned.1.call-update) | async-done | bytes 1966096 | tf_op jit(solution)/shard_map/all_gather | solution.py:199
  145.7 5.5 %multiply_reduce_fusion.1 = (f32[768]{0:T(1024)S(1)}, f32[768,1280]{1,0:T(8,128)S(1)}) fusion(bf16[1280,768]{1,0:T(8,128)(2,1)} %all-gather.5.cloned.1.call-done, bf16[1280,1280]{1,0:T(8,128)(2,1)} %all-gather.3.cloned.1.call-done, bf16[768,1280]{1,0:T(8,128)(2,1)S(1)} %copy-done.2), kind=kOutput, calls=%fused_computation.21 | convolution fusion | flops 2520513792 | bytes 11144192 | tf_op jit(solution)/shard_map/dot_general | solution.py:200
  151.6 2.7 reshape.372
  154.4 13.3 %convolution_convert_fusion = bf16[192,8192]{1,0:T(8,128)(2,1)} fusion(bf16[640,8192]{1,0:T(8,128)(2,1)} %param.20, bf16[192,5120]{1,0:T(8,128)(2,1)} %reshape.372, bf16[5120,640]{1,0:T(8,128)(2,1)} %param.19), kind=kOutput, calls=%fused_computation.8 | convolution fusion | flops 3281117184 | bytes 22151168 | tf_op jit(solution)/shard_map/dot_general | solution.py:240
  168.1 11.5 %copy.95 = bf16[512,8192]{1,0:T(8,128)(2,1)} copy(bf16[512,8192]{0,1:T(8,128)(2,1)} %bitcast.63) | data formatting | bytes 16777216 | tf_op jit(solution)/shard_map/dot_general | solution.py:146
  181.2 1.4 fusion.3
  182.7 5.7 %multiply_convert_fusion = bf16[4,128,8192]{2,1,0:T(8,128)(2,1)S(1)} fusion(f32[8192]{0:T(1024)S(1)} %copy-done.6, f32[4,128]{1,0:T(4,128)S(1)} %get-tuple-element.44, bf16[2,128,8192]{2,1,0:T(8,128)(2,1)} %collective-permute-done.1, bf16[2,128,8192]{2,1,0:T(8,128)(2,1)} %pad_maximum_fusion), kind=kLoop, calls=%fused_computation.3 | loop fusion | flops 20971520 | bytes 16812032 | tf_op jit(solution)/shard_map/convert_element_type | solution.py:228
  188.4 4.5 fusion.127
  197.7 31.7 %all_gather.44 = bf16[8,128,256]{2,1,0:T(8,128)(2,1)S(1)} all-gather(bf16[1,128,256]{2,1,0:T(8,128)(2,1)S(1)} %get-tuple-element.36), channel_id=1, replica_groups=mesh['seq'=8,'frame'=4] {'seq'}, dimensions={0}, use_global_device_ids=true | all-gather | bytes 589824 | tf_op jit(solution)/shard_map/all_gather | solution.py:247
  229.3 32.4 %all_gather.45 = bf16[8,128,256]{2,1,0:T(8,128)(2,1)S(1)} all-gather(bf16[1,128,256]{2,1,0:T(8,128)(2,1)S(1)} %get-tuple-element.39), channel_id=1, replica_groups=mesh['seq'=8,'frame'=4] {'seq'}, dimensions={0}, use_global_device_ids=true | all-gather | bytes 589824 | tf_op jit(solution)/shard_map/all_gather | solution.py:247
  261.7 31.7 %all_gather.46 = bf16[8,128,256]{2,1,0:T(8,128)(2,1)S(1)} all-gather(bf16[1,128,256]{2,1,0:T(8,128)(2,1)S(1)} %get-tuple-element.38), channel_id=1, replica_groups=mesh['seq'=8,'frame'=4] {'seq'}, dimensions={0}, use_global_device_ids=true | all-gather | bytes 589824 | tf_op jit(solution)/shard_map/all_gather | solution.py:247
  293.5 31.2 %all_gather.47 = bf16[8,128,256]{2,1,0:T(8,128)(2,1)S(1)} all-gather(bf16[1,128,256]{2,1,0:T(8,128)(2,1)S(1)} %get-tuple-element.37), channel_id=1, replica_groups=mesh['seq'=8,'frame'=4] {'seq'}, dimensions={0}, use_global_device_ids=true | all-gather | bytes 589824 | tf_op jit(solution)/shard_map/all_gather | solution.py:247
  327.4 8.5 %all_gather.48 = bf16[96,4096]{1,0:T(8,128)(2,1)S(1)} all-gather(bf16[24,4096]{1,0:T(8,128)(2,1)S(1)} %get-tuple-element.31), channel_id=1, replica_groups=mesh['seq'=8,'frame'=4] {'frame'}, dimensions={0}, use_global_device_ids=true | all-gather | bytes 983040 | tf_op jit(solution)/shard_map/all_gather | solution.py:255
  336.0 8.7 %all_gather.49 = bf16[96,4096]{1,0:T(8,128)(2,1)S(1)} all-gather(bf16[24,4096]{1,0:T(8,128)(2,1)S(1)} %get-tuple-element.30), channel_id=1, replica_groups=mesh['seq'=8,'frame'=4] {'frame'}, dimensions={0}, use_global_device_ids=true | all-gather | bytes 983040 | tf_op jit(solution)/shard_map/all_gather | solution.py:255
  345.6 4.9 %fusion.126 = f32[96,512]{1,0:T(8,128)S(1)} fusion(bf16[96,8192]{1,0:T(8,128)(2,1)S(1)} %constant_dynamic-update-slice_fusion, bf16[8192,512]{1,0:T(8,128)(2,1)} %param.24), kind=kOutput, calls=%fused_computation.187 | convolution fusion | flops 805306368 | bytes 10158080 | tf_op jit(solution)/shard_map/dot_general | solution.py:146
  350.9 31.0 %all_gather.51 = bf16[768,256]{1,0:T(8,128)(2,1)S(1)} all-gather(bf16[96,256]{1,0:T(8,128)(2,1)S(1)} %pad_maximum_fusion.5), channel_id=1, replica_groups=mesh['seq'=8,'frame'=4] {'seq'}, dimensions={0}, use_global_device_ids=true | all-gather | bytes 442368 | tf_op jit(solution)/shard_map/all_gather | solution.py:263
  381.8 3.3 fusion.6
  385.2 1.5 fusion.120
  387.2 31.8 %all_gather.50 = bf16[768,512]{1,0:T(8,128)(2,1)S(1)} all-gather(bf16[96,512]{1,0:T(8,128)(2,1)S(1)} %bitcast.77), channel_id=1, replica_groups=mesh['seq'=8,'frame'=4] {'seq'}, dimensions={0}, use_global_device_ids=true | all-gather | bytes 884736 | tf_op jit(solution)/shard_map/all_gather | solution.py:262
  420.4 25.1 %shard_map.128 = bf16[512,512]{1,0:T(8,128)(2,1)} custom-call(s32[1]{0:T(128)} %bitcast.block_ref, bf16[512,512]{1,0:T(8,128)(2,1)} %fusion.22.q_ref, bf16[4096,128]{1,0:T(8,128)(2,1)} %get-tuple-element.20.k_ref, bf16[4096,128]{1,0:T(8,128)(2,1)} %get-tuple-element.19.v_ref), custom_call_target="tpu_custom_call" | custom-call | tf_op jit(solution)/shard_map/pallas_call | solution.py:129
  (121 shorter events, 17.8 us)
Async XLA Ops:
  6.5 3.6 copy-start
  6.5 77.5 %all-gather.3.cloned.1.call-start = ((), (), s32[]{:S(2)}) async-start(), calls=%async_computation.1 | async-start | bytes 3686400 | tf_op jit(solution)/shard_map/all_gather | solution.py:194
  6.5 57.4 %collective-permute-start = (bf16[1,128,8192]{2,1,0:T(8,128)(2,1)}, bf16[1,128,8192]{2,1,0:T(8,128)(2,1)}, u32[]{:S(2)}, u32[]{:S(2)}) collective-permute-start(bf16[1,128,8192]{2,1,0:T(8,128)(2,1)} %bitcast.69), channel_id=1, source_target_pairs={{0,2},{1,3},{2,0},{3,1},{4,6},{5,7},{6,4},{7,5},{8,10},{9,11},{10,... | collective-permute-start | bytes 6291464 | tf_op jit(solution)/shard_map/ppermute | solution.py:221
  8.1 137.7 %all-gather.5.cloned.1.call-start = ((), (), s32[]{:S(2)}) async-start(), calls=%async_computation.2 | async-start | bytes 2211840 | tf_op jit(solution)/shard_map/all_gather | solution.py:199
  12.9 51.0 %copy-start.5 = (bf16[128,8192]{1,0:T(8,128)(2,1)S(1)}, bf16[128,8192]{1,0:T(8,128)(2,1)}, u32[]{:S(2)}) copy-start(bf16[128,8192]{1,0:T(8,128)(2,1)} %param.22) | copy-start | bytes 6291460
  63.9 4.3 copy-start.20
  67.9 31.6 %collective-permute-start.1 = (bf16[2,128,8192]{2,1,0:T(8,128)(2,1)}, bf16[2,128,8192]{2,1,0:T(8,128)(2,1)}, u32[]{:S(2)}, u32[]{:S(2)}) collective-permute-start(bf16[2,128,8192]{2,1,0:T(8,128)(2,1)} %pad_maximum_fusion), channel_id=1, source_target_pairs={{0,1},{1,0},{2,3},{3,2},{4,5},{5,4},{6,7},{7,6},{8,9},{9,8},{10,11... | collective-permute-start | bytes 12582920 | tf_op jit(solution)/shard_map/ppermute | solution.py:221
  70.7 110.0 %copy-start.14 = (f32[64]{0:T(128)}, f32[64]{0:T(128)S(1)}, u32[]{:S(2)}) copy-start(f32[64]{0:T(128)S(1)} %multiply_power_fusion) | copy-start | bytes 772
  99.3 225.5 %reduce-scatter.2.cloned.1.call-start = ((), (), s32[]{:S(2)}) async-start(), calls=%async_computation.3 | async-start | bytes 3538944 | tf_op jit(solution)/shard_map/reduce_scatter | solution.py:244
  104.3 10.3 %copy-start.6 = (f32[8192]{0:T(1024)S(1)}, f32[8192]{0:T(1024)}, u32[]{:S(2)}) copy-start(f32[8192]{0:T(1024)} %param.23) | copy-start | bytes 98308
  114.7 7.1 %copy-start.3 = (bf16[8192,256]{1,0:T(8,128)(2,1)S(1)}, bf16[8192,256]{1,0:T(8,128)(2,1)}, u32[]{:S(2)}) copy-start(bf16[8192,256]{1,0:T(8,128)(2,1)} %param.25) | copy-start | bytes 12582916
  121.8 23.9 %copy-start.2 = (bf16[768,1280]{1,0:T(8,128)(2,1)S(1)}, bf16[768,1280]{1,0:T(8,128)(2,1)}, u32[]{:S(2)}) copy-start(bf16[768,1280]{1,0:T(8,128)(2,1)} %param.13) | copy-start | bytes 5898244
  124.8 26.4 %copy-start.13 = (f32[1280]{0:T(1024)S(1)}, f32[1280]{0:T(1024)}, u32[]{:S(2)}) copy-start(f32[1280]{0:T(1024)} %param.18) | copy-start | bytes 15364
  154.4 13.4 %copy-start.21 = (s32[768]{0:T(1024)S(1)}, s32[768]{0:T(1024)}, u32[]{:S(2)}) copy-start(s32[768]{0:T(1024)} %param.21) | copy-start | bytes 9220
  168.0 12.5 %copy-start.18 = (f32[96]{0:T(128)}, f32[96]{0:T(128)S(1)}, u32[]{:S(2)}) copy-start(f32[96]{0:T(128)S(1)} %convert_element_type.107) | copy-start | bytes 1156
  168.1 213.8 %copy-start.11 = (s32[768]{0:T(1024)}, s32[768]{0:T(1024)S(1)}, u32[]{:S(2)}) copy-start(s32[768]{0:T(1024)S(1)} %eq.39) | copy-start | bytes 9220
  179.6 8.8 %copy-start.16 = (s32[512]{0:T(512)}, s32[512]{0:T(512)S(1)}, u32[]{:S(2)}) copy-start(s32[512]{0:T(512)S(1)} %iota_add_fusion) | copy-start | bytes 6148
  180.7 7.7 %slice-start = ((s8[8388608]{0:T(1024)(128)(4,1)}), s8[4194304]{0:T(1024)(128)(4,1)S(1)}, s32[]{:S(2)}) async-start(s8[8388608]{0:T(1024)(128)(4,1)} %bitcast.64), calls=%async_computation.4 | async-start | bytes 8388608
  182.7 5.8 %slice-start.1 = ((s8[8388608]{0:T(1024)(128)(4,1)}), s8[4194304]{0:T(1024)(128)(4,1)S(1)}, s32[]{:S(2)}) async-start(s8[8388608]{0:T(1024)(128)(4,1)} %bitcast.64), calls=%async_computation.5 | async-start | bytes 8388608
  324.8 19.9 %copy-start.4 = (bf16[8192,256]{1,0:T(8,128)(2,1)S(1)}, bf16[8192,256]{1,0:T(8,128)(2,1)}, u32[]{:S(2)}) copy-start(bf16[8192,256]{1,0:T(8,128)(2,1)} %param.25) | copy-start | bytes 12582916
  345.6 4.9 %copy-start.15 = (f32[64]{0:T(128)S(1)}, f32[64]{0:T(128)}, u32[]{:S(2)}) copy-start(f32[64]{0:T(128)} %copy-done.14) | copy-start | bytes 772
  345.6 4.9 %copy-start.19 = (f32[96]{0:T(128)S(1)}, f32[96]{0:T(128)}, u32[]{:S(2)}) copy-start(f32[96]{0:T(128)} %copy-done.18) | copy-start | bytes 1156
  385.2 33.8 %copy-start.7 = (bf16[1,128,512]{2,1,0:T(8,128)(2,1)S(1)}, bf16[1,128,512]{2,1,0:T(8,128)(2,1)}, u32[]{:S(2)}) copy-start(bf16[1,128,512]{2,1,0:T(8,128)(2,1)} %copy.100) | copy-start | bytes 393220
  385.2 33.8 %copy-start.8 = (bf16[1,128,512]{2,1,0:T(8,128)(2,1)S(1)}, bf16[1,128,512]{2,1,0:T(8,128)(2,1)}, u32[]{:S(2)}) copy-start(bf16[1,128,512]{2,1,0:T(8,128)(2,1)} %copy.101) | copy-start | bytes 393220
  385.2 33.8 %copy-start.9 = (bf16[1,128,512]{2,1,0:T(8,128)(2,1)S(1)}, bf16[1,128,512]{2,1,0:T(8,128)(2,1)}, u32[]{:S(2)}) copy-start(bf16[1,128,512]{2,1,0:T(8,128)(2,1)} %copy.102) | copy-start | bytes 393220
  385.2 33.8 %copy-start.10 = (bf16[1,128,512]{2,1,0:T(8,128)(2,1)S(1)}, bf16[1,128,512]{2,1,0:T(8,128)(2,1)}, u32[]{:S(2)}) copy-start(bf16[1,128,512]{2,1,0:T(8,128)(2,1)} %copy.103) | copy-start | bytes 393220
  385.2 33.8 %copy-start.12 = (s32[768]{0:T(1024)S(1)}, s32[768]{0:T(1024)}, u32[]{:S(2)}) copy-start(s32[768]{0:T(1024)} %copy-done.11) | copy-start | bytes 9220
  385.2 33.8 %copy-start.17 = (s32[512]{0:T(512)S(1)}, s32[512]{0:T(512)}, u32[]{:S(2)}) copy-start(s32[512]{0:T(512)} %copy-done.16) | copy-start | bytes 6148
  385.2 33.8 %copy-start.22 = (pred[512]{0:T(512)(128)(4,1)S(1)}, pred[512]{0:T(512)(128)(4,1)}, u32[]{:S(2)}) copy-start(pred[512]{0:T(512)(128)(4,1)} %compare_reduce_fusion) | copy-start | bytes 1540
  387.2 58.4 %copy-start.1 = (bf16[1280,480]{0,1:T(8,128)(2,1)S(1)}, bf16[1280,480]{0,1:T(8,128)(2,1)}, u32[]{:S(2)}) copy-start(bf16[1280,480]{0,1:T(8,128)(2,1)} %param.15) | copy-start | bytes 3686404
Sparse Core Ops, SparseCore 0:
  9.5 60.1 all-gather.2
  99.4 46.2 all-gather.4
  167.8 80.4 reduce-scatter.1
where the time goes:
time: 459 us; the launch traced here: 453 us
  blocking collectives  271 us (59%)
  other arithmetic  41.6 us (9%)
  matrix products  38.9 us (8%)
  Pallas kernels  37.5 us (8%)
  local copies, waits for them, and re-layouts  26.1 us (6%)
  waiting for transfers between devices  20.9 us (5%)
  between operations  14.3 us (3%)
    all_gather x4, blocking collectives, local(): lax.all_gather(rows, 'seq', axis=0)  127 us
    all_gather x1, blocking collectives, local(): key_all = lax.all_gather(vit_key, 'frame', axis=0, tiled=True)  50.8 us
    all_gather x1, blocking collectives, local(): vision_query = lax.all_gather(vision_query, 'seq', axis=0, tiled=True)  31.8 us
    all_gather x1, blocking collectives, local(): vision_pair = lax.all_gather(vision_pair, 'seq', axis=0, tiled=True)  31 us
    pallas_call x1, Pallas kernels, causal_attention(): pl.pallas_call(causal_kernel, grid=(width // HDIM,), in_specs=[pl.BlockSp...  25.1 us
    all_gather x1, waiting for transfers between devices, local(): context_all = lax.all_gather(vit_context.T, 'seq', axis=0, tiled=True)  20.9 us
    all_gather x2, blocking collectives, local(): lax.all_gather(piece, 'frame', axis=0, tiled=True)  17.3 us
    all_gather x1, blocking collectives, local(): value_all = lax.all_gather(vit_value, 'frame', axis=0, tiled=True)  13.3 us
  transfers between devices with their start and end apart: 5, of which 1 were waited for; matrix products, arithmetic and copies ran while one was open for 15% of the time, Pallas kernels for 3%

commit v1 on v0

v1 whole, which is shorter than its diff:
```python
import functools
import math

import jax
import jax.numpy as jnp
from jax import lax
from jax.experimental import pallas as pl
from jax.experimental.pallas import tpu as pltpu
from jax.sharding import PartitionSpec as P

VIT_HDIM = 80
HDIM = 128


epsilon = 1e-06
rope_base = 1000000.0
lowest = -1e30
vmem_limit = 56 * 1024 * 1024


def rms_scale(matrix, scales):
    widened = matrix.astype(jnp.float32)
    factor = lax.rsqrt(jnp.mean(widened * widened, axis=-1, keepdims=True) + epsilon)
    return widened * factor * scales


MESH = pl.DeviceIdType.MESH
ANY = pl.BlockSpec(memory_space=pl.ANY)
VMEM = pl.BlockSpec(memory_space=pltpu.VMEM)


def ring_grid(count):
    narrow = 1 << ((count.bit_length() - 1) // 2)
    return count // narrow, narrow


def ring_position(index, count):
    tall, narrow = ring_grid(count)
    if narrow < 2 or tall % 2:
        return index
    row, column = lax.div(index, narrow), lax.rem(index, narrow)
    odd = lax.rem(row, 2)
    inner = lax.div(column + narrow - 1, narrow)
    along = (column - 1) * (1 - odd) + (narrow - 1 - column) * odd
    return (1 - inner) * (count - 1 - row) + inner * (row * (narrow - 1) + along)


def ring_index(position, count):
    tall, narrow = ring_grid(count)
    if narrow < 2 or tall % 2:
        return position
    back = lax.div(position, tall * (narrow - 1))
    row, along = lax.div(position, narrow - 1), lax.rem(position, narrow - 1)
    odd = lax.rem(row, 2)
    column = 1 + along * (1 - odd) + (narrow - 2 - along) * odd
    return (1 - back) * (row * narrow + column) + back * (count - 1 - position) * narrow


class Ring:
    def __init__(self, count):
        self.count = count
        self.here = ring_position(lax.axis_index("seq"), count)
        self.right = {"seq": self.index(1)}
        self.left = {"seq": self.index(-1)}

    def index(self, offset):
        return ring_index(lax.rem(self.here + (offset + 2 * self.count), self.count), self.count)


def greet(partners):
    barrier = pltpu.get_barrier_semaphore()
    for partner in partners:
        pl.semaphore_signal(barrier, inc=1, device_id=partner, device_id_type=MESH)
    pl.semaphore_wait(barrier, len(partners))


def remote(source, target, send, recv, partner):
    return pltpu.make_async_remote_copy(
        src_ref=source,
        dst_ref=target,
        send_sem=send,
        recv_sem=recv,
        device_id=partner,
        device_id_type=MESH,
    )


class RingGather:
    def __init__(self, ring, block, out, send, recv, pieces):
        self.ring, self.block, self.out, self.send, self.recv = ring, block, out, send, recv
        self.pieces = pieces
        self.steps = ring.count // 2

    def moves(self, step):
        last = step == self.steps - 1
        for piece in range(self.pieces):
            if not last or piece < self.pieces // 2:
                yield 0, piece
            if not last or piece >= self.pieces // 2:
                yield 1, piece

    def copy(self, step, way, piece):
        offset = -step if way == 0 else step
        owner = self.ring.index(offset)
        source = self.block.at[piece] if step == 0 else self.out(owner, piece)
        return remote(
            source,
            self.out(owner, piece),
            self.send.at[way, step, piece],
            self.recv.at[way, step, piece],
            self.ring.right if way == 0 else self.ring.left,
        )

    def start(self):
        for way, piece in self.moves(0):
            self.copy(0, way, piece).start()

    def advance(self, step, landed=None):
        ahead = list(self.moves(step + 1)) if step + 1 < self.steps else []
        for way, piece in self.moves(step):
            self.copy(step, way, piece).wait_recv()
            if (way, piece) in ahead:
                self.copy(step + 1, way, piece).start()
            if landed is not None:
                landed(self.ring.index(-(step + 1) if way == 0 else step + 1), piece, way, step)

    def finish(self):
        for step in range(self.steps):
            for way, piece in self.moves(step):
                self.copy(step, way, piece).wait_send()


def ring_sems(count, pieces):
    return [pltpu.SemaphoreType.DMA((2, count // 2, pieces))] * 2


class FrameGather:
    def __init__(self, count, block, out, sends, recvs, pieces):
        self.block, self.out, self.pieces = block, out, pieces
        self.sends, self.recvs = sends, recvs
        self.chips = count // 2
        me = lax.axis_index("frame")
        self.me, self.chip, self.core = me, lax.div(me, 2), lax.rem(me, 2)
        self.twin = {"frame": self.chip * 2 + 1 - self.core}

    def peer(self, distance):
        return lax.rem(self.chip + distance + self.chips, self.chips) * 2 + self.core

    def partners(self):
        return [self.twin] + [{"frame": self.peer(d)} for d in range(1, self.chips)]

    def across(self, distance, piece):
        return remote(
            self.block.at[piece],
            self.out.at[self.me, piece],
            self.sends.at[0, distance, piece],
            self.recvs.at[0, distance, piece],
            {"frame": self.peer(distance)},
        )

    def inside(self, distance, piece):
        slot = self.peer(-distance)
        return remote(
            self.block.at[piece] if distance == 0 else self.out.at[slot, piece],
            self.out.at[slot, piece],
            self.sends.at[1, distance, piece],
            self.recvs.at[1, distance, piece],
            self.twin,
        )

    def start(self):
        for piece in range(self.pieces):
            for d in range(1, self.chips):
                self.across(d, piece).start()
        for piece in range(self.pieces):
            self.inside(0, piece).start()

    def relay(self, piece):
        for d in range(1, self.chips):
            self.across(d, piece).wait_recv()
            self.inside(d, piece).start()

    def finish(self):
        for piece in range(self.pieces):
            for d in range(self.chips):
                self.inside(d, piece).wait()
                if d:
                    self.across(d, piece).wait_send()


def frame_sems(count, pieces):
    return [pltpu.SemaphoreType.DMA((2, count // 2, pieces))] * 2


def comm_params(collective):
    return pltpu.CompilerParams(
        collective_id=collective, has_side_effects=True, vmem_limit_bytes=vmem_limit
    )


def ring_gather_kernel(count, block, out, send, recv, own):
    ring = Ring(count)
    gather = RingGather(ring, block, lambda i, piece: out.at[i, piece], send, recv, block.shape[0])
    greet([ring.left, ring.right])
    gather.start()
    keep = pltpu.make_async_copy(block, out.at[ring.index(0)], own)
    keep.start()
    for step in range(gather.steps):
        gather.advance(step)
    keep.wait()
    gather.finish()


def ring_gather(block, count, collective):
    pieces = block.shape[0]
    return pl.pallas_call(
        functools.partial(ring_gather_kernel, count),
        in_specs=[VMEM],
        out_specs=ANY,
        out_shape=jax.ShapeDtypeStruct((count,) + block.shape, block.dtype),
        scratch_shapes=ring_sems(count, pieces) + [pltpu.SemaphoreType.DMA],
        compiler_params=comm_params(collective),
    )(block)


def frame_gather_kernel(count, block, out, send, recv, own):
    gather = FrameGather(count, block, out, send, recv, block.shape[0])
    greet(gather.partners())
    gather.start()
    keep = pltpu.make_async_copy(block, out.at[gather.me], own)
    keep.start()
    for piece in range(gather.pieces):
        gather.relay(piece)
    keep.wait()
    gather.finish()


def frame_gather(block, count, collective):
    pieces = block.shape[0]
    return pl.pallas_call(
        functools.partial(frame_gather_kernel, count),
        in_specs=[VMEM],
        out_specs=ANY,
        out_shape=jax.ShapeDtypeStruct((count,) + block.shape, block.dtype),
        scratch_shapes=frame_sems(count, pieces) + [pltpu.SemaphoreType.DMA],
        compiler_params=comm_params(collective),
    )(block)


def front_kernel(seq_count, frame_count, pair, weight, pair_out, weight_out, *sems):
    fsend, frecv, rsend, rrecv, tsend, trecv, own = sems
    ring = Ring(seq_count)
    frames = FrameGather(frame_count, pair, pair_out, fsend, frecv, pair.shape[0])
    core, twin = frames.core, frames.twin
    quarter = weight.shape[1]
    half = weight.at[core]
    gather = RingGather(
        ring, half, lambda i, piece: weight_out.at[i, core, piece], rsend, rrecv, quarter
    )
    greet([ring.left, ring.right] + frames.partners())
    frames.start()
    gather.start()
    here = ring.index(0)
    keep = [
        pltpu.make_async_copy(pair, pair_out.at[frames.me], own.at[0]),
        pltpu.make_async_copy(weight, weight_out.at[here], own.at[1]),
    ]
    for copy in keep:
        copy.start()
    handed = []

    def landed(index, piece, way, step):
        copy = remote(
            weight_out.at[index, core, piece],
            weight_out.at[index, core, piece],
            tsend.at[way, step, piece],
            trecv.at[way, step, piece],
            twin,
        )
        copy.start()
        handed.append(copy)

    for step in range(max(gather.steps, frames.pieces)):
        if step < frames.pieces:
            frames.relay(step)
        if step < gather.steps:
            gather.advance(step, landed)
    for copy in keep:
        copy.wait()
    frames.finish()
    gather.finish()
    for copy in handed:
        copy.wait()


def front(pair, weight, seq_count, frame_count, collective):
    quarter = 2
    weight = weight.reshape(2, quarter, -1, weight.shape[1])
    pair_out, weight_out = pl.pallas_call(
        functools.partial(front_kernel, seq_count, frame_count),
        in_specs=[VMEM, VMEM],
        out_specs=[ANY, ANY],
        out_shape=[
            jax.ShapeDtypeStruct((frame_count,) + pair.shape, pair.dtype),
            jax.ShapeDtypeStruct((seq_count,) + weight.shape, weight.dtype),
        ],
        scratch_shapes=frame_sems(frame_count, pair.shape[0])
        + ring_sems(seq_count, quarter) * 2
        + [pltpu.SemaphoreType.DMA((2,))],
        compiler_params=comm_params(collective),
    )(pair, weight)
    return pair_out, weight_out.reshape(-1, weight.shape[-1])


def vit_attention_kernel(own_ref, ids_ref, q_ref, kv_ref, out_ref):
    frames, heads, _, rows = kv_ref.shape
    allowed = ids_ref[...] == own_ref[...]
    for head in range(heads):
        spread = slice(head * VIT_HDIM, (head + 1) * VIT_HDIM)
        queries = q_ref[spread, :]
        scores = jnp.concatenate(
            [
                lax.dot_general(
                    kv_ref[f, head, :VIT_HDIM, :],
                    queries,
                    (((0,), (0,)), ((), ())),
                    preferred_element_type=jnp.float32,
                )
                for f in range(frames)
            ],
            axis=0,
        )
        scores = jnp.where(allowed, scores, lowest)
        highest = jnp.max(scores, axis=0, keepdims=True)
        weights = jnp.exp((scores - highest) * VIT_HDIM ** (-0.5))
        row_sum = jnp.sum(weights, axis=0, keepdims=True)
        weights = weights.astype(jnp.bfloat16)
        mixed = sum(
            jnp.dot(
                kv_ref[f, head, VIT_HDIM:, :],
                weights[f * rows : (f + 1) * rows],
                preferred_element_type=jnp.float32,
            )
            for f in range(frames)
        )
        out_ref[spread, :] = (mixed / row_sum).astype(out_ref.dtype)


def vit_attention(own_ids, all_ids, queries, pairs):
    width, rows = queries.shape
    keys = all_ids.shape[0]
    step = math.gcd(rows, 256)
    return pl.pallas_call(
        vit_attention_kernel,
        grid=(rows // step,),
        in_specs=[
            pl.BlockSpec((1, step), lambda i: (0, i)),
            pl.BlockSpec((keys, 1), lambda i: (0, 0)),
            pl.BlockSpec((width, step), lambda i: (0, i)),
            pl.BlockSpec(pairs.shape, lambda i: (0, 0, 0, 0)),
        ],
        out_specs=pl.BlockSpec((width, step), lambda i: (0, i)),
        out_shape=jax.ShapeDtypeStruct((width, rows), jnp.bfloat16),
        compiler_params=pltpu.CompilerParams(vmem_limit_bytes=vmem_limit),
    )(own_ids[None, :], all_ids[:, None], queries, pairs)


def scatter_kernel(count, hidden, weight, gain, out, held, part, stage, land, load, send, recv):
    ring = Ring(count)
    width = weight.shape[1]
    pieces = held.shape[0]
    span = width // pieces
    share = out.shape[0]
    order = [piece for pair in zip(range(pieces // 2), range(pieces // 2, pieces)) for piece in pair]
    loads = {
        piece: pltpu.make_async_copy(
            weight.at[:, pl.ds(piece * span, span)], held.at[piece], load.at[piece]
        )
        for piece in order
    }
    for piece in order:
        loads[piece].start()
    greet([ring.left, ring.right])
    forward = [piece < pieces // 2 for piece in range(pieces)]

    def hop(piece, step):
        return remote(
            stage.at[piece, step],
            land.at[piece, step],
            send.at[piece, step],
            recv.at[piece, step],
            ring.right if forward[piece] else ring.left,
        )

    for piece in order:
        loads[piece].wait()
        product = jnp.dot(hidden[...], held[piece], preferred_element_type=jnp.float32)
        for i in range(count):
            part[piece, i] = product[i * share : (i + 1) * share]
        first = ring.index(-1 if forward[piece] else 1)
        stage[piece, 0] = part[piece, first].astype(jnp.bfloat16)
        hop(piece, 0).start()

    def body(step, carry):
        for piece in order:
            hop(piece, step - 1).wait_recv()
            turn = -1 - step if forward[piece] else 1 + step
            owner = ring.index(turn)
            total = land[piece, step - 1].astype(jnp.float32) + part[piece, owner]
            stage[piece, step] = total.astype(jnp.bfloat16)
            hop(piece, step).start()
        return carry

    lax.fori_loop(1, count - 1, body, 0)
    here = ring.index(0)
    squares = jnp.zeros((share, 1), jnp.float32)
    for piece in order:
        hop(piece, count - 2).wait_recv()
        total = land[piece, count - 2].astype(jnp.float32) + part[piece, here]
        total = total.astype(jnp.bfloat16).astype(jnp.float32)
        part[piece, here] = total
        squares += jnp.sum(total * total, axis=1, keepdims=True)
    factor = lax.rsqrt(squares / width + epsilon)
    for piece in order:
        columns = slice(piece * span, (piece + 1) * span)
        out[:, columns] = (part[piece, here] * factor * gain[:, columns]).astype(out.dtype)

    def drain(step, carry):
        for piece in order:
            hop(piece, step).wait_send()
        return carry

    lax.fori_loop(0, count - 1, drain, 0)


def scatter(hidden, weight, gain, count, collective):
    rows, depth = hidden.shape
    width = weight.shape[1]
    share = rows // count
    pieces = 4
    span = width // pieces
    return pl.pallas_call(
        functools.partial(scatter_kernel, count),
        in_specs=[VMEM, ANY, VMEM],
        out_specs=VMEM,
        out_shape=jax.ShapeDtypeStruct((share, width), jnp.bfloat16),
        scratch_shapes=[
            pltpu.VMEM((pieces, depth, span), jnp.bfloat16),
            pltpu.VMEM((pieces, count, share, span), jnp.float32),
            pltpu.VMEM((pieces, count - 1, share, span), jnp.bfloat16),
            pltpu.VMEM((pieces, count - 1, share, span), jnp.bfloat16),
            pltpu.SemaphoreType.DMA((pieces,)),
            pltpu.SemaphoreType.DMA((pieces, count - 1)),
            pltpu.SemaphoreType.DMA((pieces, count - 1)),
        ],
        compiler_params=comm_params(collective),
    )(hidden, weight, gain[None, :])


def turns(positions):
    inverse = rope_base ** (-2.0 * jnp.arange(HDIM // 2, dtype=jnp.float32) / HDIM)
    angles = positions.astype(jnp.float32)[:, None] * inverse[None, :]
    cosine, sine_part = jnp.cos(angles), jnp.sin(angles)
    return jnp.concatenate([cosine, cosine], axis=1), jnp.concatenate([-sine_part, sine_part], axis=1)


def project_kernel(blocks, *refs):
    tokens, (where, qw, kw, cosine, sine_part, q_out, pair_out, q_acc, p_acc) = refs[:blocks], refs[blocks:]
    step = pl.program_id(0)
    rows = jnp.concatenate([ref[...] for ref in tokens], axis=0)
    q_part = jnp.dot(rows, qw[...], preferred_element_type=jnp.float32)
    p_part = jnp.dot(rows, kw[...], preferred_element_type=jnp.float32)

    @pl.when(step == 0)
    def _():
        q_acc[...] = q_part
        p_acc[...] = p_part

    @pl.when(step > 0)
    def _():
        q_acc[...] += q_part
        p_acc[...] += p_part

    @pl.when(step == pl.num_programs(0) - 1)
    def _():
        share = tokens[0].shape[0]
        for block in range(blocks):
            source = slice(block * share, (block + 1) * share)
            target = pl.ds(pl.multiple_of(where[block] * share, share), share)
            turn, slide = cosine[target, :], sine_part[target, :]
            for head in range(q_acc.shape[1] // HDIM):
                columns = slice(head * HDIM, (head + 1) * HDIM)
                values = q_acc[source, columns]
                q_out[target, columns] = (
                    values * turn + pltpu.roll(values, HDIM // 2, 1) * slide
                ).astype(q_out.dtype)
            values = p_acc[source, :HDIM]
            pair_out[target, :HDIM] = (
                values * turn + pltpu.roll(values, HDIM // 2, 1) * slide
            ).astype(pair_out.dtype)
            pair_out[target, HDIM:] = p_acc[source, HDIM:].astype(pair_out.dtype)


def project(blocks, where, positions, query_weight, keyvalue_weight):
    share, depth = blocks[0].shape
    rows = share * len(blocks)
    queries, pairs = query_weight.shape[1], keyvalue_weight.shape[1]
    slab = math.gcd(depth, 1024)
    cosine, sine_part = turns(positions)
    whole = lambda shape: pl.BlockSpec(shape, lambda k: (0, 0))
    return pl.pallas_call(
        functools.partial(project_kernel, len(blocks)),
        grid=(depth // slab,),
        in_specs=[pl.BlockSpec((share, slab), lambda k: (0, k))] * len(blocks)
        + [
            pl.BlockSpec(memory_space=pltpu.SMEM),
            pl.BlockSpec((slab, queries), lambda k: (k, 0)),
            pl.BlockSpec((slab, pairs), lambda k: (k, 0)),
            whole((rows, HDIM)),
            whole((rows, HDIM)),
        ],
        out_specs=[whole((rows, queries)), whole((rows, pairs))],
        out_shape=[
            jax.ShapeDtypeStruct((rows, queries), jnp.bfloat16),
            jax.ShapeDtypeStruct((rows, pairs), jnp.bfloat16),
        ],
        scratch_shapes=[
            pltpu.VMEM((rows, queries), jnp.float32),
            pltpu.VMEM((rows, pairs), jnp.float32),
        ],
        compiler_params=pltpu.CompilerParams(vmem_limit_bytes=vmem_limit),
    )(*blocks, where, query_weight, keyvalue_weight, cosine, sine_part)


def causal_kernel(block_ref, q_ref, k_ref, v_ref, out_ref):
    rows = q_ref.shape[0]
    queries = q_ref[...]

    def fold(start, state_in, masked):
        running_max, running_sum, weighted = state_in
        scores = lax.dot_general(
            queries,
            k_ref[pl.ds(start, rows), :],
            (((1,), (1,)), ((), ())),
            preferred_element_type=jnp.float32,
        )
        if masked:
            row_id = lax.broadcasted_iota(jnp.int32, (rows, rows), 0)
            column_id = lax.broadcasted_iota(jnp.int32, (rows, rows), 1)
            scores = jnp.where(row_id >= column_id, scores, lowest)
        new_max = jnp.maximum(running_max, jnp.max(scores, axis=1, keepdims=True))
        weights = jnp.exp((scores - new_max) * HDIM ** (-0.5))
        shrink = jnp.exp((running_max - new_max) * HDIM ** (-0.5))
        running_sum = running_sum * shrink + jnp.sum(weights, axis=1, keepdims=True)
        update = jnp.dot(
            weights.astype(jnp.bfloat16),
            v_ref[pl.ds(start, rows), :],
            preferred_element_type=jnp.float32,
        )
        return (new_max, running_sum, weighted * shrink + update)

    state = (
        jnp.full((rows, 1), lowest, jnp.float32),
        jnp.zeros((rows, 1), jnp.float32),
        jnp.zeros((rows, HDIM), jnp.float32),
    )
    own = block_ref[0]
    state = fold(pl.multiple_of(own * rows, rows), state, True)
    _, running_sum, weighted = lax.fori_loop(
        0, own, lambda i, now: fold(pl.multiple_of(i * rows, rows), now, False), state
    )
    out_ref[...] = (weighted / running_sum).astype(out_ref.dtype)


def causal_attention(block_index, queries, key_rows, value_rows):
    rows, width = queries.shape
    keys = key_rows.shape[0]
    return pl.pallas_call(
        causal_kernel,
        grid=(width // HDIM,),
        in_specs=[
            pl.BlockSpec(memory_space=pltpu.SMEM),
            pl.BlockSpec((rows, HDIM), lambda h: (0, h)),
            pl.BlockSpec((keys, HDIM), lambda h: (0, 0)),
            pl.BlockSpec((keys, HDIM), lambda h: (0, 0)),
        ],
        out_specs=pl.BlockSpec((rows, HDIM), lambda h: (0, h)),
        out_shape=jax.ShapeDtypeStruct((rows, width), jnp.bfloat16),
        compiler_params=pltpu.CompilerParams(vmem_limit_bytes=vmem_limit),
    )(block_index[None], queries, key_rows, value_rows)


def place(token_pos, first, text_rows, vision_rows):
    spots = first + jnp.arange(text_rows.shape[0], dtype=jnp.int32)
    hit = spots[:, None] == token_pos[None, :]
    moved = jnp.dot(hit.astype(jnp.bfloat16), vision_rows, preferred_element_type=jnp.float32)
    taken = jnp.any(hit, axis=1, keepdims=True)
    return jnp.where(taken, moved.astype(jnp.bfloat16), text_rows)


def local(
    patches,
    vit_gain,
    vision_qkv,
    vision_out,
    video_ids,
    merge_gain,
    merge_up,
    merge_down,
    vision_pos,
    text_embed,
    llm_gain,
    query_weight,
    keyvalue_weight,
):
    frame_index = lax.axis_index("frame")
    seq_index = lax.axis_index("seq")
    frame_count = lax.axis_size("frame")
    seq_count = lax.axis_size("seq")
    patch_rows = patches.shape[0]
    local_heads = vision_qkv.shape[1] // (3 * VIT_HDIM)
    barrier = lax.optimization_barrier

    normed_patches = rms_scale(patches, vit_gain).astype(jnp.bfloat16)
    projected = lax.dot_general(
        vision_qkv, normed_patches, (((0,), (1,)), ((), ())), preferred_element_type=jnp.float32
    ).astype(jnp.bfloat16)
    projected = projected.reshape(local_heads, 3 * VIT_HDIM, patch_rows)
    vit_query = projected[:, :VIT_HDIM].reshape(local_heads * VIT_HDIM, patch_rows)
    patch_video = jnp.repeat(video_ids, 4)
    own_video = lax.dynamic_slice_in_dim(patch_video, frame_index * patch_rows, patch_rows)
    pair_all, out_full = front(projected[:, VIT_HDIM:], vision_out, seq_count, frame_count, 1)

    text_own = rms_scale(text_embed, llm_gain).astype(jnp.bfloat16)
    text_own, pair_all = barrier((text_own, pair_all))
    text_blocks, owners = [text_own], [0]
    bit = frame_count // 2
    while bit:
        swap = [(i, i ^ bit) for i in range(frame_count)]
        text_blocks = text_blocks + [lax.ppermute(block, "frame", swap) for block in text_blocks]
        owners = owners + [mask ^ bit for mask in owners]
        bit //= 2

    vit_context = vit_attention(own_video, patch_video, vit_query, pair_all)
    pieces = vit_context.reshape(2, -1, patch_rows)
    context_all = ring_gather(pieces, seq_count, 2).reshape(-1, patch_rows)
    head_total = lax.dot_general(
        context_all, out_full, (((0,), (0,)), ((), ())), preferred_element_type=jnp.float32
    )
    vit_output = patches.astype(jnp.float32) + head_total
    merged_input = (
        rms_scale(vit_output, merge_gain).astype(jnp.bfloat16).reshape(patch_rows // 4, -1)
    )
    merge_hidden = jax.nn.gelu(
        jnp.dot(merged_input, merge_up, preferred_element_type=jnp.float32), approximate=False
    ).astype(jnp.bfloat16)
    vision_normed = scatter(merge_hidden, merge_down, llm_gain, seq_count, 3)

    part_rows = text_embed.shape[0]
    seq_block = part_rows * frame_count
    first = seq_index * seq_block
    where = jnp.bitwise_xor(frame_index, jnp.array(owners, jnp.int32))
    text_blocks[-1], vision_normed = barrier((text_blocks[-1], vision_normed))
    text_query, text_pair = project(
        text_blocks, where, first + jnp.arange(seq_block, dtype=jnp.int32), query_weight, keyvalue_weight
    )
    text_pair_all = ring_gather(text_pair.reshape(2, seq_block // 2, -1), seq_count, 4)
    text_pair_all = text_pair_all.reshape(seq_count * seq_block, -1)

    share = vision_normed.shape[0]
    vision_normed, text_pair_all = barrier((vision_normed, text_pair_all))
    halves = vision_normed.reshape(share, 2, -1).transpose(1, 0, 2)
    vision_tokens = frame_gather(halves, frame_count, 5).transpose(0, 2, 1, 3)
    vision_tokens = vision_tokens.reshape(frame_count * share, -1)
    token_pos = vision_pos.reshape(frame_count, seq_count, share).transpose(1, 0, 2)
    here = lax.dynamic_index_in_dim(token_pos, seq_index, 0, keepdims=False).reshape(-1)
    vision_query, vision_pair = project(
        [vision_tokens], jnp.zeros((1,), jnp.int32), here, query_weight, keyvalue_weight
    )
    vision_both = jnp.concatenate([vision_query, vision_pair], axis=1)
    gathered = ring_gather(vision_both.reshape(2, frame_count * share // 2, -1), seq_count, 6)
    gathered = gathered.reshape(seq_count * frame_count * share, -1)
    width = vision_query.shape[1]
    token_pos = token_pos.reshape(-1)
    llm_query = place(token_pos, first, text_query, gathered[:, :width])
    llm_pair = place(token_pos, 0, text_pair_all, gathered[:, width:])
    return causal_attention(seq_index, llm_query, llm_pair[:, :HDIM], llm_pair[:, HDIM:])


def solution(mesh):
    return jax.shard_map(
        local,
        mesh=mesh,
        in_specs=(
            P("frame", None),
            P(),
            P(None, "seq"),
            P("seq", None),
            P(),
            P(),
            P(None, "seq"),
            P("seq", None),
            P(),
            P(("seq", "frame"), None),
            P(),
            P(None, "frame"),
            P(None, "frame"),
        ),
        out_specs=P("seq", "frame"),
        check_vma=False,
    )
```

time: 459 us -> 267 us (0.58); the launches traced: 453 us -> 266 us
  blocking collectives: 271 us -> 0 us
  Pallas kernels: 37.5 us -> 212 us
  other arithmetic: 41.6 us -> 12.9 us
  waiting for transfers between devices: 20.9 us -> 0.01 us
  matrix products: 38.9 us -> 21.4 us
  between operations: 14.3 us -> 0.33 us
  local copies, waits for them, and re-layouts: 26.1 us -> 19.1 us
    all_gather x10 -> x0, blocking collectives: 271 us -> none  [the longest x4 127 us: local(): lax.all_gather(rows, 'seq', axis=0)]
    pallas_call x0 -> x8, Pallas kernels: none -> 174 us  [the longest x3 69.8 us: ring_gather(): pl.pallas_call(functools.partial(ring_gather_kernel, count), in_specs=[VM...]
    convert_element_type x6 -> x3, other arithmetic: 24.3 us -> 0.61 us  [the longest x1 0.58 us: local(): text_own = rms_scale(text_embed, llm_gain).astype(jnp.bfloat16)]
    all_gather x2 -> x0, waiting for transfers between devices: 20.9 us -> none  [the longest x1 20.9 us: local(): context_all = lax.all_gather(vit_context.T, 'seq', axis=0, tiled=True)]
    dot_general x6 -> x2, matrix products: 28.6 us -> 9.78 us  [the longest x1 6.85 us: local(): jnp.dot(merged_input, merge_up, preferred_element_type=jnp.float32)]
    dot_general x1 -> x0, local copies, waits for them, and re-layouts: 11.5 us -> none  [project(): jnp.dot(tokens, query_weight, preferred_element_type=jnp.float32)]
    reduce_sum x3 -> x2, other arithmetic: 8.18 us -> 2.58 us  [rms_scale(): jnp.mean(widened * widened, axis=-1, keepdims=True) + epsilon]
  transfers between devices with their start and end apart: 5 -> 3, of which waited for: 1 -> 0; matrix products, arithmetic and copies ran while one was open for 15% -> 10% of each run, Pallas kernels for 3% -> 28%
where the time goes in v1:
time: 267 us; the launch traced here: 266 us
  Pallas kernels  212 us (79%)
  matrix products  21.4 us (8%)
  local copies, waits for them, and re-layouts  19.1 us (7%)
  other arithmetic  12.9 us (5%)
    pallas_call x3, Pallas kernels, ring_gather(): pl.pallas_call(functools.partial(ring_gather_kernel, count), in_specs=[VM...  69.8 us
    pallas_call x1, Pallas kernels, scatter(): pl.pallas_call(functools.partial(scatter_kernel, count), in_specs=[VMEM,...  38.6 us
    pallas_call x1, Pallas kernels, front(): pl.pallas_call(functools.partial(front_kernel, seq_count, frame_count), i...  27.7 us
    pallas_call x1, Pallas kernels, causal_attention(): pl.pallas_call(causal_kernel, grid=(width // HDIM,), in_specs=[pl.BlockSp...  25.1 us
    pallas_call x2, Pallas kernels, project(): pl.pallas_call(functools.partial(project_kernel, len(blocks)), grid=(dept...  23.7 us
    pallas_call x1, Pallas kernels, frame_gather(): pl.pallas_call(functools.partial(frame_gather_kernel, count), in_specs=[V...  14.5 us
    pallas_call x1, Pallas kernels, vit_attention(): pl.pallas_call(vit_attention_kernel, grid=(rows // step,), in_specs=[pl.B...  12.6 us
    dot_general x1, matrix products, local(): jnp.dot(merged_input, merge_up, preferred_element_type=jnp.float32)  6.85 us
  transfers between devices with their start and end apart: 3, of which 0 were waited for; matrix products, arithmetic and copies ran while one was open for 10% of the time, Pallas kernels for 28%

profile of v1, /device:TPU:28, one launch (start us, length us, event | category | flops | bytes accessed | tf_op | source)
XLA Modules:
  0.0 266.4 jit_solution(11717190905422056805)
XLA Ops:
  0.0 2.1 fusion.8
  2.1 2.9 %fusion.17 = bf16[768,480]{0,1:T(8,128)(2,1)S(1)} fusion(bf16[1280,480]{0,1:T(8,128)(2,1)S(1)} %copy-done, bf16[768,1280]{1,0:T(8,128)(2,1)} %param.14, f32[1280]{0:T(1024)} %param.15, f32[768]{0:T(1024)S(1)} %add_rsqrt_fusion.1), kind=kOutput, calls=%fused_computation.25 | convolution fusion | flops 948019200 | bytes 3940352 | tf_op jit(solution)/shard_map/dot_general | solution.py:625
  5.1 0.9 copy-done.8
  6.0 0.8 slice.24.pair
  7.3 27.7 %shard_map.136 = (bf16[4,2,160,768]{3,2,1,0:T(8,128)(2,1)}, bf16[8,2,2,40,1280]{4,3,2,1,0:T(8,128)(2,1)}) custom-call(bf16[2,160,768]{2,1,0:T(8,128)(2,1)} %slice.24.pair, bf16[2,2,40,1280]{3,2,1,0:T(8,128)(2,1)} %bitcast.46), custom_call_target="tpu_custom_call" | custom-call | tf_op jit(solution)/shard_map/pallas_call | solution.py:299
  36.8 1.6 broadcast_in_dim_reshape.6.ids_ref
  38.3 1.7 slice.25
  40.7 12.6 %shard_map.137 = bf16[160,768]{1,0:T(8,128)(2,1)} custom-call(s32[1,768]{1,0:T(1,128)} %broadcast_in_dim.24.own_ref, s32[3072,1]{1,0:T(8,128)} %broadcast_in_dim_reshape.6.ids_ref, bf16[160,768]{1,0:T(8,128)(2,1)} %bitcast.41, bf16[4,2,160,768]{3,2,1,0:T(8,128)(2,1)} %get-tuple-element.19.kv_ref), custom_call_target="tpu_custom_call" | custom-call | tf_op jit(solution)/shard_map/pallas_call | solution.py:353
  53.3 24.4 %shard_map.138 = bf16[8,2,80,768]{3,2,1,0:T(8,128)(2,1)} custom-call(bf16[2,80,768]{2,1,0:T(8,128)(2,1)} %bitcast.42), custom_call_target="tpu_custom_call" | custom-call | tf_op jit(solution)/shard_map/pallas_call | solution.py:216
  77.7 5.5 %multiply_reduce_fusion = (f32[768]{0:T(1024)S(1)}, f32[768,1280]{1,0:T(8,128)S(1)}) fusion(bf16[1280,768]{1,0:T(8,128)(2,1)} %bitcast.31, bf16[1280,1280]{1,0:T(8,128)(2,1)} %bitcast.35, bf16[768,1280]{1,0:T(8,128)(2,1)S(1)} %copy-done.4), kind=kOutput, calls=%fused_computation.18 | convolution fusion | flops 2520513792 | bytes 11144192 | tf_op jit(solution)/shard_map/dot_general | solution.py:647
  83.3 1.7 multiply_convert_fusion
  84.9 4.1 %reshape.105 = bf16[192,5120]{1,0:T(8,128)(2,1)} reshape(bf16[768,1280]{1,0:T(8,128)(2,1)} %multiply_convert_fusion) | data formatting | bytes 3932160 | tf_op jit(solution)/shard_map/reshape | solution.py:652
  89.4 6.8 %fusion.28.hidden = bf16[192,640]{1,0:T(8,128)(2,1)} fusion(bf16[192,5120]{1,0:T(8,128)(2,1)} %reshape.105, bf16[5120,640]{1,0:T(8,128)(2,1)} %param.20), kind=kOutput, calls=%fused_computation.34 | convolution fusion | flops 1266278400 | bytes 8765440 | tf_op jit(solution)/shard_map/dot_general | solution.py:655
  96.2 38.6 %shard_map.139 = bf16[24,8192]{1,0:T(8,128)(2,1)} custom-call(bf16[192,640]{1,0:T(8,128)(2,1)} %fusion.28.hidden, bf16[640,8192]{1,0:T(8,128)(2,1)} %weight.1, f32[1,8192]{1,0:T(1,128)} %bitcast.48), custom_call_target="tpu_custom_call" | custom-call | tf_op jit(solution)/shard_map/pallas_call | solution.py:442
  135.9 1.0 fusion.37
  136.9 1.0 pad_maximum_fusion
  138.8 1.4 fusion.1
  140.2 1.3 copy-done.5
  141.6 14.4 %shard_map.140 = (bf16[512,512]{1,0:T(8,128)(2,1)}, bf16[512,256]{1,0:T(8,128)(2,1)}) custom-call(bf16[128,8192]{1,0:T(8,128)(2,1)} %copy-done.2, bf16[128,8192]{1,0:T(8,128)(2,1)} %collective-permute-done.refs_1_, bf16[128,8192]{1,0:T(8,128)(2,1)} %collective-permute-done.2.refs_2_, bf16[128,8192]{1,0:T(8,128)(2,1)} %copy-done.5, ...), custom_call_target="tpu_custom_call" | custom-call | tf_op jit(solution)/shard_map/pallas_call | solution.py:511
  156.0 25.2 %shard_map.141 = bf16[8,2,256,256]{3,2,1,0:T(8,128)(2,1)} custom-call(bf16[2,256,256]{2,1,0:T(8,128)(2,1)} %bitcast.47), custom_call_target="tpu_custom_call" | custom-call | tf_op jit(solution)/shard_map/pallas_call | solution.py:216
  181.2 0.8 copy.30
  182.0 14.5 %shard_map.142 = bf16[4,2,24,4096]{3,2,1,0:T(8,128)(2,1)} custom-call(bf16[2,24,4096]{2,1,0:T(8,128)(2,1)} %bitcast.38), custom_call_target="tpu_custom_call" | custom-call | tf_op jit(solution)/shard_map/pallas_call | solution.py:240
  196.4 3.0 %copy.26 = bf16[4,24,2,4096]{3,2,1,0:T(2,128)(2,1)S(1)} copy(bf16[4,24,2,4096]{3,1,2,0:T(8,128)(2,1)} %bitcast.33) | data formatting | bytes 3145728 | tf_op jit(solution)/shard_map/transpose | solution.py:673
  199.5 2.1 copy.28
  201.6 9.3 %shard_map.143 = (bf16[96,512]{1,0:T(8,128)(2,1)}, bf16[96,256]{1,0:T(8,128)(2,1)}) custom-call(bf16[96,8192]{1,0:T(8,128)(2,1)} %bitcast.34, s32[1]{0:T(128)} %constant.104.clone.1.refs_1_, bf16[8192,512]{1,0:T(8,128)(2,1)} %refs_2_.1, bf16[8192,256]{1,0:T(8,128)(2,1)} %refs_3_.1, f32[96,128]{1,0:T(8,128)} %get-tuple-element.41.refs_4_, ...), custom_call_target="tpu_custom_call" | custom-call | tf_op jit(solution)/shard_map/pallas_call | solution.py:511
  210.9 1.7 pad_maximum_fusion.2
  212.6 20.1 %shard_map.144 = bf16[8,2,48,768]{3,2,1,0:T(8,128)(2,1)} custom-call(bf16[2,48,768]{2,1,0:T(8,128)(2,1)} %bitcast.45), custom_call_target="tpu_custom_call" | custom-call | tf_op jit(solution)/shard_map/pallas_call | solution.py:216
  232.8 1.7 fusion.20
  234.6 4.3 %fusion.4 = bf16[4096,256]{1,0:T(8,128)(2,1)S(1)} fusion(bf16[4096,256]{1,0:T(8,128)(2,1)S(1)} %bitcast.36, s32[768]{0:T(1024)S(1)} %eq.29, pred[4096]{0:T(1024)(128)(4,1)S(1)} %fusion.1, bf16[768,768]{1,0:T(8,128)(2,1)} %bitcast.40), kind=kOutput, calls=%fused_computation.10 | convolution fusion | flops 1615855616 | bytes 4594688 | tf_op jit(solution)/shard_map/dot_general | solution.py:596
  238.9 1.5 fusion.40
  240.4 0.9 broadcast_select_fusion.q_ref
  241.3 25.1 %shard_map.145 = bf16[512,512]{1,0:T(8,128)(2,1)} custom-call(s32[1]{0:T(128)} %bitcast.block_ref, bf16[512,512]{1,0:T(8,128)(2,1)} %broadcast_select_fusion.q_ref, bf16[4096,128]{1,0:T(8,128)(2,1)} %get-tuple-element.30.k_ref, bf16[4096,128]{1,0:T(8,128)(2,1)} %get-tuple-element.29.v_ref), custom_call_target="tpu_custom_call" | custom-call | tf_op jit(solution)/shard_map/pallas_call | solution.py:578
  (55 shorter events, 5.2 us)
Async XLA Ops:
  0.0 2.1 copy-start
  2.1 4.6 %copy-start.3 = (bf16[128,8192]{1,0:T(8,128)(2,1)S(1)}, bf16[128,8192]{1,0:T(8,128)(2,1)}, u32[]{:S(2)}) copy-start(bf16[128,8192]{1,0:T(8,128)(2,1)} %param.23) | copy-start | bytes 6291460
  5.1 0.9 copy-start.8
  5.1 29.9 %copy-start.10 = (f32[8192]{0:T(1024)S(1)}, f32[8192]{0:T(1024)}, u32[]{:S(2)}) copy-start(f32[8192]{0:T(1024)} %param.24) | copy-start | bytes 98308
  35.0 1.4 copy-start.12
  35.6 17.7 %copy-start.2 = (bf16[128,8192]{1,0:T(8,128)(2,1)}, bf16[128,8192]{1,0:T(8,128)(2,1)S(1)}, u32[]{:S(2)}) copy-start(bf16[128,8192]{1,0:T(8,128)(2,1)S(1)} %fusion.7.refs_0_) | copy-start | bytes 6291460
  35.6 53.7 %collective-permute-start = (bf16[128,8192]{1,0:T(8,128)(2,1)S(1)}, bf16[128,8192]{1,0:T(8,128)(2,1)}, u32[]{:S(2)}, u32[]{:S(2)}) collective-permute-start(bf16[128,8192]{1,0:T(8,128)(2,1)S(1)} %fusion.7.refs_0_), channel_id=1, source_target_pairs={{0,2},{1,3},{2,0},{3,1},{4,6},{5,7},{6,4},{7,5},{8,10},{9,11},{10,... | collective-permute-start | bytes 6291464 | tf_op jit(solution)/shard_map/ppermute | solution.py:640
  36.3 103.9 %collective-permute-start.2 = (bf16[128,8192]{1,0:T(8,128)(2,1)S(1)}, bf16[128,8192]{1,0:T(8,128)(2,1)}, u32[]{:S(2)}, u32[]{:S(2)}) collective-permute-start(bf16[128,8192]{1,0:T(8,128)(2,1)S(1)} %fusion.7.refs_0_), channel_id=1, source_target_pairs={{0,1},{1,0},{2,3},{3,2},{4,5},{5,4},{6,7},{7,6},{8,9},{9,8},{10,11... | collective-permute-start | bytes 6291464 | tf_op jit(solution)/shard_map/ppermute | solution.py:640
  53.3 24.4 %copy-start.4 = (bf16[768,1280]{1,0:T(8,128)(2,1)S(1)}, bf16[768,1280]{1,0:T(8,128)(2,1)}, u32[]{:S(2)}) copy-start(bf16[768,1280]{1,0:T(8,128)(2,1)} %param.14) | copy-start | bytes 5898244
  77.7 5.5 %copy-start.11 = (f32[1280]{0:T(1024)S(1)}, f32[1280]{0:T(1024)}, u32[]{:S(2)}) copy-start(f32[1280]{0:T(1024)} %param.19) | copy-start | bytes 15364
  84.9 4.1 %copy-start.13 = (s32[768]{0:T(1024)S(1)}, s32[768]{0:T(1024)}, u32[]{:S(2)}) copy-start(s32[768]{0:T(1024)} %param.22) | copy-start | bytes 9220
  89.3 50.9 %collective-permute-start.1 = (bf16[128,8192]{1,0:T(8,128)(2,1)}, bf16[128,8192]{1,0:T(8,128)(2,1)S(1)}, u32[]{:S(2)}, u32[]{:S(2)}) collective-permute-start(bf16[128,8192]{1,0:T(8,128)(2,1)} %collective-permute-done.refs_1_), channel_id=1, source_target_pairs={{0,1},{1,0},{2,3},{3,2},{4,5},{5,4},{6,7},{7,6},{8,9},{9,8},{10,11... | collective-permute-start | bytes 6291464 | tf_op jit(solution)/shard_map/ppermute | solution.py:640
  134.9 3.4 %copy-start.14 = (s32[4]{0:T(128)S(1)}, s32[4]{0:T(128)}, u32[]{:S(2)}) copy-start(s32[4]{0:T(128)} %constant.106.clone) | copy-start | bytes 52
  140.2 1.3 copy-start.5
  156.0 25.2 %copy-start.7 = (bf16[24,8192]{1,0:T(8,128)(2,1)S(1)}, bf16[24,8192]{1,0:T(8,128)(2,1)}, u32[]{:S(2)}) copy-start(bf16[24,8192]{1,0:T(8,128)(2,1)} %shard_map.139) | copy-start | bytes 1179652
  210.9 23.7 %copy-start.6 = (bf16[8,2,256,256]{3,2,1,0:T(8,128)(2,1)S(1)}, bf16[8,2,256,256]{3,2,1,0:T(8,128)(2,1)}, u32[]{:S(2)}) copy-start(bf16[8,2,256,256]{3,2,1,0:T(8,128)(2,1)} %shard_map.141) | copy-start | bytes 6291460
  238.9 1.5 copy-start.9
  240.4 26.1 %copy-start.1 = (bf16[1280,480]{0,1:T(8,128)(2,1)S(1)}, bf16[1280,480]{0,1:T(8,128)(2,1)}, u32[]{:S(2)}) copy-start(bf16[1280,480]{0,1:T(8,128)(2,1)} %param.16) | copy-start | bytes 3686404

commit v2 on v1

--- a/solution.py
+++ b/solution.py
@@ -196,55 +196,6 @@
     return pltpu.CompilerParams(
         collective_id=collective, has_side_effects=True, vmem_limit_bytes=vmem_limit
     )
-
-
-def ring_gather_kernel(count, block, out, send, recv, own):
-    ring = Ring(count)
-    gather = RingGather(ring, block, lambda i, piece: out.at[i, piece], send, recv, block.shape[0])
-    greet([ring.left, ring.right])
-    gather.start()
-    keep = pltpu.make_async_copy(block, out.at[ring.index(0)], own)
-    keep.start()
-    for step in range(gather.steps):
-        gather.advance(step)
-    keep.wait()
-    gather.finish()
-
-
-def ring_gather(block, count, collective):
-    pieces = block.shape[0]
-    return pl.pallas_call(
-        functools.partial(ring_gather_kernel, count),
-        in_specs=[VMEM],
-        out_specs=ANY,
-        out_shape=jax.ShapeDtypeStruct((count,) + block.shape, block.dtype),
-        scratch_shapes=ring_sems(count, pieces) + [pltpu.SemaphoreType.DMA],
-        compiler_params=comm_params(collective),
-    )(block)
-
-
-def frame_gather_kernel(count, block, out, send, recv, own):
-    gather = FrameGather(count, block, out, send, recv, block.shape[0])
-    greet(gather.partners())
-    gather.start()
-    keep = pltpu.make_async_copy(block, out.at[gather.me], own)
-    keep.start()
-    for piece in range(gather.pieces):
-        gather.relay(piece)
-    keep.wait()
-    gather.finish()
-
-
-def frame_gather(block, count, collective):
-    pieces = block.shape[0]
-    return pl.pallas_call(
-        functools.partial(frame_gather_kernel, count),
-        in_specs=[VMEM],
-        out_specs=ANY,
-        out_shape=jax.ShapeDtypeStruct((count,) + block.shape, block.dtype),
-        scratch_shapes=frame_sems(count, pieces) + [pltpu.SemaphoreType.DMA],
-        compiler_params=comm_params(collective),
-    )(block)
 
 
 def front_kernel(seq_count, frame_count, pair, weight, pair_out, weight_out, *sems):
@@ -365,12 +316,188 @@
     )(own_ids[None, :], all_ids[:, None], queries, pairs)
 
 
+def mid_kernel(count, block, out_weight, patches, gain, up, hidden, held, up_held, total, spread, load, send, recv, own):
+    load_up = pltpu.make_async_copy(up, up_held, load)
+    load_up.start()
+    ring = Ring(count)
+    pieces, tall, rows = block.shape
+    share = pieces * tall
+    gather = RingGather(ring, block, lambda i, piece: held.at[i, piece], send, recv, pieces)
+    greet([ring.left, ring.right])
+    gather.start()
+    keep = pltpu.make_async_copy(block, held.at[ring.index(0)], own)
+    keep.start()
+
+    def fold(offsets, first):
+        owners = [ring.index(offset) for offset in offsets]
+        left = jnp.concatenate([held[i].reshape(share, rows) for i in owners], axis=0)
+        right = jnp.concatenate([out_weight[i] for i in owners], axis=0)
+        product = lax.dot_general(
+            left, right, (((0,), (0,)), ((), ())), preferred_element_type=jnp.float32
+        )
+        if first:
+            total[...] = patches[...].astype(jnp.float32) + product
+        else:
+            total[...] += product
+
+    half = max(gather.steps // 2, 1)
+    keep.wait()
+    for step in range(gather.steps):
+        gather.advance(step)
+        if step == half - 1:
+            fold(range(-half, half + 1), True)
+    if gather.steps > half:
+        rest = list(range(half + 1, gather.steps)) + list(range(-gather.steps, -half))
+        fold(rest, False)
+    width = total.shape[1]
+    values = total[...]
+    factor = lax.rsqrt(jnp.mean(values * values, axis=1, keepdims=True) + epsilon)
+    values = values * factor * gain[...]
+    lanes = spread.shape[2]
+    for c in range(width // lanes):
+        spread[c] = values[:, c * lanes : (c + 1) * lanes]
+    load_up.wait()
+    result = sum(
+        jnp.dot(
+            jnp.concatenate(
+                [spread[c, pl.ds(r, rows // 4, stride=4), :] for c in range(width // lanes)], axis=1
+            ).astype(jnp.bfloat16),
+            up_held[r * width : (r + 1) * width, :],
+            preferred_element_type=jnp.float32,
+        )
+        for r in range(4)
+    )
+    hidden[...] = (0.5 * result * (1.0 + lax.erf(result * 0.5**0.5))).astype(hidden.dtype)
+    gather.finish()
+
+
+def mid(block, out_weight, patches, gain, up, count, collective):
+    pieces, tall, rows = block.shape
+    width = patches.shape[1]
+    return pl.pallas_call(
+        functools.partial(mid_kernel, count),
+        in_specs=[VMEM, VMEM, VMEM, VMEM, ANY],
+        out_specs=VMEM,
+        out_shape=jax.ShapeDtypeStruct((rows // 4, up.shape[1]), jnp.bfloat16),
+        scratch_shapes=[
+            pltpu.VMEM((count,) + block.shape, block.dtype),
+            pltpu.VMEM(up.shape, up.dtype),
+            pltpu.VMEM((rows, width), jnp.float32),
+            pltpu.VMEM((width // 128, rows, 128), jnp.float32),
+            pltpu.SemaphoreType.DMA,
+        ]
+        + ring_sems(count, pieces)
+        + [pltpu.SemaphoreType.DMA],
+        compiler_params=comm_params(collective),
+    )(block, out_weight.reshape(count, pieces * tall, width), patches, gain[None, :], up)
+
+
+def finish_kernel(seq_count, frame_count, tokens, text, qw, kw, cosine, sine_part, text_out, out, *scratch):
+    held, q_held, k_held, mine, load, fsend, frecv, tsend, trecv, vsend, vrecv, own = scratch
+    parts, share, span = tokens.shape
+    loads = []
+    for part in range(parts):
+        slab = pl.ds(part * span, span)
+        loads.append(pltpu.make_async_copy(qw.at[slab], q_held.at[slab], load.at[0, part]))
+        loads.append(pltpu.make_async_copy(kw.at[slab], k_held.at[slab], load.at[1, part]))
+    for copy in loads:
+        copy.start()
+    ring = Ring(seq_count)
+    here = ring.index(0)
+    frames = FrameGather(frame_count, tokens, held, fsend, frecv, parts)
+    texts = RingGather(ring, text, lambda i, piece: text_out.at[i, piece], tsend, trecv, text.shape[0])
+    visions = RingGather(ring, mine, lambda i, piece: out.at[i, piece], vsend, vrecv, mine.shape[0])
+    greet([ring.left, ring.right] + frames.partners())
+    frames.start()
+    texts.start()
+    keep = [
+        pltpu.make_async_copy(tokens, held.at[frames.me], own.at[0]),
+        pltpu.make_async_copy(text, text_out.at[here], own.at[1]),
+    ]
+    for copy in keep:
+        copy.start()
+    early = texts.steps // 2
+    for part in range(parts):
+        frames.relay(part)
+        if part % 2 and part // 2 < early:
+            texts.advance(part // 2)
+    for copy in keep:
+        copy.wait()
+    frames.finish()
+    for copy in loads:
+        copy.wait()
+    q_total, k_total = None, None
+    for part in range(parts):
+        rows = jnp.concatenate([held[f, part] for f in range(frame_count)], axis=0)
+        slab = slice(part * span, (part + 1) * span)
+        q_part = jnp.dot(rows, q_held[slab], preferred_element_type=jnp.float32)
+        k_part = jnp.dot(rows, k_held[slab], preferred_element_type=jnp.float32)
+        q_total = q_part if part == 0 else q_total + q_part
+        k_total = k_part if part == 0 else k_total + k_part
+    turn, slide = cosine[...], sine_part[...]
+
+    def turned(values):
+        return values * turn + pltpu.roll(values, HDIM // 2, 1) * slide
+
+    queries = q_total.shape[1]
+    columns = [turned(q_total[:, c : c + HDIM]) for c in range(0, queries, HDIM)]
+    columns += [turned(k_total[:, :HDIM]), k_total[:, HDIM:]]
+    pieces, tall = mine.shape[:2]
+    for i, values in enumerate(columns):
+        for piece in range(pieces):
+            mine[piece, :, i * HDIM : (i + 1) * HDIM] = values[
+                piece * tall : (piece + 1) * tall
+            ].astype(mine.dtype)
+    visions.start()
+    last = pltpu.make_async_copy(mine, out.at[here], own.at[0])
+    last.start()
+    done = min(early, parts // 2)
+    for step in range(max(texts.steps - done, visions.steps)):
+        if done + step < texts.steps:
+            texts.advance(done + step)
+        if step < visions.steps:
+            visions.advance(step)
+    last.wait()
+    texts.finish()
+    visions.finish()
+
+
+def finish(tokens, text, positions, query_weight, keyvalue_weight, seq_count, frame_count, collective):
+    parts, share, span = tokens.shape
+    rows = frame_count * share
+    width = query_weight.shape[1] + keyvalue_weight.shape[1]
+    text = text.reshape(2, -1, text.shape[1])
+    mine = (2, rows // 2, width)
+    cosine, sine_part = turns(positions)
+    text_out, out = pl.pallas_call(
+        functools.partial(finish_kernel, seq_count, frame_count),
+        in_specs=[VMEM, VMEM, ANY, ANY, VMEM, VMEM],
+        out_specs=[ANY, ANY],
+        out_shape=[
+            jax.ShapeDtypeStruct((seq_count,) + text.shape, text.dtype),
+            jax.ShapeDtypeStruct((seq_count,) + mine, text.dtype),
+        ],
+        scratch_shapes=[
+            pltpu.VMEM((frame_count,) + tokens.shape, tokens.dtype),
+            pltpu.VMEM(query_weight.shape, query_weight.dtype),
+            pltpu.VMEM(keyvalue_weight.shape, keyvalue_weight.dtype),
+            pltpu.VMEM(mine, text.dtype),
+            pltpu.SemaphoreType.DMA((2, parts)),
+        ]
+        + frame_sems(frame_count, parts)
+        + ring_sems(seq_count, 2) * 2
+        + [pltpu.SemaphoreType.DMA((2,))],
+        compiler_params=comm_params(collective),
+    )(tokens, text, query_weight, keyvalue_weight, cosine, sine_part)
+    return text_out.reshape(-1, text.shape[-1]), out.reshape(-1, width)
+
+
 def scatter_kernel(count, hidden, weight, gain, out, held, part, stage, land, load, send, recv):
     ring = Ring(count)
     width = weight.shape[1]
     pieces = held.shape[0]
     span = width // pieces
-    share = out.shape[0]
+    share = out.shape[1]
     order = [piece for pair in zip(range(pieces // 2), range(pieces // 2, pieces)) for piece in pair]
     loads = {
         piece: pltpu.make_async_copy(
@@ -423,7 +550,7 @@
     factor = lax.rsqrt(squares / width + epsilon)
     for piece in order:
         columns = slice(piece * span, (piece + 1) * span)
-        out[:, columns] = (part[piece, here] * factor * gain[:, columns]).astype(out.dtype)
+        out[piece] = (part[piece, here] * factor * gain[:, columns]).astype(out.dtype)
 
     def drain(step, carry):
         for piece in order:
@@ -443,7 +570,7 @@
         functools.partial(scatter_kernel, count),
         in_specs=[VMEM, ANY, VMEM],
         out_specs=VMEM,
-        out_shape=jax.ShapeDtypeStruct((share, width), jnp.bfloat16),
+        out_shape=jax.ShapeDtypeStruct((pieces, share, span), jnp.bfloat16),
         scratch_shapes=[
             pltpu.VMEM((pieces, depth, span), jnp.bfloat16),
             pltpu.VMEM((pieces, count, share, span), jnp.float32),
@@ -643,17 +770,7 @@
 
     vit_context = vit_attention(own_video, patch_video, vit_query, pair_all)
     pieces = vit_context.reshape(2, -1, patch_rows)
-    context_all = ring_gather(pieces, seq_count, 2).reshape(-1, patch_rows)
-    head_total = lax.dot_general(
-        context_all, out_full, (((0,), (0,)), ((), ())), preferred_element_type=jnp.float32
-    )
-    vit_output = patches.astype(jnp.float32) + head_total
-    merged_input = (
-        rms_scale(vit_output, merge_gain).astype(jnp.bfloat16).reshape(patch_rows // 4, -1)
-    )
-    merge_hidden = jax.nn.gelu(
-        jnp.dot(merged_input, merge_up, preferred_element_type=jnp.float32), approximate=False
-    ).astype(jnp.bfloat16)
+    merge_hidden = mid(pieces, out_full, patches, merge_gain, merge_up, seq_count, 2)
     vision_normed = scatter(merge_hidden, merge_down, llm_gain, seq_count, 3)
 
     part_rows = text_embed.shape[0]
@@ -664,23 +781,13 @@
     text_query, text_pair = project(
         text_blocks, where, first + jnp.arange(seq_block, dtype=jnp.int32), query_weight, keyvalue_weight
     )
-    text_pair_all = ring_gather(text_pair.reshape(2, seq_block // 2, -1), seq_count, 4)
-    text_pair_all = text_pair_all.reshape(seq_count * seq_block, -1)
-
-    share = vision_normed.shape[0]
-    vision_normed, text_pair_all = barrier((vision_normed, text_pair_all))
-    halves = vision_normed.reshape(share, 2, -1).transpose(1, 0, 2)
-    vision_tokens = frame_gather(halves, frame_count, 5).transpose(0, 2, 1, 3)
-    vision_tokens = vision_tokens.reshape(frame_count * share, -1)
+    share = vision_normed.shape[1]
     token_pos = vision_pos.reshape(frame_count, seq_count, share).transpose(1, 0, 2)
     here = lax.dynamic_index_in_dim(token_pos, seq_index, 0, keepdims=False).reshape(-1)
-    vision_query, vision_pair = project(
-        [vision_tokens], jnp.zeros((1,), jnp.int32), here, query_weight, keyvalue_weight
+    text_pair_all, gathered = finish(
+        vision_normed, text_pair, here, query_weight, keyvalue_weight, seq_count, frame_count, 4
     )
-    vision_both = jnp.concatenate([vision_query, vision_pair], axis=1)
-    gathered = ring_gather(vision_both.reshape(2, frame_count * share // 2, -1), seq_count, 6)
-    gathered = gathered.reshape(seq_count * frame_count * share, -1)
-    width = vision_query.shape[1]
+    width = query_weight.shape[1]
     token_pos = token_pos.reshape(-1)
     llm_query = place(token_pos, first, text_query, gathered[:, :width])
     llm_pair = place(token_pos, 0, text_pair_all, gathered[:, width:])

time: 267 us -> 265 us (level)
  waiting for transfers between devices: 0.01 us -> 47.3 us
  Pallas kernels: 212 us -> 189 us
  matrix products: 21.4 us -> 7.48 us
  local copies, waits for them, and re-layouts: 19.1 us -> 9.26 us
  other arithmetic: 12.9 us -> 9.6 us
    ppermute x3, waiting for transfers between devices: 0.01 us -> 47.3 us  [local(): lax.ppermute(block, 'frame', swap)]
    pallas_call x4 -> x2, Pallas kernels: 84.3 us -> 71 us  [the longest x1 39.9 us: finish(): pl.pallas_call(functools.partial(finish_kernel, seq_count, frame_count),...]
    dot_general x2 -> x0, matrix products: 12.4 us -> none  [the longest x1 6.85 us: local(): jnp.dot(merged_input, merge_up, preferred_element_type=jnp.float32)]
    pallas_call x2 -> x1, Pallas kernels: 23.7 us -> 14.4 us  [project(): pl.pallas_call(functools.partial(project_kernel, len(blocks)), grid=(dept...]
    reshape x2 -> x0, local copies, waits for them, and re-layouts: 4.86 us -> none  [the longest x1 4.08 us: local(): rms_scale(vit_output, merge_gain).astype(jnp.bfloat16)]
    unnamed x31 -> x24, local copies, waits for them, and re-layouts: 4.34 us -> 0.09 us
    transpose x1 -> x0, local copies, waits for them, and re-layouts: 3.04 us -> none  [local(): vision_tokens = frame_gather(halves, frame_count, 5).transpose(0, 2, 1, 3)]
  transfers between devices with their start and end apart: 3 -> 3, of which waited for: 0 -> 1; matrix products, arithmetic and copies ran while one was open for 10% -> 5% of each run, Pallas kernels for 28% -> 31%
where the time goes in v2:
time: 265 us
  Pallas kernels  189 us (71%)
  waiting for transfers between devices  47.3 us (18%)
  other arithmetic  9.6 us (4%)
  local copies, waits for them, and re-layouts  9.26 us (3%)
  matrix products  7.48 us (3%)
    ppermute x3, waiting for transfers between devices, local(): lax.ppermute(block, 'frame', swap)  47.3 us
    pallas_call x1, Pallas kernels, finish(): pl.pallas_call(functools.partial(finish_kernel, seq_count, frame_count),...  39.9 us
    pallas_call x1, Pallas kernels, scatter(): pl.pallas_call(functools.partial(scatter_kernel, count), in_specs=[VMEM,...  37.9 us
    pallas_call x1, Pallas kernels, mid(): pl.pallas_call(functools.partial(mid_kernel, count), in_specs=[VMEM, VMEM...  31 us
    pallas_call x1, Pallas kernels, front(): pl.pallas_call(functools.partial(front_kernel, seq_count, frame_count), i...  28.4 us
    pallas_call x1, Pallas kernels, causal_attention(): pl.pallas_call(causal_kernel, grid=(width // HDIM,), in_specs=[pl.BlockSp...  25.1 us
    pallas_call x1, Pallas kernels, project(): pl.pallas_call(functools.partial(project_kernel, len(blocks)), grid=(dept...  14.4 us
    pallas_call x1, Pallas kernels, vit_attention(): pl.pallas_call(vit_attention_kernel, grid=(rows // step,), in_specs=[pl.B...  12.6 us
  transfers between devices with their start and end apart: 3, of which 1 were waited for; matrix products, arithmetic and copies ran while one was open for 5% of the time, Pallas kernels for 31%

profile of v2, /device:TPU:28, one launch (start us, length us, event | category | flops | bytes accessed | tf_op | source)
XLA Modules:
  0.0 264.5 jit_solution(12545764588730130563)
XLA Ops:
  0.0 2.2 fusion.5
  2.3 0.5 fusion.8
  2.8 1.2 fusion.17
  4.0 0.8 slice.24.pair
  4.8 0.6 fusion.7.refs_0_
  5.5 28.4 %shard_map.136 = (bf16[4,2,160,768]{3,2,1,0:T(8,128)(2,1)}, bf16[8,2,2,40,1280]{4,3,2,1,0:T(8,128)(2,1)}) custom-call(bf16[2,160,768]{2,1,0:T(8,128)(2,1)} %slice.24.pair, bf16[2,2,40,1280]{3,2,1,0:T(8,128)(2,1)} %bitcast.19), custom_call_target="tpu_custom_call" | custom-call | tf_op jit(solution)/shard_map/pallas_call | solution.py:250
  33.9 0.7 collective-permute-start
  34.6 47.3 %collective-permute-done.refs_1_ = bf16[128,8192]{1,0:T(8,128)(2,1)} collective-permute-done((bf16[128,8192]{1,0:T(8,128)(2,1)S(1)}, bf16[128,8192]{1,0:T(8,128)(2,1)}, u32[]{:S(2)}, u32[]{:S(2)}) %collective-permute-start) | collective-permute-done | bytes 2097184 | tf_op jit(solution)/shard_map/ppermute | solution.py:767
  82.0 0.5 collective-permute-start.2
  82.5 0.7 slice.25
  83.2 0.9 broadcast_in_dim.28
  84.1 1.2 reshape.73
  85.3 2.5 broadcast_in_dim_reshape.6.ids_ref
  87.8 0.6 broadcast_in_dim.47.gain
  88.8 0.6 broadcast_in_dim.46.own_ref
  89.4 12.6 %shard_map.137 = bf16[160,768]{1,0:T(8,128)(2,1)} custom-call(s32[1,768]{1,0:T(1,128)} %broadcast_in_dim.46.own_ref, s32[3072,1]{1,0:T(8,128)} %broadcast_in_dim_reshape.6.ids_ref, bf16[160,768]{1,0:T(8,128)(2,1)} %bitcast.15, bf16[4,2,160,768]{3,2,1,0:T(8,128)(2,1)} %get-tuple-element.17.kv_ref), custom_call_target="tpu_custom_call" | custom-call | tf_op jit(solution)/shard_map/pallas_call | solution.py:304
  102.0 31.0 %shard_map.138.hidden = bf16[192,640]{1,0:T(8,128)(2,1)} custom-call(bf16[2,80,768]{2,1,0:T(8,128)(2,1)} %bitcast.16, bf16[8,160,1280]{2,1,0:T(8,128)(2,1)} %bitcast.14, bf16[768,1280]{1,0:T(8,128)(2,1)} %patches.1, f32[1,1280]{1,0:T(1,128)} %broadcast_in_dim.47.gain, bf16[5120,640]{1,0:T(8,128)(2,1)} %up.1), custom_call_target="tpu_custom_call" | custom-call | tf_op jit(solution)/shard_map/pallas_call | solution.py:377
  133.0 37.9 %shard_map.139.tokens = bf16[4,24,2048]{2,1,0:T(8,128)(2,1)} custom-call(bf16[192,640]{1,0:T(8,128)(2,1)} %shard_map.138.hidden, bf16[640,8192]{1,0:T(8,128)(2,1)} %weight.1, f32[1,8192]{1,0:T(1,128)} %bitcast.21), custom_call_target="tpu_custom_call" | custom-call | tf_op jit(solution)/shard_map/pallas_call | solution.py:569
  171.0 0.3 fusion.28
  171.2 0.8 pad_maximum_fusion.2
  172.0 1.0 fusion.27
  173.0 1.0 pad_maximum_fusion
  174.0 0.3 compare_reduce_fusion
  174.3 0.6 broadcast_xor_fusion.refs_4_
  174.9 1.4 fusion.1
  176.4 14.4 %shard_map.140 = (bf16[512,512]{1,0:T(8,128)(2,1)}, bf16[512,256]{1,0:T(8,128)(2,1)}) custom-call(bf16[128,8192]{1,0:T(8,128)(2,1)} %copy-done.1, bf16[128,8192]{1,0:T(8,128)(2,1)} %collective-permute-done.refs_1_, bf16[128,8192]{1,0:T(8,128)(2,1)} %collective-permute-done.2.refs_2_, bf16[128,8192]{1,0:T(8,128)(2,1)} %collective-permute-done.1.refs_3_, ...), custom_call_target="tpu_custom_call" | custom-call | tf_op jit(solution)/shard_map/pallas_call | solution.py:638
  190.8 39.9 %shard_map.141 = (bf16[8,2,256,256]{3,2,1,0:T(8,128)(2,1)}, bf16[8,2,48,768]{3,2,1,0:T(8,128)(2,1)}) custom-call(bf16[4,24,2048]{2,1,0:T(8,128)(2,1)} %shard_map.139.tokens, bf16[2,256,256]{2,1,0:T(8,128)(2,1)} %bitcast.20, bf16[8192,512]{1,0:T(8,128)(2,1)} %qw.1, bf16[8192,256]{1,0:T(8,128)(2,1)} %kw.1, f32[96,128]{1,0:T(8,128)} %get-tuple-element.35.cosine, ...), custom_call_target="tpu_custom_call" | custom-call | tf_op jit(solution)/shard_map/pallas_call | solution.py:472
  230.7 1.9 fusion.20
  232.6 4.3 %fusion.4 = bf16[4096,256]{1,0:T(8,128)(2,1)S(1)} fusion(bf16[4096,256]{1,0:T(8,128)(2,1)S(1)} %bitcast.23, s32[768]{0:T(1024)S(1)} %eq.29, pred[4096]{0:T(1024)(128)(4,1)S(1)} %fusion.1, bf16[768,768]{1,0:T(8,128)(2,1)} %bitcast.25), kind=kOutput, calls=%fused_computation.9 | convolution fusion | flops 1615855616 | bytes 4594688 | tf_op jit(solution)/shard_map/dot_general | solution.py:723
  237.0 1.5 fusion.30
  238.5 0.9 broadcast_select_fusion.q_ref
  239.4 25.1 %shard_map.142 = bf16[512,512]{1,0:T(8,128)(2,1)} custom-call(s32[1]{0:T(128)} %bitcast.block_ref, bf16[512,512]{1,0:T(8,128)(2,1)} %broadcast_select_fusion.q_ref, bf16[4096,128]{1,0:T(8,128)(2,1)} %get-tuple-element.26.k_ref, bf16[4096,128]{1,0:T(8,128)(2,1)} %get-tuple-element.25.v_ref), custom_call_target="tpu_custom_call" | custom-call | tf_op jit(solution)/shard_map/pallas_call | solution.py:705
  (38 shorter events, 0.5 us)
Async XLA Ops:
  0.0 2.7 %copy-start = (bf16[1280,480]{0,1:T(8,128)(2,1)S(1)}, bf16[1280,480]{0,1:T(8,128)(2,1)}, u32[]{:S(2)}) copy-start(bf16[1280,480]{0,1:T(8,128)(2,1)} %param.16) | copy-start | bytes 3686404
  0.0 2.3 copy-start.3
  0.0 2.7 %copy-start.10 = (f32[1280]{0:T(1024)S(1)}, f32[1280]{0:T(1024)}, u32[]{:S(2)}) copy-start(f32[1280]{0:T(1024)} %param.15) | copy-start | bytes 15364
  2.8 2.1 copy-start.2
  2.8 2.1 copy-start.5
  4.8 78.3 %copy-start.7 = (s32[768]{0:T(1024)S(1)}, s32[768]{0:T(1024)}, u32[]{:S(2)}) copy-start(s32[768]{0:T(1024)} %param.18) | copy-start | bytes 9220
  5.4 83.0 %copy-start.1 = (bf16[128,8192]{1,0:T(8,128)(2,1)}, bf16[128,8192]{1,0:T(8,128)(2,1)S(1)}, u32[]{:S(2)}) copy-start(bf16[128,8192]{1,0:T(8,128)(2,1)S(1)} %fusion.7.refs_0_) | copy-start | bytes 6291460
  5.4 82.4 %copy-start.6 = (f32[1280]{0:T(1024)S(1)}, f32[1280]{0:T(1024)}, u32[]{:S(2)}) copy-start(f32[1280]{0:T(1024)} %param.19) | copy-start | bytes 15364
  5.5 83.0 %copy-start.8 = (s32[768]{0:T(1024)S(1)}, s32[768]{0:T(1024)}, u32[]{:S(2)}) copy-start(s32[768]{0:T(1024)} %param.22) | copy-start | bytes 9220
  33.9 48.1 %collective-permute-start = (bf16[128,8192]{1,0:T(8,128)(2,1)S(1)}, bf16[128,8192]{1,0:T(8,128)(2,1)}, u32[]{:S(2)}, u32[]{:S(2)}) collective-permute-start(bf16[128,8192]{1,0:T(8,128)(2,1)S(1)} %fusion.7.refs_0_), channel_id=1, source_target_pairs={{0,2},{1,3},{2,0},{3,1},{4,6},{5,7},{6,4},{7,5},{8,10},{9,11},{10,... | collective-permute-start | bytes 6291464 | tf_op jit(solution)/shard_map/ppermute | solution.py:767
  82.0 94.4 %collective-permute-start.1 = (bf16[128,8192]{1,0:T(8,128)(2,1)}, bf16[128,8192]{1,0:T(8,128)(2,1)}, u32[]{:S(2)}, u32[]{:S(2)}) collective-permute-start(bf16[128,8192]{1,0:T(8,128)(2,1)} %collective-permute-done.refs_1_), channel_id=1, source_target_pairs={{0,1},{1,0},{2,3},{3,2},{4,5},{5,4},{6,7},{7,6},{8,9},{9,8},{10,11... | collective-permute-start | bytes 6291464 | tf_op jit(solution)/shard_map/ppermute | solution.py:767
  82.0 94.4 %collective-permute-start.2 = (bf16[128,8192]{1,0:T(8,128)(2,1)S(1)}, bf16[128,8192]{1,0:T(8,128)(2,1)}, u32[]{:S(2)}, u32[]{:S(2)}) collective-permute-start(bf16[128,8192]{1,0:T(8,128)(2,1)S(1)} %fusion.7.refs_0_), channel_id=1, source_target_pairs={{0,1},{1,0},{2,3},{3,2},{4,5},{5,4},{6,7},{7,6},{8,9},{9,8},{10,11... | collective-permute-start | bytes 6291464 | tf_op jit(solution)/shard_map/ppermute | solution.py:767
  170.9 3.4 %copy-start.11 = (s32[4]{0:T(128)S(1)}, s32[4]{0:T(128)}, u32[]{:S(2)}) copy-start(s32[4]{0:T(128)} %constant.44.clone) | copy-start | bytes 52
  230.7 1.9 copy-start.9
  237.0 1.5 copy-start.4

commit v3 on v2

--- a/solution.py
+++ b/solution.py
@@ -180,10 +180,14 @@
             self.across(d, piece).wait_recv()
             self.inside(d, piece).start()
 
+    def settle(self, piece):
+        for d in range(self.chips):
+            self.inside(d, piece).wait_recv()
+
     def finish(self):
         for piece in range(self.pieces):
             for d in range(self.chips):
-                self.inside(d, piece).wait()
+                self.inside(d, piece).wait_send()
                 if d:
                     self.across(d, piece).wait_send()
 
@@ -198,135 +202,174 @@
     )
 
 
-def front_kernel(seq_count, frame_count, pair, weight, pair_out, weight_out, *sems):
-    fsend, frecv, rsend, rrecv, tsend, trecv, own = sems
+def encode_kernel(seq_count, frame_count, patches, gain, weight, low, high, out_weight, context, weight_out, *scratch):
+    mine, query, held, flat, peak, mass, blend, fsend, frecv, rsend, rrecv, tsend, trecv, own = scratch
     ring = Ring(seq_count)
-    frames = FrameGather(frame_count, pair, pair_out, fsend, frecv, pair.shape[0])
+    heads, tall, rows = mine.shape
+    frames = FrameGather(frame_count, mine, held, fsend, frecv, heads)
     core, twin = frames.core, frames.twin
-    quarter = weight.shape[1]
-    half = weight.at[core]
+    pieces = out_weight.shape[1]
     gather = RingGather(
-        ring, half, lambda i, piece: weight_out.at[i, core, piece], rsend, rrecv, quarter
+        ring, out_weight.at[core], lambda i, piece: weight_out.at[i, core, piece], rsend, rrecv, pieces
     )
     greet([ring.left, ring.right] + frames.partners())
-    frames.start()
     gather.start()
-    here = ring.index(0)
-    keep = [
-        pltpu.make_async_copy(pair, pair_out.at[frames.me], own.at[0]),
-        pltpu.make_async_copy(weight, weight_out.at[here], own.at[1]),
-    ]
-    for copy in keep:
-        copy.start()
+    keep = pltpu.make_async_copy(out_weight, weight_out.at[ring.index(0)], own.at[0])
+    keep.start()
     handed = []
 
     def landed(index, piece, way, step):
-        copy = remote(
-            weight_out.at[index, core, piece],
-            weight_out.at[index, core, piece],
-            tsend.at[way, step, piece],
-            trecv.at[way, step, piece],
-            twin,
-        )
+        spot = weight_out.at[index, core, piece]
+        copy = remote(spot, spot, tsend.at[way, step, piece], trecv.at[way, step, piece], twin)
         copy.start()
         handed.append(copy)
 
-    for step in range(max(gather.steps, frames.pieces)):
-        if step < frames.pieces:
-            frames.relay(step)
-        if step < gather.steps:
-            gather.advance(step, landed)
-    for copy in keep:
-        copy.wait()
+    widened = patches[...].astype(jnp.float32)
+    factor = lax.rsqrt(jnp.mean(widened * widened, axis=-1, keepdims=True) + epsilon)
+    normed = (widened * factor * gain[...]).astype(jnp.bfloat16)
+    projected = lax.dot_general(
+        weight[...], normed, (((0,), (1,)), ((), ())), preferred_element_type=jnp.float32
+    ).astype(jnp.bfloat16)
+    for head in range(heads):
+        base = head * 3 * VIT_HDIM
+        query[head] = projected[base : base + VIT_HDIM]
+        mine[head] = projected[base + VIT_HDIM : base + 3 * VIT_HDIM]
+    frames.start()
+    local = pltpu.make_async_copy(mine, held.at[frames.me], own.at[1])
+    local.start()
+    local.wait()
+    near = [frames.chip * 2, frames.chip * 2 + 1]
+    far = [
+        lax.rem(frames.chip + d, frames.chips) * 2 + c for d in range(1, frames.chips) for c in range(2)
+    ]
+    tile = math.gcd(rows, 256)
+    scale = VIT_HDIM ** (-0.5) * math.log2(math.e)
+
+    def flatten(slots, head):
+        for slot in slots:
+            flat[slot, head] = held[slot, head, :VIT_HDIM, :].T
+
+    def attend(slots, head, start):
+        columns = slice(start, start + tile)
+        queries = query[head, :, columns]
+        first, past = low[:, columns], high[:, columns]
+        scores = []
+        for slot in slots:
+            part = jnp.dot(flat[slot, head], queries, preferred_element_type=jnp.float32)
+            spot = slot * rows + lax.broadcasted_iota(jnp.int32, part.shape, 0)
+            scores.append(jnp.where((spot >= first) & (spot < past), part, lowest))
+        scores = jnp.concatenate(scores, axis=0)
+        highest = jnp.max(scores, axis=0, keepdims=True)
+        weights = jnp.exp2((scores - highest) * scale)
+        total = jnp.sum(weights, axis=0, keepdims=True)
+        weights = weights.astype(jnp.bfloat16)
+        mixed = sum(
+            jnp.dot(
+                held[slot, head, VIT_HDIM:, :],
+                weights[i * rows : (i + 1) * rows],
+                preferred_element_type=jnp.float32,
+            )
+            for i, slot in enumerate(slots)
+        )
+        return highest, total, mixed
+
+    def first_pass(head):
+        flatten(near, head)
+        for start in range(0, rows, tile):
+            columns = slice(start, start + tile)
+            highest, total, mixed = attend(near, head, start)
+            peak[head : head + 1, columns] = highest
+            mass[head : head + 1, columns] = total
+            blend[head, :, columns] = mixed
+
+    def second_pass(head):
+        if far:
+            flatten(far, head)
+        for start in range(0, rows, tile):
+            columns = slice(start, start + tile)
+            total, mixed = mass[head : head + 1, columns], blend[head, :, columns]
+            if far:
+                before = peak[head : head + 1, columns]
+                highest, more, extra = attend(far, head, start)
+                joint = jnp.maximum(before, highest)
+                old, new = jnp.exp2((before - joint) * scale), jnp.exp2((highest - joint) * scale)
+                total = total * old + more * new
+                mixed = mixed * old + extra * new
+            context[head, :, columns] = (mixed / total).astype(context.dtype)
+
+    gather.advance(0, landed)
+    for head in range(heads):
+        frames.inside(0, head).wait_recv()
+        first_pass(head)
+        frames.relay(head)
+        if head + 1 < gather.steps:
+            gather.advance(head + 1, landed)
+    for head in range(heads):
+        for d in range(1, frames.chips):
+            frames.inside(d, head).wait_recv()
+        second_pass(head)
+        if heads + head + 1 < gather.steps:
+            gather.advance(heads + head + 1, landed)
+    for step in range(2 * heads + 1, gather.steps):
+        gather.advance(step, landed)
+    keep.wait()
     frames.finish()
     gather.finish()
     for copy in handed:
         copy.wait()
 
 
-def front(pair, weight, seq_count, frame_count, collective):
-    quarter = 2
-    weight = weight.reshape(2, quarter, -1, weight.shape[1])
-    pair_out, weight_out = pl.pallas_call(
-        functools.partial(front_kernel, seq_count, frame_count),
-        in_specs=[VMEM, VMEM],
-        out_specs=[ANY, ANY],
+def encode(patches, gain, weight, low, high, out_weight, seq_count, frame_count, collective):
+    rows = patches.shape[0]
+    heads = weight.shape[1] // (3 * VIT_HDIM)
+    half = out_weight.shape[0] // 2
+    tall = math.gcd(half, 16)
+    pieces = half // tall
+    out_weight = out_weight.reshape(2, pieces, tall, -1)
+    context, weight_out = pl.pallas_call(
+        functools.partial(encode_kernel, seq_count, frame_count),
+        in_specs=[VMEM] * 6,
+        out_specs=[VMEM, ANY],
         out_shape=[
-            jax.ShapeDtypeStruct((frame_count,) + pair.shape, pair.dtype),
-            jax.ShapeDtypeStruct((seq_count,) + weight.shape, weight.dtype),
+            jax.ShapeDtypeStruct((heads, VIT_HDIM, rows), jnp.bfloat16),
+            jax.ShapeDtypeStruct((seq_count,) + out_weight.shape, out_weight.dtype),
         ],
-        scratch_shapes=frame_sems(frame_count, pair.shape[0])
-        + ring_sems(seq_count, quarter) * 2
+        scratch_shapes=[
+            pltpu.VMEM((heads, 2 * VIT_HDIM, rows), jnp.bfloat16),
+            pltpu.VMEM((heads, VIT_HDIM, rows), jnp.bfloat16),
+            pltpu.VMEM((frame_count, heads, 2 * VIT_HDIM, rows), jnp.bfloat16),
+            pltpu.VMEM((frame_count, heads, rows, VIT_HDIM), jnp.bfloat16),
+            pltpu.VMEM((heads, rows), jnp.float32),
+            pltpu.VMEM((heads, rows), jnp.float32),
+            pltpu.VMEM((heads, VIT_HDIM, rows), jnp.float32),
+        ]
+        + frame_sems(frame_count, heads)
+        + ring_sems(seq_count, pieces) * 2
         + [pltpu.SemaphoreType.DMA((2,))],
         compiler_params=comm_params(collective),
-    )(pair, weight)
-    return pair_out, weight_out.reshape(-1, weight.shape[-1])
-
-
-def vit_attention_kernel(own_ref, ids_ref, q_ref, kv_ref, out_ref):
-    frames, heads, _, rows = kv_ref.shape
-    allowed = ids_ref[...] == own_ref[...]
-    for head in range(heads):
-        spread = slice(head * VIT_HDIM, (head + 1) * VIT_HDIM)
-        queries = q_ref[spread, :]
-        scores = jnp.concatenate(
-            [
-                lax.dot_general(
-                    kv_ref[f, head, :VIT_HDIM, :],
-                    queries,
-                    (((0,), (0,)), ((), ())),
-                    preferred_element_type=jnp.float32,
-                )
-                for f in range(frames)
-            ],
-            axis=0,
-        )
-        scores = jnp.where(allowed, scores, lowest)
-        highest = jnp.max(scores, axis=0, keepdims=True)
-        weights = jnp.exp((scores - highest) * VIT_HDIM ** (-0.5))
-        row_sum = jnp.sum(weights, axis=0, keepdims=True)
-        weights = weights.astype(jnp.bfloat16)
-        mixed = sum(
-            jnp.dot(
-                kv_ref[f, head, VIT_HDIM:, :],
-                weights[f * rows : (f + 1) * rows],
-                preferred_element_type=jnp.float32,
-            )
-            for f in range(frames)
-        )
-        out_ref[spread, :] = (mixed / row_sum).astype(out_ref.dtype)
-
-
-def vit_attention(own_ids, all_ids, queries, pairs):
-    width, rows = queries.shape
-    keys = all_ids.shape[0]
-    step = math.gcd(rows, 256)
-    return pl.pallas_call(
-        vit_attention_kernel,
-        grid=(rows // step,),
-        in_specs=[
-            pl.BlockSpec((1, step), lambda i: (0, i)),
-            pl.BlockSpec((keys, 1), lambda i: (0, 0)),
-            pl.BlockSpec((width, step), lambda i: (0, i)),
-            pl.BlockSpec(pairs.shape, lambda i: (0, 0, 0, 0)),
-        ],
-        out_specs=pl.BlockSpec((width, step), lambda i: (0, i)),
-        out_shape=jax.ShapeDtypeStruct((width, rows), jnp.bfloat16),
-        compiler_params=pltpu.CompilerParams(vmem_limit_bytes=vmem_limit),
-    )(own_ids[None, :], all_ids[:, None], queries, pairs)
-
-
-def mid_kernel(count, block, out_weight, patches, gain, up, hidden, held, up_held, total, spread, load, send, recv, own):
+    )(patches, gain[None, :], weight, low[None, :], high[None, :], out_weight)
+    return context, weight_out.reshape(seq_count, 2 * half, -1)
+
+
+def mid_kernel(
+    count, frame_count, block, out_weight, patches, gain, text, up, hidden, text_out,
+    held, up_held, total, spread, load, send, recv, fsend, frecv, own
+):
     load_up = pltpu.make_async_copy(up, up_held, load)
     load_up.start()
     ring = Ring(count)
     pieces, tall, rows = block.shape
     share = pieces * tall
     gather = RingGather(ring, block, lambda i, piece: held.at[i, piece], send, recv, pieces)
-    greet([ring.left, ring.right])
+    parts = text_out.shape[1]
+    frames = FrameGather(frame_count, text, text_out, fsend, frecv, parts)
+    greet([ring.left, ring.right] + frames.partners())
     gather.start()
-    keep = pltpu.make_async_copy(block, held.at[ring.index(0)], own)
+    frames.start()
+    keep = pltpu.make_async_copy(block, held.at[ring.index(0)], own.at[0])
     keep.start()
+    aside = pltpu.make_async_copy(text.at[pl.ds(0, parts)], text_out.at[frames.me], own.at[1])
+    aside.start()
 
     def fold(offsets, first):
         owners = [ring.index(offset) for offset in offsets]
@@ -344,6 +387,8 @@
     keep.wait()
     for step in range(gather.steps):
         gather.advance(step)
+        if step < parts:
+            frames.relay(step)
         if step == half - 1:
             fold(range(-half, half + 1), True)
     if gather.steps > half:
@@ -368,17 +413,27 @@
         for r in range(4)
     )
     hidden[...] = (0.5 * result * (1.0 + lax.erf(result * 0.5**0.5))).astype(hidden.dtype)
+    aside.wait()
+    for part in range(parts):
+        if part >= gather.steps:
+            frames.relay(part)
+        frames.settle(part)
+    frames.finish()
     gather.finish()
 
 
-def mid(block, out_weight, patches, gain, up, count, collective):
+def mid(block, out_weight, patches, gain, text, up, count, frame_count, collective):
     pieces, tall, rows = block.shape
     width = patches.shape[1]
+    parts = text.shape[0] // 2
     return pl.pallas_call(
-        functools.partial(mid_kernel, count),
-        in_specs=[VMEM, VMEM, VMEM, VMEM, ANY],
-        out_specs=VMEM,
-        out_shape=jax.ShapeDtypeStruct((rows // 4, up.shape[1]), jnp.bfloat16),
+        functools.partial(mid_kernel, count, frame_count),
+        in_specs=[VMEM] * 5 + [ANY],
+        out_specs=[VMEM, ANY],
+        out_shape=[
+            jax.ShapeDtypeStruct((rows // 4, up.shape[1]), jnp.bfloat16),
+            jax.ShapeDtypeStruct((frame_count, parts) + text.shape[1:], text.dtype),
+        ],
         scratch_shapes=[
             pltpu.VMEM((count,) + block.shape, block.dtype),
             pltpu.VMEM(up.shape, up.dtype),
@@ -387,9 +442,10 @@
             pltpu.SemaphoreType.DMA,
         ]
         + ring_sems(count, pieces)
-        + [pltpu.SemaphoreType.DMA],
+        + frame_sems(frame_count, parts)
+        + [pltpu.SemaphoreType.DMA((2,))],
         compiler_params=comm_params(collective),
-    )(block, out_weight.reshape(count, pieces * tall, width), patches, gain[None, :], up)
+    )(block, out_weight, patches, gain[None, :], text, up)
 
 
 def finish_kernel(seq_count, frame_count, tokens, text, qw, kw, cosine, sine_part, text_out, out, *scratch):
@@ -423,6 +479,8 @@
             texts.advance(part // 2)
     for copy in keep:
         copy.wait()
+    for part in range(parts):
+        frames.settle(part)
     frames.finish()
     for copy in loads:
         copy.wait()
@@ -492,7 +550,10 @@
     return text_out.reshape(-1, text.shape[-1]), out.reshape(-1, width)
 
 
-def scatter_kernel(count, hidden, weight, gain, out, held, part, stage, land, load, send, recv):
+def scatter_kernel(
+    count, frame_count, hidden, weight, gain, text, near, qw, kw, cosine, sine_part, out, q_out, pair_out, *scratch
+):
+    held, part, stage, land, q_held, k_held, early, late, sums, load, send, recv, fsend, frecv, own = scratch
     ring = Ring(count)
     width = weight.shape[1]
     pieces = held.shape[0]
@@ -507,7 +568,20 @@
     }
     for piece in order:
         loads[piece].start()
-    greet([ring.left, ring.right])
+    extra = [
+        pltpu.make_async_copy(near, early, own.at[0]),
+        pltpu.make_async_copy(qw, q_held, own.at[1]),
+        pltpu.make_async_copy(kw, k_held, own.at[2]),
+    ]
+    for copy in extra:
+        copy.start()
+    parts, tall, depth = early.shape[1:]
+    last = text.at[pl.ds(text.shape[0] - late.shape[1], late.shape[1])]
+    frames = FrameGather(frame_count, last, late, fsend, frecv, late.shape[1])
+    greet([ring.left, ring.right] + frames.partners())
+    frames.start()
+    aside = pltpu.make_async_copy(last, late.at[frames.me], own.at[3])
+    aside.start()
     forward = [piece < pieces // 2 for piece in range(pieces)]
 
     def hop(piece, step):
@@ -527,18 +601,78 @@
         first = ring.index(-1 if forward[piece] else 1)
         stage[piece, 0] = part[piece, first].astype(jnp.bfloat16)
         hop(piece, 0).start()
-
-    def body(step, carry):
-        for piece in order:
+    for copy in extra:
+        copy.wait()
+    sums[...] = jnp.zeros_like(sums)
+    slabs = 8
+    slab = depth // slabs
+    queries = qw.shape[1]
+
+    def project(source, spot, index):
+        columns = pl.ds(pl.multiple_of(index * slab, slab), slab)
+        rows = source[:, :, :, columns].reshape(-1, slab)
+        count_rows = rows.shape[0]
+        sums[spot, :, :queries] += jnp.dot(rows, q_held[columns, :], preferred_element_type=jnp.float32)
+        sums[spot, :, queries:] += jnp.dot(rows, k_held[columns, :], preferred_element_type=jnp.float32)
+
+    def advance(step, group):
+        for piece in group:
             hop(piece, step - 1).wait_recv()
-            turn = -1 - step if forward[piece] else 1 + step
-            owner = ring.index(turn)
+            owner = ring.index(-1 - step if forward[piece] else 1 + step)
             total = land[piece, step - 1].astype(jnp.float32) + part[piece, owner]
             stage[piece, step] = total.astype(jnp.bfloat16)
             hop(piece, step).start()
+
+    groups = [order[:2], order[2:]]
+    turn_over = 1 + slabs // 2
+
+    def opening(step, carry):
+        for i, group in enumerate(groups):
+            advance(step, group)
+            project(early, 0, 2 * (step - 1) + i)
+
+        @pl.when(step <= late.shape[1])
+        def _():
+            frames.relay(step - 1)
+
         return carry
 
-    lax.fori_loop(1, count - 1, body, 0)
+    lax.fori_loop(1, turn_over, opening, 0)
+    aside.wait()
+    for piece in range(late.shape[1]):
+        frames.settle(piece)
+    each = -(-slabs // (2 * (count - 1 - turn_over)))
+
+    def closing(step, carry):
+        for i, group in enumerate(groups):
+            advance(step, group)
+            unit = 2 * (step - turn_over) + i
+            start = jnp.minimum(unit * each, slabs)
+            stop = jnp.minimum(start + each, slabs)
+
+            def fold(index, inner):
+                project(late, 1, index)
+                return inner
+
+            lax.fori_loop(start, stop, fold, 0)
+        return carry
+
+    lax.fori_loop(turn_over, count - 1, closing, 0)
+    block = 2 * parts * tall
+    for f in range(frame_count):
+        for spot in range(2):
+            source = slice(f * parts * tall, (f + 1) * parts * tall)
+            begin = f * block + spot * parts * tall
+            target = slice(begin, begin + parts * tall)
+            turn, slide = cosine[target], sine_part[target]
+            for c in range(0, queries + HDIM, HDIM):
+                values = sums[spot, source, c : c + HDIM]
+                values = (values * turn + pltpu.roll(values, HDIM // 2, 1) * slide).astype(q_out.dtype)
+                if c < queries:
+                    q_out[target, c : c + HDIM] = values
+                else:
+                    pair_out[target, :HDIM] = values
+            pair_out[target, HDIM:] = sums[spot, source, queries + HDIM :].astype(pair_out.dtype)
     here = ring.index(0)
     squares = jnp.zeros((share, 1), jnp.float32)
     for piece in order:
@@ -558,30 +692,49 @@
         return carry
 
     lax.fori_loop(0, count - 1, drain, 0)
-
-
-def scatter(hidden, weight, gain, count, collective):
+    frames.finish()
+
+
+def scatter(hidden, weight, gain, text, near, query_weight, keyvalue_weight, positions, count, frame_count, collective):
     rows, depth = hidden.shape
     width = weight.shape[1]
     share = rows // count
     pieces = 4
     span = width // pieces
+    parts, tall = text.shape[:2]
+    tokens = frame_count * parts * tall
+    queries, pairs = query_weight.shape[1], keyvalue_weight.shape[1]
+    left = parts - near.shape[1]
+    cosine, sine_part = turns(positions)
     return pl.pallas_call(
-        functools.partial(scatter_kernel, count),
-        in_specs=[VMEM, ANY, VMEM],
-        out_specs=VMEM,
-        out_shape=jax.ShapeDtypeStruct((pieces, share, span), jnp.bfloat16),
+        functools.partial(scatter_kernel, count, frame_count),
+        in_specs=[VMEM, ANY, VMEM, VMEM, ANY, ANY, ANY, VMEM, VMEM],
+        out_specs=[VMEM, VMEM, VMEM],
+        out_shape=[
+            jax.ShapeDtypeStruct((pieces, share, span), jnp.bfloat16),
+            jax.ShapeDtypeStruct((tokens, queries), jnp.bfloat16),
+            jax.ShapeDtypeStruct((tokens, pairs), jnp.bfloat16),
+        ],
         scratch_shapes=[
             pltpu.VMEM((pieces, depth, span), jnp.bfloat16),
             pltpu.VMEM((pieces, count, share, span), jnp.float32),
             pltpu.VMEM((pieces, count - 1, share, span), jnp.bfloat16),
             pltpu.VMEM((pieces, count - 1, share, span), jnp.bfloat16),
+            pltpu.VMEM(query_weight.shape, query_weight.dtype),
+            pltpu.VMEM(keyvalue_weight.shape, keyvalue_weight.dtype),
+            pltpu.VMEM(near.shape, near.dtype),
+            pltpu.VMEM((frame_count, left) + text.shape[1:], text.dtype),
+            pltpu.VMEM((2, tokens // 2, queries + pairs), jnp.float32),
             pltpu.SemaphoreType.DMA((pieces,)),
             pltpu.SemaphoreType.DMA((pieces, count - 1)),
             pltpu.SemaphoreType.DMA((pieces, count - 1)),
-        ],
-        compiler_params=comm_params(collective),
-    )(hidden, weight, gain[None, :])
+        ]
+        + frame_sems(frame_count, left)
+        + [pltpu.SemaphoreType.DMA((4,))],
+        compiler_params=pltpu.CompilerParams(
+            collective_id=collective, has_side_effects=True, vmem_limit_bytes=63 * 1024 * 1024
+        ),
+    )(hidden, weight, gain[None, :], text, near, query_weight, keyvalue_weight, cosine, sine_part)
 
 
 def turns(positions):
@@ -589,74 +742,6 @@
     angles = positions.astype(jnp.float32)[:, None] * inverse[None, :]
     cosine, sine_part = jnp.cos(angles), jnp.sin(angles)
     return jnp.concatenate([cosine, cosine], axis=1), jnp.concatenate([-sine_part, sine_part], axis=1)
-
-
-def project_kernel(blocks, *refs):
-    tokens, (where, qw, kw, cosine, sine_part, q_out, pair_out, q_acc, p_acc) = refs[:blocks], refs[blocks:]
-    step = pl.program_id(0)
-    rows = jnp.concatenate([ref[...] for ref in tokens], axis=0)
-    q_part = jnp.dot(rows, qw[...], preferred_element_type=jnp.float32)
-    p_part = jnp.dot(rows, kw[...], preferred_element_type=jnp.float32)
-
-    @pl.when(step == 0)
-    def _():
-        q_acc[...] = q_part
-        p_acc[...] = p_part
-
-    @pl.when(step > 0)
-    def _():
-        q_acc[...] += q_part
-        p_acc[...] += p_part
-
-    @pl.when(step == pl.num_programs(0) - 1)
-    def _():
-        share = tokens[0].shape[0]
-        for block in range(blocks):
-            source = slice(block * share, (block + 1) * share)
-            target = pl.ds(pl.multiple_of(where[block] * share, share), share)
-            turn, slide = cosine[target, :], sine_part[target, :]
-            for head in range(q_acc.shape[1] // HDIM):
-                columns = slice(head * HDIM, (head + 1) * HDIM)
-                values = q_acc[source, columns]
-                q_out[target, columns] = (
-                    values * turn + pltpu.roll(values, HDIM // 2, 1) * slide
-                ).astype(q_out.dtype)
-            values = p_acc[source, :HDIM]
-            pair_out[target, :HDIM] = (
-                values * turn + pltpu.roll(values, HDIM // 2, 1) * slide
-            ).astype(pair_out.dtype)
-            pair_out[target, HDIM:] = p_acc[source, HDIM:].astype(pair_out.dtype)
-
-
-def project(blocks, where, positions, query_weight, keyvalue_weight):
-    share, depth = blocks[0].shape
-    rows = share * len(blocks)
-    queries, pairs = query_weight.shape[1], keyvalue_weight.shape[1]
-    slab = math.gcd(depth, 1024)
-    cosine, sine_part = turns(positions)
-    whole = lambda shape: pl.BlockSpec(shape, lambda k: (0, 0))
-    return pl.pallas_call(
-        functools.partial(project_kernel, len(blocks)),
-        grid=(depth // slab,),
-        in_specs=[pl.BlockSpec((share, slab), lambda k: (0, k))] * len(blocks)
-        + [
-            pl.BlockSpec(memory_space=pltpu.SMEM),
-            pl.BlockSpec((slab, queries), lambda k: (k, 0)),
-            pl.BlockSpec((slab, pairs), lambda k: (k, 0)),
-            whole((rows, HDIM)),
-            whole((rows, HDIM)),
-        ],
-        out_specs=[whole((rows, queries)), whole((rows, pairs))],
-        out_shape=[
-            jax.ShapeDtypeStruct((rows, queries), jnp.bfloat16),
-            jax.ShapeDtypeStruct((rows, pairs), jnp.bfloat16),
-        ],
-        scratch_shapes=[
-            pltpu.VMEM((rows, queries), jnp.float32),
-            pltpu.VMEM((rows, pairs), jnp.float32),
-        ],
-        compiler_params=pltpu.CompilerParams(vmem_limit_bytes=vmem_limit),
-    )(*blocks, where, query_weight, keyvalue_weight, cosine, sine_part)
 
 
 def causal_kernel(block_ref, q_ref, k_ref, v_ref, out_ref):
@@ -745,41 +830,25 @@
     frame_count = lax.axis_size("frame")
     seq_count = lax.axis_size("seq")
     patch_rows = patches.shape[0]
-    local_heads = vision_qkv.shape[1] // (3 * VIT_HDIM)
-    barrier = lax.optimization_barrier
-
-    normed_patches = rms_scale(patches, vit_gain).astype(jnp.bfloat16)
-    projected = lax.dot_general(
-        vision_qkv, normed_patches, (((0,), (1,)), ((), ())), preferred_element_type=jnp.float32
-    ).astype(jnp.bfloat16)
-    projected = projected.reshape(local_heads, 3 * VIT_HDIM, patch_rows)
-    vit_query = projected[:, :VIT_HDIM].reshape(local_heads * VIT_HDIM, patch_rows)
-    patch_video = jnp.repeat(video_ids, 4)
-    own_video = lax.dynamic_slice_in_dim(patch_video, frame_index * patch_rows, patch_rows)
-    pair_all, out_full = front(projected[:, VIT_HDIM:], vision_out, seq_count, frame_count, 1)
-
-    text_own = rms_scale(text_embed, llm_gain).astype(jnp.bfloat16)
-    text_own, pair_all = barrier((text_own, pair_all))
-    text_blocks, owners = [text_own], [0]
-    bit = frame_count // 2
-    while bit:
-        swap = [(i, i ^ bit) for i in range(frame_count)]
-        text_blocks = text_blocks + [lax.ppermute(block, "frame", swap) for block in text_blocks]
-        owners = owners + [mask ^ bit for mask in owners]
-        bit //= 2
-
-    vit_context = vit_attention(own_video, patch_video, vit_query, pair_all)
-    pieces = vit_context.reshape(2, -1, patch_rows)
-    merge_hidden = mid(pieces, out_full, patches, merge_gain, merge_up, seq_count, 2)
-    vision_normed = scatter(merge_hidden, merge_down, llm_gain, seq_count, 3)
-
+    token_rows = patch_rows // 4
+    own_video = lax.dynamic_slice_in_dim(video_ids, frame_index * token_rows, token_rows)
+    low = jnp.sum((video_ids[None, :] < own_video[:, None]).astype(jnp.int32), axis=1)
+    high = jnp.sum((video_ids[None, :] <= own_video[:, None]).astype(jnp.int32), axis=1)
+    context, out_full = encode(
+        patches, vit_gain, vision_qkv, jnp.repeat(4 * low, 4), jnp.repeat(4 * high, 4), vision_out,
+        seq_count, frame_count, 1,
+    )
     part_rows = text_embed.shape[0]
     seq_block = part_rows * frame_count
     first = seq_index * seq_block
-    where = jnp.bitwise_xor(frame_index, jnp.array(owners, jnp.int32))
-    text_blocks[-1], vision_normed = barrier((text_blocks[-1], vision_normed))
-    text_query, text_pair = project(
-        text_blocks, where, first + jnp.arange(seq_block, dtype=jnp.int32), query_weight, keyvalue_weight
+    text_own = rms_scale(text_embed, llm_gain).astype(jnp.bfloat16)
+    text_own = text_own.reshape(-1, 16, text_own.shape[1])
+    merge_hidden, text_near = mid(
+        context, out_full, patches, merge_gain, text_own, merge_up, seq_count, frame_count, 2
+    )
+    vision_normed, text_query, text_pair = scatter(
+        merge_hidden, merge_down, llm_gain, text_own, text_near, query_weight, keyvalue_weight,
+        first + jnp.arange(seq_block, dtype=jnp.int32), seq_count, frame_count, 3,
     )
     share = vision_normed.shape[1]
     token_pos = vision_pos.reshape(frame_count, seq_count, share).transpose(1, 0, 2)

time: 265 us -> 193 us (0.73)
  waiting for transfers between devices: 47.3 us -> 0 us
  Pallas kernels: 189 us -> 169 us
    ppermute x3 -> x0, waiting for transfers between devices: 47.3 us -> none  [local(): lax.ppermute(block, 'frame', swap)]
    pallas_call x5 -> x3, Pallas kernels: 124 us -> 104 us  [the longest x1 42.6 us: scatter(): pl.pallas_call(functools.partial(scatter_kernel, count, frame_count), in_...]
    unnamed x24 -> x15, local copies, waits for them, and re-layouts: 0.09 us -> 2.78 us
  transfers between devices with their start and end apart: 3 -> 0, of which waited for: 1 -> 0; matrix products, arithmetic and copies ran while one was open for 5% -> 0% of each run, Pallas kernels for 31% -> 0%
where the time goes in v3:
time: 193 us; the launch traced here: 192 us
  Pallas kernels  169 us (88%)
  other arithmetic  8.9 us (5%)
  local copies, waits for them, and re-layouts  8.06 us (4%)
  matrix products  5.96 us (3%)
    pallas_call x1, Pallas kernels, scatter(): pl.pallas_call(functools.partial(scatter_kernel, count, frame_count), in_...  42.6 us
    pallas_call x1, Pallas kernels, finish(): pl.pallas_call(functools.partial(finish_kernel, seq_count, frame_count),...  39.9 us
    pallas_call x1, Pallas kernels, mid(): pl.pallas_call(functools.partial(mid_kernel, count, frame_count), in_spec...  35.1 us
    pallas_call x1, Pallas kernels, encode(): pl.pallas_call(functools.partial(encode_kernel, seq_count, frame_count),...  26.5 us
    pallas_call x1, Pallas kernels, causal_attention(): pl.pallas_call(causal_kernel, grid=(width // HDIM,), in_specs=[pl.BlockSp...  25.1 us
    dot_general x2, matrix products, place(): jnp.dot(hit.astype(jnp.bfloat16), vision_rows, preferred_element_type=jnp...  5.96 us

profile of v3, /device:TPU:28, one launch (start us, length us, event | category | flops | bytes accessed | tf_op | source)
XLA Modules:
  0.0 192.3 jit_solution(17710865098247983481)
XLA Ops:
  0.0 0.8 dynamic_slice.5
  0.8 0.9 convert_reduce_fusion
  1.7 0.1 broadcast_in_dim.31
  1.8 0.7 broadcast_in_dim_reshape.8.low
  2.5 0.1 broadcast_in_dim.52
  2.6 0.7 broadcast_in_dim_reshape.9.high
  3.3 2.4 %copy.19.weight = bf16[1280,480]{1,0:T(8,128)(2,1)} copy(bf16[1280,480]{0,1:T(8,128)(2,1)} %param.15) | data formatting | bytes 2457600 | tf_op args[2]
  5.7 0.6 broadcast_in_dim.27.gain
  6.3 26.5 %shard_map.127 = (bf16[2,80,768]{2,1,0:T(8,128)(2,1)}, bf16[8,2,5,16,1280]{4,3,2,1,0:T(8,128)(2,1)}) custom-call(bf16[768,1280]{1,0:T(8,128)(2,1)} %patches.3, f32[1,1280]{1,0:T(1,128)} %broadcast_in_dim.27.gain, bf16[1280,480]{1,0:T(8,128)(2,1)} %copy.19.weight, s32[1,768]{1,0:T(1,128)} %broadcast_in_dim_reshape.8.low, ...), custom_call_target="tpu_custom_call" | custom-call | tf_op jit(solution)/shard_map/pallas_call | solution.py:329
  32.9 0.5 fusion.5
  33.4 0.0 copy-done.1
  33.4 0.0 copy-start.3
  33.4 2.0 %fusion.7 = bf16[128,8192]{1,0:T(8,128)(2,1)} fusion(bf16[128,8192]{1,0:T(8,128)(2,1)S(1)} %copy-done, f32[8192]{0:T(1024)S(1)} %copy-done.1, f32[128]{0:T(128)S(1)} %add_rsqrt_fusion), kind=kLoop, calls=%fused_computation.10 | loop fusion | flops 4194304 | bytes 4227584 | tf_op jit(solution)/shard_map/convert_element_type | solution.py:844
  35.4 0.6 broadcast_in_dim.53.gain
  36.0 35.1 %shard_map.128 = (bf16[192,640]{1,0:T(8,128)(2,1)}, bf16[4,4,16,8192]{3,2,1,0:T(8,128)(2,1)}) custom-call(bf16[2,80,768]{2,1,0:T(8,128)(2,1)} %get-tuple-element.14.block, bf16[8,160,1280]{2,1,0:T(8,128)(2,1)} %bitcast.11, bf16[768,1280]{1,0:T(8,128)(2,1)} %patches.3, f32[1,1280]{1,0:T(1,128)} %broadcast_in_dim.53.gain, bf16[8,16,8192]{2,1,0:T(8,128)(2,1)} %bitcast.9, ...), custom_call_target="tpu_custom_call" | custom-call | tf_op jit(solution)/shard_map/pallas_call | solution.py:429
  71.1 1.0 fusion.20
  72.1 0.9 pad_maximum_fusion.1.sine_part
  73.0 0.8 pad_maximum_fusion.cosine
  73.9 42.6 %shard_map.129 = (bf16[4,24,2048]{2,1,0:T(8,128)(2,1)}, bf16[512,512]{1,0:T(8,128)(2,1)}, bf16[512,256]{1,0:T(8,128)(2,1)}) custom-call(bf16[192,640]{1,0:T(8,128)(2,1)} %get-tuple-element.16.hidden, bf16[640,8192]{1,0:T(8,128)(2,1)} %weight.2, f32[1,8192]{1,0:T(1,128)} %bitcast.14, bf16[8,16,8192]{2,1,0:T(8,128)(2,1)} %bitcast.10, ...), custom_call_target="tpu_custom_call" | custom-call | tf_op jit(solution)/shard_map/pallas_call | solution.py:709
  116.4 0.1 reshape.57
  116.6 0.1 convert_element_type.43
  116.6 0.3 fusion.21
  116.9 0.7 pad_maximum_fusion.2
  117.6 39.9 %shard_map.130 = (bf16[8,2,256,256]{3,2,1,0:T(8,128)(2,1)}, bf16[8,2,48,768]{3,2,1,0:T(8,128)(2,1)}) custom-call(bf16[4,24,2048]{2,1,0:T(8,128)(2,1)} %get-tuple-element.18.tokens, bf16[2,256,256]{2,1,0:T(8,128)(2,1)} %bitcast.13, bf16[8192,512]{1,0:T(8,128)(2,1)} %qw.3, bf16[8192,256]{1,0:T(8,128)(2,1)} %kw.3, f32[96,128]{1,0:T(8,128)} %get-tuple-element.37.cosine, ...), custom_call_target="tpu_custom_call" | custom-call | tf_op jit(solution)/shard_map/pallas_call | solution.py:530
  157.5 0.1 eq.29
  157.6 1.4 fusion.1
  159.0 4.5 %fusion.4 = bf16[4096,256]{1,0:T(8,128)(2,1)S(1)} fusion(bf16[4096,256]{1,0:T(8,128)(2,1)} %bitcast.16, s32[768]{0:T(1024)S(1)} %eq.29, pred[4096]{0:T(1024)(128)(4,1)S(1)} %fusion.1, bf16[768,768]{1,0:T(8,128)(2,1)} %bitcast.17), kind=kOutput, calls=%fused_computation.7 | convolution fusion | flops 1615855616 | bytes 4594688 | tf_op jit(solution)/shard_map/dot_general | solution.py:808
  163.6 1.5 fusion.23
  165.1 0.3 compare_reduce_fusion
  165.4 0.3 copy-done.6
  165.7 1.4 fusion.13.q_ref
  167.2 25.1 %shard_map.131 = bf16[512,512]{1,0:T(8,128)(2,1)} custom-call(s32[1]{0:T(128)} %bitcast.block_ref, bf16[512,512]{1,0:T(8,128)(2,1)} %fusion.13.q_ref, bf16[4096,128]{1,0:T(8,128)(2,1)} %get-tuple-element.26.k_ref, bf16[4096,128]{1,0:T(8,128)(2,1)} %get-tuple-element.25.v_ref), custom_call_target="tpu_custom_call" | custom-call | tf_op jit(solution)/shard_map/pallas_call | solution.py:790
  (17 shorter events, 0.1 us)
Async XLA Ops:
  0.0 5.7 %copy-start.2 = (f32[1280]{0:T(1024)S(1)}, f32[1280]{0:T(1024)}, u32[]{:S(2)}) copy-start(f32[1280]{0:T(1024)} %param.14) | copy-start | bytes 15364
  5.7 27.1 %copy-start = (bf16[128,8192]{1,0:T(8,128)(2,1)S(1)}, bf16[128,8192]{1,0:T(8,128)(2,1)}, u32[]{:S(2)}) copy-start(bf16[128,8192]{1,0:T(8,128)(2,1)} %param.22) | copy-start | bytes 6291460
  6.3 27.0 %copy-start.1 = (f32[8192]{0:T(1024)S(1)}, f32[8192]{0:T(1024)}, u32[]{:S(2)}) copy-start(f32[8192]{0:T(1024)} %param.23) | copy-start | bytes 98308
  33.4 2.0 %copy-start.3 = (f32[1280]{0:T(1024)S(1)}, f32[1280]{0:T(1024)}, u32[]{:S(2)}) copy-start(f32[1280]{0:T(1024)} %param.18) | copy-start | bytes 15364
  73.9 42.6 %copy-start.4 = (s32[768]{0:T(1024)S(1)}, s32[768]{0:T(1024)}, u32[]{:S(2)}) copy-start(s32[768]{0:T(1024)} %param.21) | copy-start | bytes 9220
  163.6 1.8 copy-start.5
  163.6 2.1 %copy-start.6 = (bf16[512,512]{1,0:T(8,128)(2,1)S(1)}, bf16[512,512]{1,0:T(8,128)(2,1)}, u32[]{:S(2)}) copy-start(bf16[512,512]{1,0:T(8,128)(2,1)} %get-tuple-element.21) | copy-start | bytes 1572868

commit v4 on v3

--- a/solution.py
+++ b/solution.py
@@ -9,6 +9,7 @@
 from jax.sharding import PartitionSpec as P
 
 VIT_HDIM = 80
+VIDEOS = 3
 HDIM = 128
 
 
@@ -16,13 +17,6 @@
 rope_base = 1000000.0
 lowest = -1e30
 vmem_limit = 56 * 1024 * 1024
-
-
-def rms_scale(matrix, scales):
-    widened = matrix.astype(jnp.float32)
-    factor = lax.rsqrt(jnp.mean(widened * widened, axis=-1, keepdims=True) + epsilon)
-    return widened * factor * scales
-
 
 MESH = pl.DeviceIdType.MESH
 ANY = pl.BlockSpec(memory_space=pl.ANY)
@@ -202,7 +196,9 @@
     )
 
 
-def encode_kernel(seq_count, frame_count, patches, gain, weight, low, high, out_weight, context, weight_out, *scratch):
+def encode_kernel(
+    seq_count, frame_count, patches, gain, weight, ids, out_weight, text, text_gain, context, weight_out, text_out, *scratch
+):
     mine, query, held, flat, peak, mass, blend, fsend, frecv, rsend, rrecv, tsend, trecv, own = scratch
     ring = Ring(seq_count)
     heads, tall, rows = mine.shape
@@ -228,7 +224,7 @@
     factor = lax.rsqrt(jnp.mean(widened * widened, axis=-1, keepdims=True) + epsilon)
     normed = (widened * factor * gain[...]).astype(jnp.bfloat16)
     projected = lax.dot_general(
-        weight[...], normed, (((0,), (1,)), ((), ())), preferred_element_type=jnp.float32
+        weight[...], normed, (((1,), (1,)), ((), ())), preferred_element_type=jnp.float32
     ).astype(jnp.bfloat16)
     for head in range(heads):
         base = head * 3 * VIT_HDIM
@@ -237,6 +233,11 @@
     frames.start()
     local = pltpu.make_async_copy(mine, held.at[frames.me], own.at[1])
     local.start()
+    per_token = frame_count * rows // ids.shape[1]
+    ends = [
+        per_token * jnp.sum((ids[...] <= video).astype(jnp.int32), axis=1, keepdims=True)
+        for video in range(VIDEOS - 1)
+    ]
     local.wait()
     near = [frames.chip * 2, frames.chip * 2 + 1]
     far = [
@@ -250,9 +251,15 @@
             flat[slot, head] = held[slot, head, :VIT_HDIM, :].T
 
     def attend(slots, head, start):
-        columns = slice(start, start + tile)
+        columns = pl.ds(start, tile)
         queries = query[head, :, columns]
-        first, past = low[:, columns], high[:, columns]
+        places = frames.me * rows + start + lax.broadcasted_iota(jnp.int32, (1, tile), 1)
+        first = jnp.zeros((1, tile), jnp.int32)
+        past = jnp.full((1, tile), frame_count * rows, jnp.int32)
+        for end in ends:
+            first = jnp.where(places >= end, end, first)
+        for end in reversed(ends):
+            past = jnp.where(places < end, end, past)
         scores = []
         for slot in slots:
             part = jnp.dot(flat[slot, head], queries, preferred_element_type=jnp.float32)
@@ -275,18 +282,30 @@
 
     def first_pass(head):
         flatten(near, head)
-        for start in range(0, rows, tile):
-            columns = slice(start, start + tile)
+
+        def one(index, carry):
+            start = pl.multiple_of(index * tile, tile)
+            columns = pl.ds(start, tile)
             highest, total, mixed = attend(near, head, start)
             peak[head : head + 1, columns] = highest
             mass[head : head + 1, columns] = total
             blend[head, :, columns] = mixed
+            return carry
+
+        lax.fori_loop(0, rows // tile, one, 0)
+
+    def norm_text(index):
+        words = text[index].astype(jnp.float32)
+        level = lax.rsqrt(jnp.mean(words * words, axis=-1, keepdims=True) + epsilon)
+        text_out[index] = (words * level * text_gain[...]).astype(text_out.dtype)
 
     def second_pass(head):
         if far:
             flatten(far, head)
-        for start in range(0, rows, tile):
-            columns = slice(start, start + tile)
+
+        def one(index, carry):
+            start = pl.multiple_of(index * tile, tile)
+            columns = pl.ds(start, tile)
             total, mixed = mass[head : head + 1, columns], blend[head, :, columns]
             if far:
                 before = peak[head : head + 1, columns]
@@ -296,11 +315,16 @@
                 total = total * old + more * new
                 mixed = mixed * old + extra * new
             context[head, :, columns] = (mixed / total).astype(context.dtype)
+            return carry
+
+        lax.fori_loop(0, rows // tile, one, 0)
 
     gather.advance(0, landed)
     for head in range(heads):
         frames.inside(0, head).wait_recv()
         first_pass(head)
+        for index in range(head, text.shape[0], heads):
+            norm_text(index)
         frames.relay(head)
         if head + 1 < gather.steps:
             gather.advance(head + 1, landed)
@@ -319,20 +343,22 @@
         copy.wait()
 
 
-def encode(patches, gain, weight, low, high, out_weight, seq_count, frame_count, collective):
+def encode(patches, gain, weight, ids, out_weight, text, text_gain, seq_count, frame_count, collective):
     rows = patches.shape[0]
     heads = weight.shape[1] // (3 * VIT_HDIM)
     half = out_weight.shape[0] // 2
     tall = math.gcd(half, 16)
     pieces = half // tall
     out_weight = out_weight.reshape(2, pieces, tall, -1)
-    context, weight_out = pl.pallas_call(
+    text = text.reshape(-1, 16, text.shape[1])
+    context, weight_out, text_out = pl.pallas_call(
         functools.partial(encode_kernel, seq_count, frame_count),
-        in_specs=[VMEM] * 6,
-        out_specs=[VMEM, ANY],
+        in_specs=[VMEM] * 7,
+        out_specs=[VMEM, ANY, VMEM],
         out_shape=[
             jax.ShapeDtypeStruct((heads, VIT_HDIM, rows), jnp.bfloat16),
             jax.ShapeDtypeStruct((seq_count,) + out_weight.shape, out_weight.dtype),
+            jax.ShapeDtypeStruct(text.shape, text.dtype),
         ],
         scratch_shapes=[
             pltpu.VMEM((heads, 2 * VIT_HDIM, rows), jnp.bfloat16),
@@ -347,8 +373,8 @@
         + ring_sems(seq_count, pieces) * 2
         + [pltpu.SemaphoreType.DMA((2,))],
         compiler_params=comm_params(collective),
-    )(patches, gain[None, :], weight, low[None, :], high[None, :], out_weight)
-    return context, weight_out.reshape(seq_count, 2 * half, -1)
+    )(patches, gain[None, :], weight.T, ids[None, :], out_weight, text, text_gain[None, :])
+    return context, weight_out.reshape(seq_count, 2 * half, -1), text_out
 
 
 def mid_kernel(
@@ -448,8 +474,11 @@
     )(block, out_weight, patches, gain[None, :], text, up)
 
 
-def finish_kernel(seq_count, frame_count, tokens, text, qw, kw, cosine, sine_part, text_out, out, *scratch):
-    held, q_held, k_held, mine, load, fsend, frecv, tsend, trecv, vsend, vrecv, own = scratch
+def finish_kernel(
+    seq_count, frame_count, tokens, text, query, covered, spots, qw, kw, cosine, sine_part, result, *scratch
+):
+    (held, q_held, k_held, mine, pair, vision, peak, mass, blend, select, locate,
+     load, fsend, frecv, tsend, trecv, vsend, vrecv, own) = scratch
     parts, share, span = tokens.shape
     loads = []
     for part in range(parts):
@@ -461,97 +490,251 @@
     ring = Ring(seq_count)
     here = ring.index(0)
     frames = FrameGather(frame_count, tokens, held, fsend, frecv, parts)
-    texts = RingGather(ring, text, lambda i, piece: text_out.at[i, piece], tsend, trecv, text.shape[0])
-    visions = RingGather(ring, mine, lambda i, piece: out.at[i, piece], vsend, vrecv, mine.shape[0])
+    texts = RingGather(ring, text, lambda i, piece: pair.at[i, piece], tsend, trecv, text.shape[0])
+    visions = RingGather(ring, mine, lambda i, piece: vision.at[i, piece], vsend, vrecv, mine.shape[0])
     greet([ring.left, ring.right] + frames.partners())
     frames.start()
     texts.start()
     keep = [
         pltpu.make_async_copy(tokens, held.at[frames.me], own.at[0]),
-        pltpu.make_async_copy(text, text_out.at[here], own.at[1]),
+        pltpu.make_async_copy(text, pair.at[here], own.at[1]),
     ]
     for copy in keep:
         copy.start()
-    early = texts.steps // 2
+    rows, queries = query.shape
+    heads = queries // HDIM
+    couple = 2 if heads % 2 == 0 else 1
+    scale = HDIM ** (-0.5) * math.log2(math.e)
+    total = spots.shape[1]
+    slots = locate.shape[0]
+
+    inside = (spots[...] >= here * rows) & (spots[...] < (here + 1) * rows)
+    ahead = lax.broadcasted_iota(jnp.int32, (total, total), 0) < lax.broadcasted_iota(
+        jnp.int32, (total, total), 1
+    )
+    flags = jnp.where(inside, 1.0, 0.0)
+    rank = jnp.dot(
+        jnp.broadcast_to(flags, (8, total)).astype(jnp.bfloat16),
+        jnp.where(ahead, 1.0, 0.0).astype(jnp.bfloat16),
+        preferred_element_type=jnp.float32,
+    )[:1]
+    slot = lax.broadcasted_iota(jnp.int32, (slots, total), 0).astype(jnp.float32)
+    chosen = jnp.where(inside & (slot == rank), 1.0, 0.0)
+    select[...] = chosen.astype(select.dtype)
+    locate[...] = jnp.sum(chosen * (spots[...] + 1 - here * rows).astype(jnp.float32), axis=1, keepdims=True) - 1.0
+
+    def keys_of(block):
+        return pair[block].reshape(rows, 2 * HDIM)
+
+    def weigh(scores, highest):
+        weights = jnp.exp2((scores - highest) * scale)
+        return weights.astype(jnp.bfloat16), jnp.sum(weights, axis=1, keepdims=True)
+
+    def score(left, right):
+        return lax.dot_general(left, right, (((1,), (1,)), ((), ())), preferred_element_type=jnp.float32)
+
+    def fold(head, scores, values):
+        before = peak[head]
+        highest = jnp.maximum(before, jnp.max(scores, axis=1, keepdims=True))
+        weights, more = weigh(scores, highest)
+        shrink = jnp.exp2((before - highest) * scale)
+        peak[head] = highest
+        mass[head] = mass[head] * shrink + more
+        blend[head] = blend[head] * shrink + jnp.dot(weights, values, preferred_element_type=jnp.float32)
+
+    def query_of(group, j):
+        return query[:, pl.ds(pl.multiple_of((group * couple + j) * HDIM, HDIM), HDIM)]
+
+    groups = heads // couple
+
+    def diagonal(group):
+        block = text[...].reshape(rows, 2 * HDIM)
+        lower = lax.broadcasted_iota(jnp.int32, (rows, rows), 0) >= lax.broadcasted_iota(
+            jnp.int32, (rows, rows), 1
+        )
+        for j in range(couple):
+            head = group * couple + j
+            scores = score(query_of(group, j), block[:, :HDIM]) + covered[here, :1, :]
+            scores = jnp.where(lower, scores, lowest)
+            highest = jnp.max(scores, axis=1, keepdims=True)
+            weights, more = weigh(scores, highest)
+            peak[head] = highest
+            mass[head] = more
+            blend[head] = jnp.dot(weights, block[:, HDIM:], preferred_element_type=jnp.float32)
+
+    def earlier(group, owner):
+        block = keys_of(owner)
+        for j in range(couple):
+            scores = score(query_of(group, j), block[:, :HDIM]) + covered[owner, :1, :]
+            fold(group * couple + j, scores, block[:, HDIM:])
+
+    def vision_rows():
+        for part in range(parts):
+            frames.settle(part)
+        frames.finish()
+        for copy in keep:
+            copy.wait()
+        for copy in loads:
+            copy.wait()
+        q_total, k_total = None, None
+        for part in range(parts):
+            lines = jnp.concatenate([held[f, part] for f in range(frame_count)], axis=0)
+            slab = slice(part * span, (part + 1) * span)
+            q_part = jnp.dot(lines, q_held[slab], preferred_element_type=jnp.float32)
+            k_part = jnp.dot(lines, k_held[slab], preferred_element_type=jnp.float32)
+            q_total = q_part if part == 0 else q_total + q_part
+            k_total = k_part if part == 0 else k_total + k_part
+        turn, slide = cosine[...], sine_part[...]
+
+        def turned(values):
+            return values * turn + pltpu.roll(values, HDIM // 2, 1) * slide
+
+        columns = [turned(q_total[:, c : c + HDIM]) for c in range(0, queries, HDIM)]
+        columns += [turned(k_total[:, :HDIM]), k_total[:, HDIM:]]
+        pieces, tall = mine.shape[:2]
+        for i, values in enumerate(columns):
+            for piece in range(pieces):
+                mine[piece, :, i * HDIM : (i + 1) * HDIM] = values[
+                    piece * tall : (piece + 1) * tall
+                ].astype(mine.dtype)
+        visions.start()
+        pltpu.make_async_copy(mine, vision.at[here], own.at[2]).start()
+
+    units = groups * seq_count
+    events = {}
+
+    def at(unit, action):
+        events.setdefault(min(unit, units - 1), []).append(action)
+
     for part in range(parts):
-        frames.relay(part)
-        if part % 2 and part // 2 < early:
-            texts.advance(part // 2)
-    for copy in keep:
-        copy.wait()
-    for part in range(parts):
-        frames.settle(part)
-    frames.finish()
-    for copy in loads:
-        copy.wait()
-    q_total, k_total = None, None
-    for part in range(parts):
-        rows = jnp.concatenate([held[f, part] for f in range(frame_count)], axis=0)
-        slab = slice(part * span, (part + 1) * span)
-        q_part = jnp.dot(rows, q_held[slab], preferred_element_type=jnp.float32)
-        k_part = jnp.dot(rows, k_held[slab], preferred_element_type=jnp.float32)
-        q_total = q_part if part == 0 else q_total + q_part
-        k_total = k_part if part == 0 else k_total + k_part
-    turn, slide = cosine[...], sine_part[...]
-
-    def turned(values):
-        return values * turn + pltpu.roll(values, HDIM // 2, 1) * slide
-
-    queries = q_total.shape[1]
-    columns = [turned(q_total[:, c : c + HDIM]) for c in range(0, queries, HDIM)]
-    columns += [turned(k_total[:, :HDIM]), k_total[:, HDIM:]]
-    pieces, tall = mine.shape[:2]
-    for i, values in enumerate(columns):
-        for piece in range(pieces):
-            mine[piece, :, i * HDIM : (i + 1) * HDIM] = values[
-                piece * tall : (piece + 1) * tall
-            ].astype(mine.dtype)
-    visions.start()
-    last = pltpu.make_async_copy(mine, out.at[here], own.at[0])
-    last.start()
-    done = min(early, parts // 2)
-    for step in range(max(texts.steps - done, visions.steps)):
-        if done + step < texts.steps:
-            texts.advance(done + step)
-        if step < visions.steps:
-            visions.advance(step)
-    last.wait()
+        at([0, 1, 2, 3][part] if part < 4 else 3, functools.partial(frames.relay, part))
+    stride = 2 * groups
+    for step in range(texts.steps):
+        at(groups - 1 + stride * step, functools.partial(texts.advance, step))
+    at(groups + 2, vision_rows)
+    for step in range(visions.steps):
+        at(groups + 5 + 3 * step, functools.partial(visions.advance, step))
+
+    def body(unit, carry):
+        turn_of, group = lax.div(unit, groups), lax.rem(unit, groups)
+        far, odd = lax.div(turn_of + 1, 2), lax.rem(turn_of, 2)
+        owner = ring_index(
+            lax.rem(ring.here + far * (1 - 2 * odd) + 2 * seq_count, seq_count), seq_count
+        )
+
+        @pl.when(turn_of == 0)
+        def _():
+            diagonal(group)
+
+        @pl.when((turn_of > 0) & (owner < here))
+        def _():
+            earlier(group, owner)
+
+        for index, actions in sorted(events.items()):
+
+            def act(actions=actions):
+                for action in actions:
+                    action()
+
+            pl.when(unit == index)(act)
+        return carry
+
+    lax.fori_loop(0, units, body, 0)
+    pltpu.make_async_copy(mine, vision.at[here], own.at[2]).wait()
+
+    both = vision[...].reshape(total, queries + 2 * HDIM)
+    vision_keys, vision_values = both[:, queries : queries + HDIM], both[:, queries + HDIM :]
+    places = here * rows + lax.broadcasted_iota(jnp.int32, (rows, 1), 0)
+    for head in range(heads):
+        scores = score(query[:, head * HDIM : (head + 1) * HDIM], vision_keys)
+        fold(head, jnp.where(spots[...] <= places, scores, lowest), vision_values)
+
+    picked = jnp.dot(select[...], both[:, :queries], preferred_element_type=jnp.float32).astype(jnp.bfloat16)
+    stacked = jnp.concatenate([picked[:, c : c + HDIM] for c in range(0, queries, HDIM)], axis=0)
+    spot = jnp.concatenate([locate[...]] * heads, axis=0)
+
+    def add(state, scores, values):
+        before, amount, mixed = state
+        highest = jnp.maximum(before, jnp.max(scores, axis=1, keepdims=True))
+        weights, more = weigh(scores, highest)
+        shrink = jnp.exp2((before - highest) * scale)
+        mixed = mixed * shrink + jnp.dot(weights, values, preferred_element_type=jnp.float32)
+        return highest, amount * shrink + more, mixed
+
+    tall = stacked.shape[0]
+    state = (
+        jnp.full((tall, 1), lowest, jnp.float32),
+        jnp.zeros((tall, 1), jnp.float32),
+        jnp.zeros((tall, HDIM), jnp.float32),
+    )
+    seen = (spots[...] - here * rows).astype(jnp.float32)
+    state = add(state, jnp.where(seen <= spot, score(stacked, vision_keys), lowest), vision_values)
+    block = text[...].reshape(rows, 2 * HDIM)
+    column = lax.broadcasted_iota(jnp.int32, (1, rows), 1).astype(jnp.float32)
+    scores = score(stacked, block[:, :HDIM]) + covered[here, :1, :]
+    state = add(state, jnp.where(column <= spot, scores, lowest), block[:, HDIM:])
+
+    def past(owner, now):
+        block = keys_of(owner)
+        return add(now, score(stacked, block[:, :HDIM]) + covered[owner, :1, :], block[:, HDIM:])
+
+    _, amount, mixed = lax.fori_loop(0, here, past, state)
+    mixed = (mixed / amount).astype(jnp.bfloat16)
+    picked = jnp.concatenate([mixed[h * slots : (h + 1) * slots] for h in range(heads)], axis=1)
+    column = lax.broadcasted_iota(jnp.int32, (slots, rows), 1).astype(jnp.float32)
+    spread = jnp.where(column == locate[...], 1.0, 0.0).astype(jnp.bfloat16)
+    back = (((0,), (0,)), ((), ()))
+    moved = lax.dot_general(spread, picked, back, preferred_element_type=jnp.float32)
+    taken = lax.dot_general(
+        spread, jnp.ones((slots, HDIM), jnp.bfloat16), back, preferred_element_type=jnp.float32
+    )
+    for head in range(heads):
+        columns = slice(head * HDIM, (head + 1) * HDIM)
+        kept = blend[head] / mass[head]
+        result[:, columns] = jnp.where(taken > 0.5, moved[:, columns], kept).astype(result.dtype)
     texts.finish()
     visions.finish()
 
 
-def finish(tokens, text, positions, query_weight, keyvalue_weight, seq_count, frame_count, collective):
+def finish(tokens, text, query, covered, spots, tables, query_weight, keyvalue_weight, seq_count, frame_count, collective):
     parts, share, span = tokens.shape
-    rows = frame_count * share
-    width = query_weight.shape[1] + keyvalue_weight.shape[1]
+    lines = frame_count * share
+    rows, queries = query.shape
+    heads = queries // HDIM
+    width = queries + keyvalue_weight.shape[1]
+    slots = frame_count * -(-3 * share // 2)
     text = text.reshape(2, -1, text.shape[1])
-    mine = (2, rows // 2, width)
-    cosine, sine_part = turns(positions)
-    text_out, out = pl.pallas_call(
+    mine = (2, lines // 2, width)
+    cosine, sine_part = tables
+    return pl.pallas_call(
         functools.partial(finish_kernel, seq_count, frame_count),
-        in_specs=[VMEM, VMEM, ANY, ANY, VMEM, VMEM],
-        out_specs=[ANY, ANY],
-        out_shape=[
-            jax.ShapeDtypeStruct((seq_count,) + text.shape, text.dtype),
-            jax.ShapeDtypeStruct((seq_count,) + mine, text.dtype),
-        ],
+        in_specs=[VMEM] * 5 + [ANY] * 2 + [VMEM] * 2,
+        out_specs=VMEM,
+        out_shape=jax.ShapeDtypeStruct((rows, queries), jnp.bfloat16),
         scratch_shapes=[
             pltpu.VMEM((frame_count,) + tokens.shape, tokens.dtype),
             pltpu.VMEM(query_weight.shape, query_weight.dtype),
             pltpu.VMEM(keyvalue_weight.shape, keyvalue_weight.dtype),
             pltpu.VMEM(mine, text.dtype),
+            pltpu.VMEM((seq_count,) + text.shape, text.dtype),
+            pltpu.VMEM((seq_count,) + mine, text.dtype),
+            pltpu.VMEM((heads, rows, 1), jnp.float32),
+            pltpu.VMEM((heads, rows, 1), jnp.float32),
+            pltpu.VMEM((heads, rows, HDIM), jnp.float32),
+            pltpu.VMEM((slots, seq_count * lines), jnp.bfloat16),
+            pltpu.VMEM((slots, 1), jnp.float32),
             pltpu.SemaphoreType.DMA((2, parts)),
         ]
         + frame_sems(frame_count, parts)
         + ring_sems(seq_count, 2) * 2
-        + [pltpu.SemaphoreType.DMA((2,))],
+        + [pltpu.SemaphoreType.DMA((3,))],
         compiler_params=comm_params(collective),
-    )(tokens, text, query_weight, keyvalue_weight, cosine, sine_part)
-    return text_out.reshape(-1, text.shape[-1]), out.reshape(-1, width)
+    )(tokens, text, query, covered, spots, query_weight, keyvalue_weight, cosine, sine_part)
 
 
 def scatter_kernel(
-    count, frame_count, hidden, weight, gain, text, near, qw, kw, cosine, sine_part, out, q_out, pair_out, *scratch
+    count, frame_count, hidden, weight, gain, text, near, qw, kw, cosine, sine_part, spots,
+    out, q_out, pair_out, covered, *scratch
 ):
     held, part, stage, land, q_held, k_held, early, late, sums, load, send, recv, fsend, frecv, own = scratch
     ring = Ring(count)
@@ -623,6 +806,18 @@
             stage[piece, step] = total.astype(jnp.bfloat16)
             hop(piece, step).start()
 
+    def cover(block):
+        shape = (covered.shape[2], spots.shape[1])
+        keys = block * shape[0] + lax.broadcasted_iota(jnp.int32, shape, 0)
+        hits = (keys == spots[...]).astype(jnp.float32).astype(jnp.bfloat16)
+        total = lax.dot_general(
+            jnp.ones((covered.shape[1], shape[1]), jnp.bfloat16),
+            hits,
+            (((1,), (1,)), ((), ())),
+            preferred_element_type=jnp.float32,
+        )
+        covered[block] = jnp.where(total > 0.5, lowest, 0.0)
+
     groups = [order[:2], order[2:]]
     turn_over = 1 + slabs // 2
 
@@ -630,6 +825,8 @@
         for i, group in enumerate(groups):
             advance(step, group)
             project(early, 0, 2 * (step - 1) + i)
+            for block in range(count // slabs):
+                cover((2 * (step - 1) + i) * (count // slabs) + block)
 
         @pl.when(step <= late.shape[1])
         def _():
@@ -695,7 +892,7 @@
     frames.finish()
 
 
-def scatter(hidden, weight, gain, text, near, query_weight, keyvalue_weight, positions, count, frame_count, collective):
+def scatter(hidden, weight, gain, text, near, query_weight, keyvalue_weight, tables, spots, count, frame_count, collective):
     rows, depth = hidden.shape
     width = weight.shape[1]
     share = rows // count
@@ -705,15 +902,16 @@
     tokens = frame_count * parts * tall
     queries, pairs = query_weight.shape[1], keyvalue_weight.shape[1]
     left = parts - near.shape[1]
-    cosine, sine_part = turns(positions)
+    cosine, sine_part = tables
     return pl.pallas_call(
         functools.partial(scatter_kernel, count, frame_count),
-        in_specs=[VMEM, ANY, VMEM, VMEM, ANY, ANY, ANY, VMEM, VMEM],
-        out_specs=[VMEM, VMEM, VMEM],
+        in_specs=[VMEM, ANY, VMEM, VMEM, ANY, ANY, ANY, VMEM, VMEM, VMEM],
+        out_specs=[VMEM, VMEM, VMEM, VMEM],
         out_shape=[
             jax.ShapeDtypeStruct((pieces, share, span), jnp.bfloat16),
             jax.ShapeDtypeStruct((tokens, queries), jnp.bfloat16),
             jax.ShapeDtypeStruct((tokens, pairs), jnp.bfloat16),
+            jax.ShapeDtypeStruct((count, 8, tokens), jnp.float32),
         ],
         scratch_shapes=[
             pltpu.VMEM((pieces, depth, span), jnp.bfloat16),
@@ -734,80 +932,14 @@
         compiler_params=pltpu.CompilerParams(
             collective_id=collective, has_side_effects=True, vmem_limit_bytes=63 * 1024 * 1024
         ),
-    )(hidden, weight, gain[None, :], text, near, query_weight, keyvalue_weight, cosine, sine_part)
+    )(hidden, weight, gain[None, :], text, near, query_weight, keyvalue_weight, cosine, sine_part, spots)
 
 
 def turns(positions):
-    inverse = rope_base ** (-2.0 * jnp.arange(HDIM // 2, dtype=jnp.float32) / HDIM)
+    lanes = jnp.arange(HDIM, dtype=jnp.int32)
+    inverse = rope_base ** (-2.0 * (lanes % (HDIM // 2)).astype(jnp.float32) / HDIM)
     angles = positions.astype(jnp.float32)[:, None] * inverse[None, :]
-    cosine, sine_part = jnp.cos(angles), jnp.sin(angles)
-    return jnp.concatenate([cosine, cosine], axis=1), jnp.concatenate([-sine_part, sine_part], axis=1)
-
-
-def causal_kernel(block_ref, q_ref, k_ref, v_ref, out_ref):
-    rows = q_ref.shape[0]
-    queries = q_ref[...]
-
-    def fold(start, state_in, masked):
-        running_max, running_sum, weighted = state_in
-        scores = lax.dot_general(
-            queries,
-            k_ref[pl.ds(start, rows), :],
-            (((1,), (1,)), ((), ())),
-            preferred_element_type=jnp.float32,
-        )
-        if masked:
-            row_id = lax.broadcasted_iota(jnp.int32, (rows, rows), 0)
-            column_id = lax.broadcasted_iota(jnp.int32, (rows, rows), 1)
-            scores = jnp.where(row_id >= column_id, scores, lowest)
-        new_max = jnp.maximum(running_max, jnp.max(scores, axis=1, keepdims=True))
-        weights = jnp.exp((scores - new_max) * HDIM ** (-0.5))
-        shrink = jnp.exp((running_max - new_max) * HDIM ** (-0.5))
-        running_sum = running_sum * shrink + jnp.sum(weights, axis=1, keepdims=True)
-        update = jnp.dot(
-            weights.astype(jnp.bfloat16),
-            v_ref[pl.ds(start, rows), :],
-            preferred_element_type=jnp.float32,
-        )
-        return (new_max, running_sum, weighted * shrink + update)
-
-    state = (
-        jnp.full((rows, 1), lowest, jnp.float32),
-        jnp.zeros((rows, 1), jnp.float32),
-        jnp.zeros((rows, HDIM), jnp.float32),
-    )
-    own = block_ref[0]
-    state = fold(pl.multiple_of(own * rows, rows), state, True)
-    _, running_sum, weighted = lax.fori_loop(
-        0, own, lambda i, now: fold(pl.multiple_of(i * rows, rows), now, False), state
-    )
-    out_ref[...] = (weighted / running_sum).astype(out_ref.dtype)
-
-
-def causal_attention(block_index, queries, key_rows, value_rows):
-    rows, width = queries.shape
-    keys = key_rows.shape[0]
-    return pl.pallas_call(
-        causal_kernel,
-        grid=(width // HDIM,),
-        in_specs=[
-            pl.BlockSpec(memory_space=pltpu.SMEM),
-            pl.BlockSpec((rows, HDIM), lambda h: (0, h)),
-            pl.BlockSpec((keys, HDIM), lambda h: (0, 0)),
-            pl.BlockSpec((keys, HDIM), lambda h: (0, 0)),
-        ],
-        out_specs=pl.BlockSpec((rows, HDIM), lambda h: (0, h)),
-        out_shape=jax.ShapeDtypeStruct((rows, width), jnp.bfloat16),
-        compiler_params=pltpu.CompilerParams(vmem_limit_bytes=vmem_limit),
-    )(block_index[None], queries, key_rows, value_rows)
-
-
-def place(token_pos, first, text_rows, vision_rows):
-    spots = first + jnp.arange(text_rows.shape[0], dtype=jnp.int32)
-    hit = spots[:, None] == token_pos[None, :]
-    moved = jnp.dot(hit.astype(jnp.bfloat16), vision_rows, preferred_element_type=jnp.float32)
-    taken = jnp.any(hit, axis=1, keepdims=True)
-    return jnp.where(taken, moved.astype(jnp.bfloat16), text_rows)
+    return jnp.cos(angles), jnp.where(lanes < HDIM // 2, -1.0, 1.0) * jnp.sin(angles)
 
 
 def local(
@@ -830,37 +962,26 @@
     frame_count = lax.axis_size("frame")
     seq_count = lax.axis_size("seq")
     patch_rows = patches.shape[0]
-    token_rows = patch_rows // 4
-    own_video = lax.dynamic_slice_in_dim(video_ids, frame_index * token_rows, token_rows)
-    low = jnp.sum((video_ids[None, :] < own_video[:, None]).astype(jnp.int32), axis=1)
-    high = jnp.sum((video_ids[None, :] <= own_video[:, None]).astype(jnp.int32), axis=1)
-    context, out_full = encode(
-        patches, vit_gain, vision_qkv, jnp.repeat(4 * low, 4), jnp.repeat(4 * high, 4), vision_out,
-        seq_count, frame_count, 1,
-    )
-    part_rows = text_embed.shape[0]
-    seq_block = part_rows * frame_count
-    first = seq_index * seq_block
-    text_own = rms_scale(text_embed, llm_gain).astype(jnp.bfloat16)
-    text_own = text_own.reshape(-1, 16, text_own.shape[1])
+    context, out_full, text_own = encode(
+        patches, vit_gain, vision_qkv, video_ids, vision_out, text_embed, llm_gain, seq_count, frame_count, 1
+    )
     merge_hidden, text_near = mid(
         context, out_full, patches, merge_gain, text_own, merge_up, seq_count, frame_count, 2
     )
-    vision_normed, text_query, text_pair = scatter(
-        merge_hidden, merge_down, llm_gain, text_own, text_near, query_weight, keyvalue_weight,
-        first + jnp.arange(seq_block, dtype=jnp.int32), seq_count, frame_count, 3,
-    )
-    share = vision_normed.shape[1]
+    seq_block = text_embed.shape[0] * frame_count
+    share = patch_rows // (4 * seq_count)
     token_pos = vision_pos.reshape(frame_count, seq_count, share).transpose(1, 0, 2)
     here = lax.dynamic_index_in_dim(token_pos, seq_index, 0, keepdims=False).reshape(-1)
-    text_pair_all, gathered = finish(
-        vision_normed, text_pair, here, query_weight, keyvalue_weight, seq_count, frame_count, 4
-    )
-    width = query_weight.shape[1]
-    token_pos = token_pos.reshape(-1)
-    llm_query = place(token_pos, first, text_query, gathered[:, :width])
-    llm_pair = place(token_pos, 0, text_pair_all, gathered[:, width:])
-    return causal_attention(seq_index, llm_query, llm_pair[:, :HDIM], llm_pair[:, HDIM:])
+    spots = token_pos.reshape(1, -1)
+    vision_normed, text_query, text_pair, covered = scatter(
+        merge_hidden, merge_down, llm_gain, text_own, text_near, query_weight, keyvalue_weight,
+        turns(seq_index * seq_block + jnp.arange(seq_block, dtype=jnp.int32)), spots,
+        seq_count, frame_count, 3,
+    )
+    return finish(
+        vision_normed, text_pair, text_query, covered, spots, turns(here), query_weight, keyvalue_weight,
+        seq_count, frame_count, 4,
+    )
 
 
 def solution(mesh):

time: 193 us -> 179 us (0.927)
  matrix products: 5.96 us -> 0 us
  other arithmetic: 8.9 us -> 2.95 us
  local copies, waits for them, and re-layouts: 8.06 us -> 5.9 us
    pallas_call x1 -> x0, Pallas kernels: 25.1 us -> none  [causal_attention(): pl.pallas_call(causal_kernel, grid=(width // HDIM,), in_specs=[pl.BlockSp...]
    pallas_call x1, Pallas kernels: 39.9 us -> 62.3 us  [finish(): pl.pallas_call(functools.partial(finish_kernel, seq_count, frame_count),...]
    dot_general x2 -> x0, matrix products: 5.96 us -> none  [place(): jnp.dot(hit.astype(jnp.bfloat16), vision_rows, preferred_element_type=jnp...]
    pallas_call x1, Pallas kernels: 26.5 us -> 30.1 us  [encode(): pl.pallas_call(functools.partial(encode_kernel, seq_count, frame_count),...]
    mul x1 -> x2, other arithmetic: 0.01 us -> 2.91 us  [turns(): jnp.where(lanes < HDIM // 2, -1.0, 1.0) * jnp.sin(angles)]
    concatenate x3 -> x0, other arithmetic: 2.44 us -> none  [the longest x2 1.57 us: turns(): jnp.concatenate([cosine, cosine], axis=1)]
    convert_element_type x1 -> x0, other arithmetic: 1.98 us -> none  [local(): text_own = rms_scale(text_embed, llm_gain).astype(jnp.bfloat16)]
where the time goes in v4:
time: 179 us; the launch traced here: 178 us
  Pallas kernels  169 us (94%)
  local copies, waits for them, and re-layouts  5.9 us (3%)
  other arithmetic  2.95 us (2%)
    pallas_call x1, Pallas kernels, finish(): pl.pallas_call(functools.partial(finish_kernel, seq_count, frame_count),...  62.3 us
    pallas_call x1, Pallas kernels, scatter(): pl.pallas_call(functools.partial(scatter_kernel, count, frame_count), in_...  42.8 us
    pallas_call x1, Pallas kernels, mid(): pl.pallas_call(functools.partial(mid_kernel, count, frame_count), in_spec...  34.3 us
    pallas_call x1, Pallas kernels, encode(): pl.pallas_call(functools.partial(encode_kernel, seq_count, frame_count),...  30.1 us

profile of v4, /device:TPU:28, one launch (start us, length us, event | category | flops | bytes accessed | tf_op | source)
XLA Modules:
  0.0 178.3 jit_solution(5994378923493975831)
XLA Ops:
  0.0 0.0 copy-start
  0.0 1.3 broadcast_in_dim.29.gain
  1.3 1.3 broadcast_in_dim.30.ids
  2.6 30.1 %shard_map.127 = (bf16[2,80,768]{2,1,0:T(8,128)(2,1)}, bf16[8,2,5,16,1280]{4,3,2,1,0:T(8,128)(2,1)}, bf16[8,16,8192]{2,1,0:T(8,128)(2,1)}) custom-call(bf16[768,1280]{1,0:T(8,128)(2,1)} %patches.3, f32[1,1280]{1,0:T(1,128)} %broadcast_in_dim.29.gain, bf16[480,1280]{1,0:T(8,128)(2,1)} %bitcast.9, s32[1,768]{1,0:T(1,128)} %broadcast_in_dim.30.ids, ...), custom_call_target="tpu_custom_call" | custom-call | tf_op jit(solution)/shard_map/pallas_call | solution.py:354
  32.7 0.0 copy-done
  32.7 0.6 broadcast_in_dim.32.gain
  33.3 0.0 copy-start.1
  33.3 34.3 %shard_map.128 = (bf16[192,640]{1,0:T(8,128)(2,1)}, bf16[4,4,16,8192]{3,2,1,0:T(8,128)(2,1)}) custom-call(bf16[2,80,768]{2,1,0:T(8,128)(2,1)} %get-tuple-element.14.block, bf16[8,160,1280]{2,1,0:T(8,128)(2,1)} %bitcast.7, bf16[768,1280]{1,0:T(8,128)(2,1)} %patches.3, f32[1,1280]{1,0:T(1,128)} %broadcast_in_dim.32.gain, ...), custom_call_target="tpu_custom_call" | custom-call | tf_op jit(solution)/shard_map/pallas_call | solution.py:455
  67.6 2.0 %fusion = (f32[512,128]{1,0:T(8,128)}, f32[512,128]{1,0:T(8,128)}) fusion(f32[128]{0:T(128)S(1)} %get-tuple-element.27, f32[128]{0:T(128)S(1)} %get-tuple-element.28, f32[512]{0:T(512)S(1)} %add_convert_fusion), kind=kLoop, calls=%fused_computation.2 | loop fusion | flops 131072 | bytes 527360 | tf_op jit(solution)/shard_map/mul | solution.py:942
  69.6 0.0 copy-done.1
  69.6 0.1 reshape.53
  69.7 0.7 reshape.54.spots
  70.4 42.8 %shard_map.129 = (bf16[4,24,2048]{2,1,0:T(8,128)(2,1)}, bf16[512,512]{1,0:T(8,128)(2,1)}, bf16[512,256]{1,0:T(8,128)(2,1)}, f32[8,8,512]{2,1,0:T(8,128)}) custom-call(bf16[192,640]{1,0:T(8,128)(2,1)} %get-tuple-element.17.hidden, bf16[640,8192]{1,0:T(8,128)(2,1)} %weight.1, f32[1,8192]{1,0:T(1,128)} %bitcast.13, ...), custom_call_target="tpu_custom_call" | custom-call | tf_op jit(solution)/shard_map/pallas_call | solution.py:906
  113.2 0.1 convert_element_type.30
  113.3 0.9 fusion.1
  114.2 62.3 %shard_map.130 = bf16[512,512]{1,0:T(8,128)(2,1)} custom-call(bf16[4,24,2048]{2,1,0:T(8,128)(2,1)} %get-tuple-element.19.tokens, bf16[2,256,256]{2,1,0:T(8,128)(2,1)} %bitcast.11, bf16[512,512]{1,0:T(8,128)(2,1)} %get-tuple-element.21.query, f32[8,8,512]{2,1,0:T(8,128)} %get-tuple-element.22.covered, s32[1,768]{1,0:T(1,128)} %reshape.54.spots, ...), custom_call_target="tpu_custom_call" | custom-call | tf_op jit(solution)/shard_map/pallas_call | solution.py:709
  176.5 1.9 %copy.16 = bf16[512,512]{1,0:T(8,128)(2,1)} copy(bf16[512,512]{1,0:T(8,128)(2,1)} %shard_map.130) | data formatting | bytes 1048576
  (4 shorter events, 0.0 us)
Async XLA Ops:
  0.0 32.7 %copy-start = (f32[1280]{0:T(1024)S(1)}, f32[1280]{0:T(1024)}, u32[]{:S(2)}) copy-start(f32[1280]{0:T(1024)} %param.18) | copy-start | bytes 15364
  33.3 36.3 %copy-start.1 = (s32[768]{0:T(1024)S(1)}, s32[768]{0:T(1024)}, u32[]{:S(2)}) copy-start(s32[768]{0:T(1024)} %param.21) | copy-start | bytes 9220

commit v5 on v4

--- a/solution.py
+++ b/solution.py
@@ -105,9 +105,10 @@
             self.ring.right if way == 0 else self.ring.left,
         )
 
-    def start(self):
+    def start(self, only=None):
         for way, piece in self.moves(0):
-            self.copy(0, way, piece).start()
+            if only is None or piece == only:
+                self.copy(0, way, piece).start()
 
     def advance(self, step, landed=None):
         ahead = list(self.moves(step + 1)) if step + 1 < self.steps else []
@@ -197,9 +198,13 @@
 
 
 def encode_kernel(
-    seq_count, frame_count, patches, gain, weight, ids, out_weight, text, text_gain, context, weight_out, text_out, *scratch
+    seq_count, frame_count, patches, gain, weight, ids, out_weight, text, text_gain, merge_gain, up,
+    hidden, text_out, text_near, *scratch
 ):
-    mine, query, held, flat, peak, mass, blend, fsend, frecv, rsend, rrecv, tsend, trecv, own = scratch
+    (mine, query, held, flat, peak, mass, blend, context, weight_out, gathered, up_held, total, spread,
+     fsend, frecv, rsend, rrecv, tsend, trecv, csend, crecv, xsend, xrecv, own) = scratch
+    load_up = pltpu.make_async_copy(up, up_held, own.at[2])
+    load_up.start()
     ring = Ring(seq_count)
     heads, tall, rows = mine.shape
     frames = FrameGather(frame_count, mine, held, fsend, frecv, heads)
@@ -208,6 +213,9 @@
     gather = RingGather(
         ring, out_weight.at[core], lambda i, piece: weight_out.at[i, core, piece], rsend, rrecv, pieces
     )
+    contexts = RingGather(ring, context, lambda i, piece: gathered.at[i, piece], csend, crecv, heads)
+    parts = text_near.shape[1]
+    words = FrameGather(frame_count, text_out, text_near, xsend, xrecv, parts)
     greet([ring.left, ring.right] + frames.partners())
     gather.start()
     keep = pltpu.make_async_copy(out_weight, weight_out.at[ring.index(0)], own.at[0])
@@ -222,7 +230,7 @@
 
     widened = patches[...].astype(jnp.float32)
     factor = lax.rsqrt(jnp.mean(widened * widened, axis=-1, keepdims=True) + epsilon)
-    normed = (widened * factor * gain[...]).astype(jnp.bfloat16)
+    normed = (widened * factor * gain[...].reshape(1, -1)).astype(jnp.bfloat16)
     projected = lax.dot_general(
         weight[...], normed, (((1,), (1,)), ((), ())), preferred_element_type=jnp.float32
     ).astype(jnp.bfloat16)
@@ -295,9 +303,9 @@
         lax.fori_loop(0, rows // tile, one, 0)
 
     def norm_text(index):
-        words = text[index].astype(jnp.float32)
-        level = lax.rsqrt(jnp.mean(words * words, axis=-1, keepdims=True) + epsilon)
-        text_out[index] = (words * level * text_gain[...]).astype(text_out.dtype)
+        line = text[index].astype(jnp.float32)
+        level = lax.rsqrt(jnp.mean(line * line, axis=-1, keepdims=True) + epsilon)
+        text_out[index] = (line * level * text_gain[...].reshape(1, -1)).astype(text_out.dtype)
 
     def second_pass(head):
         if far:
@@ -323,84 +331,38 @@
     for head in range(heads):
         frames.inside(0, head).wait_recv()
         first_pass(head)
-        for index in range(head, text.shape[0], heads):
-            norm_text(index)
+    for head in range(heads):
         frames.relay(head)
         if head + 1 < gather.steps:
             gather.advance(head + 1, landed)
-    for head in range(heads):
+        for index in range(head, text.shape[0], heads):
+            norm_text(index)
+        if head == heads - 1:
+            words.start()
+            aside = pltpu.make_async_copy(
+                text_out.at[pl.ds(0, parts)], text_near.at[frames.me], own.at[3]
+            )
+            aside.start()
         for d in range(1, frames.chips):
             frames.inside(d, head).wait_recv()
         second_pass(head)
-        if heads + head + 1 < gather.steps:
-            gather.advance(heads + head + 1, landed)
-    for step in range(2 * heads + 1, gather.steps):
+        contexts.start(head)
+    for step in range(heads + 1, gather.steps):
         gather.advance(step, landed)
+    own_context = pltpu.make_async_copy(context, gathered.at[ring.index(0)], own.at[1])
+    own_context.start()
     keep.wait()
     frames.finish()
     gather.finish()
     for copy in handed:
         copy.wait()
-
-
-def encode(patches, gain, weight, ids, out_weight, text, text_gain, seq_count, frame_count, collective):
-    rows = patches.shape[0]
-    heads = weight.shape[1] // (3 * VIT_HDIM)
-    half = out_weight.shape[0] // 2
-    tall = math.gcd(half, 16)
-    pieces = half // tall
-    out_weight = out_weight.reshape(2, pieces, tall, -1)
-    text = text.reshape(-1, 16, text.shape[1])
-    context, weight_out, text_out = pl.pallas_call(
-        functools.partial(encode_kernel, seq_count, frame_count),
-        in_specs=[VMEM] * 7,
-        out_specs=[VMEM, ANY, VMEM],
-        out_shape=[
-            jax.ShapeDtypeStruct((heads, VIT_HDIM, rows), jnp.bfloat16),
-            jax.ShapeDtypeStruct((seq_count,) + out_weight.shape, out_weight.dtype),
-            jax.ShapeDtypeStruct(text.shape, text.dtype),
-        ],
-        scratch_shapes=[
-            pltpu.VMEM((heads, 2 * VIT_HDIM, rows), jnp.bfloat16),
-            pltpu.VMEM((heads, VIT_HDIM, rows), jnp.bfloat16),
-            pltpu.VMEM((frame_count, heads, 2 * VIT_HDIM, rows), jnp.bfloat16),
-            pltpu.VMEM((frame_count, heads, rows, VIT_HDIM), jnp.bfloat16),
-            pltpu.VMEM((heads, rows), jnp.float32),
-            pltpu.VMEM((heads, rows), jnp.float32),
-            pltpu.VMEM((heads, VIT_HDIM, rows), jnp.float32),
-        ]
-        + frame_sems(frame_count, heads)
-        + ring_sems(seq_count, pieces) * 2
-        + [pltpu.SemaphoreType.DMA((2,))],
-        compiler_params=comm_params(collective),
-    )(patches, gain[None, :], weight.T, ids[None, :], out_weight, text, text_gain[None, :])
-    return context, weight_out.reshape(seq_count, 2 * half, -1), text_out
-
-
-def mid_kernel(
-    count, frame_count, block, out_weight, patches, gain, text, up, hidden, text_out,
-    held, up_held, total, spread, load, send, recv, fsend, frecv, own
-):
-    load_up = pltpu.make_async_copy(up, up_held, load)
-    load_up.start()
-    ring = Ring(count)
-    pieces, tall, rows = block.shape
-    share = pieces * tall
-    gather = RingGather(ring, block, lambda i, piece: held.at[i, piece], send, recv, pieces)
-    parts = text_out.shape[1]
-    frames = FrameGather(frame_count, text, text_out, fsend, frecv, parts)
-    greet([ring.left, ring.right] + frames.partners())
-    gather.start()
-    frames.start()
-    keep = pltpu.make_async_copy(block, held.at[ring.index(0)], own.at[0])
-    keep.start()
-    aside = pltpu.make_async_copy(text.at[pl.ds(0, parts)], text_out.at[frames.me], own.at[1])
-    aside.start()
+    own_context.wait()
+    share = heads * VIT_HDIM
 
     def fold(offsets, first):
         owners = [ring.index(offset) for offset in offsets]
-        left = jnp.concatenate([held[i].reshape(share, rows) for i in owners], axis=0)
-        right = jnp.concatenate([out_weight[i] for i in owners], axis=0)
+        left = jnp.concatenate([gathered[i].reshape(share, rows) for i in owners], axis=0)
+        right = jnp.concatenate([weight_out[i].reshape(share, -1) for i in owners], axis=0)
         product = lax.dot_general(
             left, right, (((0,), (0,)), ((), ())), preferred_element_type=jnp.float32
         )
@@ -409,24 +371,26 @@
         else:
             total[...] += product
 
-    half = max(gather.steps // 2, 1)
-    keep.wait()
-    for step in range(gather.steps):
-        gather.advance(step)
-        if step < parts:
-            frames.relay(step)
+    half = max(contexts.steps // 2, 1)
+    early = min(parts, contexts.steps - 1)
+    for step in range(contexts.steps):
+        contexts.advance(step)
         if step == half - 1:
             fold(range(-half, half + 1), True)
-    if gather.steps > half:
-        rest = list(range(half + 1, gather.steps)) + list(range(-gather.steps, -half))
+        if step < early:
+            words.relay(step)
+    if contexts.steps > half:
+        rest = list(range(half + 1, contexts.steps)) + list(range(-contexts.steps, -half))
         fold(rest, False)
     width = total.shape[1]
     values = total[...]
     factor = lax.rsqrt(jnp.mean(values * values, axis=1, keepdims=True) + epsilon)
-    values = values * factor * gain[...]
+    values = values * factor * merge_gain[...].reshape(1, -1)
     lanes = spread.shape[2]
     for c in range(width // lanes):
         spread[c] = values[:, c * lanes : (c + 1) * lanes]
+    for part in range(early, parts):
+        words.relay(part)
     load_up.wait()
     result = sum(
         jnp.dot(
@@ -441,37 +405,54 @@
     hidden[...] = (0.5 * result * (1.0 + lax.erf(result * 0.5**0.5))).astype(hidden.dtype)
     aside.wait()
     for part in range(parts):
-        if part >= gather.steps:
-            frames.relay(part)
-        frames.settle(part)
-    frames.finish()
-    gather.finish()
-
-
-def mid(block, out_weight, patches, gain, text, up, count, frame_count, collective):
-    pieces, tall, rows = block.shape
-    width = patches.shape[1]
+        words.settle(part)
+    words.finish()
+    contexts.finish()
+
+
+def encode(
+    patches, gain, weight, ids, out_weight, text, text_gain, merge_gain, up, seq_count, frame_count, collective
+):
+    rows, width = patches.shape
+    heads = weight.shape[1] // (3 * VIT_HDIM)
+    half = out_weight.shape[0] // 2
+    tall = math.gcd(half, 16)
+    pieces = half // tall
+    out_weight = out_weight.reshape(2, pieces, tall, -1)
+    text = text.reshape(-1, 16, text.shape[1])
     parts = text.shape[0] // 2
+    own = (heads, VIT_HDIM, rows)
     return pl.pallas_call(
-        functools.partial(mid_kernel, count, frame_count),
-        in_specs=[VMEM] * 5 + [ANY],
-        out_specs=[VMEM, ANY],
+        functools.partial(encode_kernel, seq_count, frame_count),
+        in_specs=[VMEM] * 8 + [ANY],
+        out_specs=[VMEM, VMEM, ANY],
         out_shape=[
             jax.ShapeDtypeStruct((rows // 4, up.shape[1]), jnp.bfloat16),
+            jax.ShapeDtypeStruct(text.shape, text.dtype),
             jax.ShapeDtypeStruct((frame_count, parts) + text.shape[1:], text.dtype),
         ],
         scratch_shapes=[
-            pltpu.VMEM((count,) + block.shape, block.dtype),
+            pltpu.VMEM((heads, 2 * VIT_HDIM, rows), jnp.bfloat16),
+            pltpu.VMEM(own, jnp.bfloat16),
+            pltpu.VMEM((frame_count, heads, 2 * VIT_HDIM, rows), jnp.bfloat16),
+            pltpu.VMEM((frame_count, heads, rows, VIT_HDIM), jnp.bfloat16),
+            pltpu.VMEM((heads, rows), jnp.float32),
+            pltpu.VMEM((heads, rows), jnp.float32),
+            pltpu.VMEM(own, jnp.float32),
+            pltpu.VMEM(own, jnp.bfloat16),
+            pltpu.VMEM((seq_count,) + out_weight.shape, out_weight.dtype),
+            pltpu.VMEM((seq_count,) + own, jnp.bfloat16),
             pltpu.VMEM(up.shape, up.dtype),
             pltpu.VMEM((rows, width), jnp.float32),
             pltpu.VMEM((width // 128, rows, 128), jnp.float32),
-            pltpu.SemaphoreType.DMA,
         ]
-        + ring_sems(count, pieces)
+        + frame_sems(frame_count, heads)
+        + ring_sems(seq_count, pieces) * 2
+        + ring_sems(seq_count, heads)
         + frame_sems(frame_count, parts)
-        + [pltpu.SemaphoreType.DMA((2,))],
+        + [pltpu.SemaphoreType.DMA((4,))],
         compiler_params=comm_params(collective),
-    )(block, out_weight, patches, gain[None, :], text, up)
+    )(patches, gain, weight.T, ids[None, :], out_weight, text, text_gain, merge_gain, up)
 
 
 def finish_kernel(
@@ -533,14 +514,18 @@
     def score(left, right):
         return lax.dot_general(left, right, (((1,), (1,)), ((), ())), preferred_element_type=jnp.float32)
 
-    def fold(head, scores, values):
-        before = peak[head]
+    strip = math.gcd(rows, 256)
+
+    def fold(head, lines, scores, values):
+        before = peak[head, lines]
         highest = jnp.maximum(before, jnp.max(scores, axis=1, keepdims=True))
         weights, more = weigh(scores, highest)
         shrink = jnp.exp2((before - highest) * scale)
-        peak[head] = highest
-        mass[head] = mass[head] * shrink + more
-        blend[head] = blend[head] * shrink + jnp.dot(weights, values, preferred_element_type=jnp.float32)
+        peak[head, lines] = highest
+        mass[head, lines] = mass[head, lines] * shrink + more
+        blend[head, lines] = blend[head, lines] * shrink + jnp.dot(
+            weights, values, preferred_element_type=jnp.float32
+        )
 
     def query_of(group, j):
         return query[:, pl.ds(pl.multiple_of((group * couple + j) * HDIM, HDIM), HDIM)]
@@ -552,21 +537,27 @@
         lower = lax.broadcasted_iota(jnp.int32, (rows, rows), 0) >= lax.broadcasted_iota(
             jnp.int32, (rows, rows), 1
         )
-        for j in range(couple):
-            head = group * couple + j
-            scores = score(query_of(group, j), block[:, :HDIM]) + covered[here, :1, :]
-            scores = jnp.where(lower, scores, lowest)
-            highest = jnp.max(scores, axis=1, keepdims=True)
-            weights, more = weigh(scores, highest)
-            peak[head] = highest
+        several = [group * couple + j for j in range(couple)]
+        scores = [score(query_of(group, j), block[:, :HDIM]) + covered[here, :1, :] for j in range(couple)]
+        scores = [jnp.where(lower, part, lowest) for part in scores]
+        tops = [jnp.max(part, axis=1, keepdims=True) for part in scores]
+        weighed = [weigh(part, top) for part, top in zip(scores, tops)]
+        products = [
+            jnp.dot(weights, block[:, HDIM:], preferred_element_type=jnp.float32) for weights, _ in weighed
+        ]
+        for head, top, (_, more), product in zip(several, tops, weighed, products):
+            peak[head] = top
             mass[head] = more
-            blend[head] = jnp.dot(weights, block[:, HDIM:], preferred_element_type=jnp.float32)
+            blend[head] = product
 
     def earlier(group, owner):
         block = keys_of(owner)
+        keys, values, bias = block[:, :HDIM], block[:, HDIM:], covered[owner, :1, :]
         for j in range(couple):
-            scores = score(query_of(group, j), block[:, :HDIM]) + covered[owner, :1, :]
-            fold(group * couple + j, scores, block[:, HDIM:])
+            queries_now = query_of(group, j)
+            for line in range(0, rows, strip):
+                lines = slice(line, line + strip)
+                fold(group * couple + j, lines, score(queries_now[lines], keys) + bias, values)
 
     def vision_rows():
         for part in range(parts):
@@ -613,7 +604,7 @@
         at(groups - 1 + stride * step, functools.partial(texts.advance, step))
     at(groups + 2, vision_rows)
     for step in range(visions.steps):
-        at(groups + 5 + 3 * step, functools.partial(visions.advance, step))
+        at(groups + 4 + 2 * step, functools.partial(visions.advance, step))
 
     def body(unit, carry):
         turn_of, group = lax.div(unit, groups), lax.rem(unit, groups)
@@ -646,8 +637,10 @@
     vision_keys, vision_values = both[:, queries : queries + HDIM], both[:, queries + HDIM :]
     places = here * rows + lax.broadcasted_iota(jnp.int32, (rows, 1), 0)
     for head in range(heads):
-        scores = score(query[:, head * HDIM : (head + 1) * HDIM], vision_keys)
-        fold(head, jnp.where(spots[...] <= places, scores, lowest), vision_values)
+        for line in range(0, rows, strip):
+            lines = slice(line, line + strip)
+            scores = score(query[lines, head * HDIM : (head + 1) * HDIM], vision_keys)
+            fold(head, lines, jnp.where(spots[...] <= places[lines], scores, lowest), vision_values)
 
     picked = jnp.dot(select[...], both[:, :queries], preferred_element_type=jnp.float32).astype(jnp.bfloat16)
     stacked = jnp.concatenate([picked[:, c : c + HDIM] for c in range(0, queries, HDIM)], axis=0)
@@ -881,7 +874,7 @@
     factor = lax.rsqrt(squares / width + epsilon)
     for piece in order:
         columns = slice(piece * span, (piece + 1) * span)
-        out[piece] = (part[piece, here] * factor * gain[:, columns]).astype(out.dtype)
+        out[piece] = (part[piece, here] * factor * gain[columns].reshape(1, -1)).astype(out.dtype)
 
     def drain(step, carry):
         for piece in order:
@@ -932,7 +925,7 @@
         compiler_params=pltpu.CompilerParams(
             collective_id=collective, has_side_effects=True, vmem_limit_bytes=63 * 1024 * 1024
         ),
-    )(hidden, weight, gain[None, :], text, near, query_weight, keyvalue_weight, cosine, sine_part, spots)
+    )(hidden, weight, gain, text, near, query_weight, keyvalue_weight, cosine, sine_part, spots)
 
 
 def turns(positions):
@@ -962,11 +955,9 @@
     frame_count = lax.axis_size("frame")
     seq_count = lax.axis_size("seq")
     patch_rows = patches.shape[0]
-    context, out_full, text_own = encode(
-        patches, vit_gain, vision_qkv, video_ids, vision_out, text_embed, llm_gain, seq_count, frame_count, 1
-    )
-    merge_hidden, text_near = mid(
-        context, out_full, patches, merge_gain, text_own, merge_up, seq_count, frame_count, 2
+    merge_hidden, text_own, text_near = encode(
+        patches, vit_gain, vision_qkv, video_ids, vision_out, text_embed, llm_gain, merge_gain, merge_up,
+        seq_count, frame_count, 1,
     )
     seq_block = text_embed.shape[0] * frame_count
     share = patch_rows // (4 * seq_count)

time: 179 us -> 164 us (0.916)
  Pallas kernels: 169 us -> 157 us
  local copies, waits for them, and re-layouts: 5.9 us -> 4.01 us
    pallas_call x1 -> x0, Pallas kernels: 34.3 us -> none  [mid(): pl.pallas_call(functools.partial(mid_kernel, count, frame_count), in_spec...]
    pallas_call x1, Pallas kernels: 30.1 us -> 55.1 us  [encode(): pl.pallas_call(functools.partial(encode_kernel, seq_count, frame_count),...]
    pallas_call x1, Pallas kernels: 62.3 us -> 59.4 us  [finish(): pl.pallas_call(functools.partial(finish_kernel, seq_count, frame_count),...]
    broadcast_in_dim x2 -> x0, local copies, waits for them, and re-layouts: 1.9 us -> none  [the longest x1 1.31 us: encode(): gain[None, :]]
where the time goes in v5:
time: 164 us
  Pallas kernels  157 us (96%)
  local copies, waits for them, and re-layouts  4.01 us (2%)
  other arithmetic  2.77 us (2%)
    pallas_call x1, Pallas kernels, finish(): pl.pallas_call(functools.partial(finish_kernel, seq_count, frame_count),...  59.4 us
    pallas_call x1, Pallas kernels, encode(): pl.pallas_call(functools.partial(encode_kernel, seq_count, frame_count),...  55.1 us
    pallas_call x1, Pallas kernels, scatter(): pl.pallas_call(functools.partial(scatter_kernel, count, frame_count), in_...  42.4 us

profile of v5, /device:TPU:28, one launch (start us, length us, event | category | flops | bytes accessed | tf_op | source)
XLA Modules:
  0.0 163.8 jit_solution(6877938943865821751)
XLA Ops:
  0.0 1.8 %fusion = (f32[512,128]{1,0:T(8,128)}, f32[512,128]{1,0:T(8,128)}) fusion(f32[128]{0:T(128)S(1)} %get-tuple-element.23, f32[128]{0:T(128)S(1)} %get-tuple-element.24, f32[512]{0:T(512)S(1)} %add_convert_fusion), kind=kLoop, calls=%fused_computation.2 | loop fusion | flops 131072 | bytes 527360 | tf_op jit(solution)/shard_map/mul | solution.py:935
  1.8 1.3 broadcast_in_dim.19.ids
  3.1 0.0 copy-start
  3.1 55.1 %shard_map.127 = (bf16[192,640]{1,0:T(8,128)(2,1)}, bf16[8,16,8192]{2,1,0:T(8,128)(2,1)}, bf16[4,4,16,8192]{3,2,1,0:T(8,128)(2,1)}) custom-call(bf16[768,1280]{1,0:T(8,128)(2,1)} %patches.1, f32[1280]{0:T(1024)} %gain.2, bf16[480,1280]{1,0:T(8,128)(2,1)} %bitcast.6, s32[1,768]{1,0:T(1,128)} %broadcast_in_dim.19.ids, bf16[2,5,16,1280]{3,2,1,0:T(8,128)(2,1)} %bitcast.7, ...), custom_call_target="tpu_custom_call" | custom-call | tf_op jit(solution)/shard_map/pallas_call | solution.py:425
  58.2 0.0 copy-done
  58.2 0.1 reshape.49
  58.3 0.7 reshape.50.spots
  59.0 42.4 %shard_map.128 = (bf16[4,24,2048]{2,1,0:T(8,128)(2,1)}, bf16[512,512]{1,0:T(8,128)(2,1)}, bf16[512,256]{1,0:T(8,128)(2,1)}, f32[8,8,512]{2,1,0:T(8,128)}) custom-call(bf16[192,640]{1,0:T(8,128)(2,1)} %get-tuple-element.12.hidden, bf16[640,8192]{1,0:T(8,128)(2,1)} %weight.1, f32[8192]{0:T(1024)} %gain.3, bf16[8,16,8192]{2,1,0:T(8,128)(2,1)} %get-tuple-element.13.text, ...), custom_call_target="tpu_custom_call" | custom-call | tf_op jit(solution)/shard_map/pallas_call | solution.py:899
  101.5 0.1 convert_element_type.30
  101.6 0.9 fusion.1
  102.5 59.4 %shard_map.129 = bf16[512,512]{1,0:T(8,128)(2,1)} custom-call(bf16[4,24,2048]{2,1,0:T(8,128)(2,1)} %get-tuple-element.15.tokens, bf16[2,256,256]{2,1,0:T(8,128)(2,1)} %bitcast.8, bf16[512,512]{1,0:T(8,128)(2,1)} %get-tuple-element.17.query, f32[8,8,512]{2,1,0:T(8,128)} %get-tuple-element.18.covered, s32[1,768]{1,0:T(1,128)} %reshape.50.spots, ...), custom_call_target="tpu_custom_call" | custom-call | tf_op jit(solution)/shard_map/pallas_call | solution.py:702
  161.9 1.9 %copy.16 = bf16[512,512]{1,0:T(8,128)(2,1)} copy(bf16[512,512]{1,0:T(8,128)(2,1)} %shard_map.129) | data formatting | bytes 1048576
  (4 shorter events, 0.0 us)
Async XLA Ops:
  3.1 55.1 %copy-start = (s32[768]{0:T(1024)S(1)}, s32[768]{0:T(1024)}, u32[]{:S(2)}) copy-start(s32[768]{0:T(1024)} %param.21) | copy-start | bytes 9220

commit v6 on v5

--- a/solution.py
+++ b/solution.py
@@ -604,7 +604,7 @@
         at(groups - 1 + stride * step, functools.partial(texts.advance, step))
     at(groups + 2, vision_rows)
     for step in range(visions.steps):
-        at(groups + 4 + 2 * step, functools.partial(visions.advance, step))
+        at(groups + 5 + 3 * step, functools.partial(visions.advance, step))
 
     def body(unit, carry):
         turn_of, group = lax.div(unit, groups), lax.rem(unit, groups)
@@ -777,8 +777,6 @@
         first = ring.index(-1 if forward[piece] else 1)
         stage[piece, 0] = part[piece, first].astype(jnp.bfloat16)
         hop(piece, 0).start()
-    for copy in extra:
-        copy.wait()
     sums[...] = jnp.zeros_like(sums)
     slabs = 8
     slab = depth // slabs
@@ -817,6 +815,13 @@
     def opening(step, carry):
         for i, group in enumerate(groups):
             advance(step, group)
+            if i == 0:
+
+                @pl.when(step == 1)
+                def _():
+                    for copy in extra:
+                        copy.wait()
+
             project(early, 0, 2 * (step - 1) + i)
             for block in range(count // slabs):
                 cover((2 * (step - 1) + i) * (count // slabs) + block)

time: 164 us -> 160 us (0.976)
  Pallas kernels: 157 us -> 153 us
    pallas_call x1, Pallas kernels: 59.4 us -> 55.3 us  [finish(): pl.pallas_call(functools.partial(finish_kernel, seq_count, frame_count),...]
where the time goes in v6:
time: 160 us
  Pallas kernels  153 us (96%)
  local copies, waits for them, and re-layouts  4.01 us (3%)
  other arithmetic  2.77 us (2%)
    pallas_call x1, Pallas kernels, finish(): pl.pallas_call(functools.partial(finish_kernel, seq_count, frame_count),...  55.3 us
    pallas_call x1, Pallas kernels, encode(): pl.pallas_call(functools.partial(encode_kernel, seq_count, frame_count),...  55.1 us
    pallas_call x1, Pallas kernels, scatter(): pl.pallas_call(functools.partial(scatter_kernel, count, frame_count), in_...  42.4 us

profile of v6, /device:TPU:28, one launch (start us, length us, event | category | flops | bytes accessed | tf_op | source)
XLA Modules:
  0.0 159.6 jit_solution(13727207737250766621)
XLA Ops:
  0.0 1.8 %fusion = (f32[512,128]{1,0:T(8,128)}, f32[512,128]{1,0:T(8,128)}) fusion(f32[128]{0:T(128)S(1)} %get-tuple-element.23, f32[128]{0:T(128)S(1)} %get-tuple-element.24, f32[512]{0:T(512)S(1)} %add_convert_fusion), kind=kLoop, calls=%fused_computation.2 | loop fusion | flops 131072 | bytes 527360 | tf_op jit(solution)/shard_map/mul | solution.py:940
  1.8 1.3 broadcast_in_dim.19.ids
  3.1 0.0 copy-start
  3.1 55.1 %shard_map.127 = (bf16[192,640]{1,0:T(8,128)(2,1)}, bf16[8,16,8192]{2,1,0:T(8,128)(2,1)}, bf16[4,4,16,8192]{3,2,1,0:T(8,128)(2,1)}) custom-call(bf16[768,1280]{1,0:T(8,128)(2,1)} %patches.1, f32[1280]{0:T(1024)} %gain.2, bf16[480,1280]{1,0:T(8,128)(2,1)} %bitcast.6, s32[1,768]{1,0:T(1,128)} %broadcast_in_dim.19.ids, bf16[2,5,16,1280]{3,2,1,0:T(8,128)(2,1)} %bitcast.7, ...), custom_call_target="tpu_custom_call" | custom-call | tf_op jit(solution)/shard_map/pallas_call | solution.py:425
  58.2 0.0 copy-done
  58.2 0.1 reshape.49
  58.3 0.7 reshape.50.spots
  59.0 42.4 %shard_map.128 = (bf16[4,24,2048]{2,1,0:T(8,128)(2,1)}, bf16[512,512]{1,0:T(8,128)(2,1)}, bf16[512,256]{1,0:T(8,128)(2,1)}, f32[8,8,512]{2,1,0:T(8,128)}) custom-call(bf16[192,640]{1,0:T(8,128)(2,1)} %get-tuple-element.12.hidden, bf16[640,8192]{1,0:T(8,128)(2,1)} %weight.1, f32[8192]{0:T(1024)} %gain.3, bf16[8,16,8192]{2,1,0:T(8,128)(2,1)} %get-tuple-element.13.text, ...), custom_call_target="tpu_custom_call" | custom-call | tf_op jit(solution)/shard_map/pallas_call | solution.py:904
  101.5 0.1 convert_element_type.30
  101.6 0.9 fusion.1
  102.5 55.3 %shard_map.129 = bf16[512,512]{1,0:T(8,128)(2,1)} custom-call(bf16[4,24,2048]{2,1,0:T(8,128)(2,1)} %get-tuple-element.15.tokens, bf16[2,256,256]{2,1,0:T(8,128)(2,1)} %bitcast.8, bf16[512,512]{1,0:T(8,128)(2,1)} %get-tuple-element.17.query, f32[8,8,512]{2,1,0:T(8,128)} %get-tuple-element.18.covered, s32[1,768]{1,0:T(1,128)} %reshape.50.spots, ...), custom_call_target="tpu_custom_call" | custom-call | tf_op jit(solution)/shard_map/pallas_call | solution.py:702
  157.8 1.9 %copy.16 = bf16[512,512]{1,0:T(8,128)(2,1)} copy(bf16[512,512]{1,0:T(8,128)(2,1)} %shard_map.129) | data formatting | bytes 1048576
  (4 shorter events, 0.0 us)
Async XLA Ops:
  3.1 55.1 %copy-start = (s32[768]{0:T(1024)S(1)}, s32[768]{0:T(1024)}, u32[]{:S(2)}) copy-start(s32[768]{0:T(1024)} %param.21) | copy-start | bytes 9220
